TPU v7x, 256 devices: a whole 4x4x8 slice. The times are simulated.
256 devices in a mesh: dp: 32 (over z, y), ep: 8 (over x, core).
Axes of the slice: x: 4, y: 4, z: 8, core: 2. Of those that a mesh axis runs over, the one named last changes fastest.
Arguments:
- hidden: bfloat16 [8192, 2048], P(('dp', 'ep'))
- grad_out: bfloat16 [8192, 2048], P(('dp', 'ep'))
- expert_ids: int32 [8192, 2], P(('dp', 'ep'))
- norm_gain: float32 [2048], replicated
- w_router: float32 [2048, 8], replicated
- w_gate: bfloat16 [8, 2048, 5632], P('ep')
- w_up: bfloat16 [8, 2048, 5632], P('ep')
- w_down: bfloat16 [8, 5632, 2048], P('ep')
Outputs:
- output 1: bfloat16 [8192, 2048], P(('dp', 'ep'))
- output 2: float32 [], replicated
- output 3: bfloat16 [8192, 2048], P(('dp', 'ep'))
- output 4: float32 [2048], replicated
- output 5: float32 [2048, 8], replicated
- output 6: bfloat16 [8, 2048, 5632], P('ep')
- output 7: bfloat16 [8, 2048, 5632], P('ep')
- output 8: bfloat16 [8, 5632, 2048], P('ep')
All inputs are finite; a program needn't handle non-finite values.
Results may differ from a plain program's by a relative error of at most 0.0155116.
Values are sent between devices in bfloat16 or wider.
A program may use at most 768 MiB of HBM per device.

v0:
```python
import jax
import jax.numpy as jnp
from jax import lax
from jax.sharding import PartitionSpec as P

EPS = 1e-6
AUX_COEF = 0.001


def route_tables(expert_ids, n_exp, capacity):
    flat_ids = expert_ids.reshape(-1)
    n_choice = flat_ids.shape[0]
    one_hot = (flat_ids[:, None] == jnp.arange(n_exp, dtype=jnp.int32)[None, :]).astype(jnp.int32)
    running = jnp.cumsum(one_hot, axis=0) - 1
    dest_rows = flat_ids * capacity + jnp.sum(running * one_hot, axis=1)
    slot_owner = jnp.full((n_exp * capacity,), n_choice, jnp.int32).at[dest_rows].set(jnp.arange(n_choice, dtype=jnp.int32))
    return dest_rows, slot_owner, jnp.sum(one_hot, axis=0)


def solution(mesh):
    n_dev = mesh.shape["dp"] * mesh.shape["ep"]
    all_axes = ("dp", "ep")

    def local_step(hidden, grad_out, expert_ids, norm_gain, w_router, w_gate, w_up, w_down):
        n_tok, width = hidden.shape
        n_exp = w_router.shape[1]
        capacity = 4 * n_tok // n_exp
        total_tok = n_tok * n_dev
        dest_rows, slot_owner, loads = route_tables(expert_ids, n_exp, capacity)
        choice_hot = (expert_ids[:, :, None] == jnp.arange(n_exp, dtype=jnp.int32)).astype(jnp.float32)

        x_f32 = hidden.astype(jnp.float32)
        inv_rms = lax.rsqrt(jnp.mean(x_f32 * x_f32, axis=-1, keepdims=True) + EPS)
        x_hat = x_f32 * inv_rms
        x_norm = (x_hat * norm_gain).astype(jnp.bfloat16)
        xn_f32 = x_norm.astype(jnp.float32)
        router_probs = jax.nn.softmax(jnp.dot(xn_f32, w_router, preferred_element_type=jnp.float32), axis=-1)
        gate_vals = jnp.sum(router_probs[:, None, :] * choice_hot, axis=-1)
        route_stats = lax.psum(jnp.concatenate([loads.astype(jnp.float32), jnp.sum(router_probs, axis=0)]), all_axes)
        load_frac = route_stats[:n_exp] / (2 * total_tok)
        aux_loss = AUX_COEF * n_exp * jnp.sum(load_frac * route_stats[n_exp:] / total_tok)

        send_rows = jnp.take(x_norm, slot_owner // 2, axis=0, mode="fill", fill_value=0).reshape(n_exp, capacity, width)
        recv_rows = lax.all_to_all(send_rows, "ep", 0, 1, tiled=True)
        h_gate = jnp.einsum("nrd,ndf->nrf", recv_rows, w_gate, preferred_element_type=jnp.float32).astype(jnp.bfloat16)
        h_up = jnp.einsum("nrd,ndf->nrf", recv_rows, w_up, preferred_element_type=jnp.float32).astype(jnp.bfloat16)
        gate_f32 = h_gate.astype(jnp.float32)
        up_f32 = h_up.astype(jnp.float32)
        sig_gate = jax.nn.sigmoid(gate_f32)
        silu_gate = gate_f32 * sig_gate
        act_rows = (silu_gate * up_f32).astype(jnp.bfloat16)
        exp_out = jnp.einsum("nrf,nfd->nrd", act_rows, w_down, preferred_element_type=jnp.float32).astype(jnp.bfloat16)
        back_rows = lax.all_to_all(exp_out, "ep", 1, 0, tiled=True).reshape(n_exp * capacity, width)
        picked = jnp.take(back_rows, dest_rows, axis=0).reshape(n_tok, 2, width)
        out_hidden = (x_f32 + jnp.sum(gate_vals[:, :, None] * picked, axis=1)).astype(jnp.bfloat16)

        dy_f32 = grad_out.astype(jnp.float32)
        d_gates = jnp.sum(dy_f32[:, None, :] * picked, axis=-1)
        d_picked = (dy_f32[:, None, :] * gate_vals[:, :, None]).astype(jnp.bfloat16).reshape(n_tok * 2, width)
        d_send = jnp.take(d_picked, slot_owner, axis=0, mode="fill", fill_value=0).reshape(n_exp, capacity, width)
        d_recv = lax.all_to_all(d_send, "ep", 0, 1, tiled=True)
        d_act = jnp.einsum("nrd,nfd->nrf", d_recv, w_down, preferred_element_type=jnp.float32)
        d_act = d_act.astype(jnp.bfloat16).astype(jnp.float32)
        g_down = jnp.einsum("nrf,nrd->nfd", act_rows, d_recv, preferred_element_type=jnp.float32)
        d_hup = (d_act * silu_gate).astype(jnp.bfloat16)
        d_hgate = (d_act * up_f32 * sig_gate * (1.0 + gate_f32 * (1.0 - sig_gate))).astype(jnp.bfloat16)
        g_gate = jnp.einsum("nrd,nrf->ndf", recv_rows, d_hgate, preferred_element_type=jnp.float32)
        g_up = jnp.einsum("nrd,nrf->ndf", recv_rows, d_hup, preferred_element_type=jnp.float32)
        d_rows = (jnp.einsum("nrf,ndf->nrd", d_hgate, w_gate, preferred_element_type=jnp.float32) + jnp.einsum("nrf,ndf->nrd", d_hup, w_up, preferred_element_type=jnp.float32)).astype(jnp.bfloat16)
        d_back = lax.all_to_all(d_rows, "ep", 1, 0, tiled=True).reshape(n_exp * capacity, width)
        d_xn_exp = jnp.take(d_back, dest_rows, axis=0).reshape(n_tok, 2, width)

        d_probs = jnp.sum(d_gates[:, :, None] * choice_hot, axis=1) + (AUX_COEF * n_exp / total_tok) * load_frac
        d_logits = router_probs * (d_probs - jnp.sum(router_probs * d_probs, axis=-1, keepdims=True))
        d_xnorm = jnp.einsum("te,de->td", d_logits, w_router) + d_xn_exp[:, 0].astype(jnp.float32) + d_xn_exp[:, 1].astype(jnp.float32)
        d_xnorm = d_xnorm.astype(jnp.bfloat16).astype(jnp.float32)
        value_a6 = d_xnorm * norm_gain
        grad_hidden = (inv_rms * (value_a6 - x_hat * jnp.mean(value_a6 * x_hat, axis=-1, keepdims=True)) + dy_f32).astype(jnp.bfloat16)
        small_grads = lax.psum((jnp.sum(d_xnorm * x_hat, axis=0), jnp.einsum("td,te->de", xn_f32, d_logits)), all_axes)
        big_grads = lax.psum((g_gate, g_up, g_down), "dp")
        return (out_hidden, aux_loss, grad_hidden, small_grads[0], small_grads[1], big_grads[0].astype(jnp.bfloat16), big_grads[1].astype(jnp.bfloat16), big_grads[2].astype(jnp.bfloat16))

    tok_spec = P(all_axes, None)
    w_spec = P("ep", None, None)
    return jax.shard_map(local_step, mesh=mesh, in_specs=(tok_spec, tok_spec, tok_spec, P(), P(), w_spec, w_spec, w_spec), out_specs=(tok_spec, P(), tok_spec, P(), P(), w_spec, w_spec, w_spec), check_vma=False)
```

profile of v0, /device:TPU:1, one launch (start us, length us, event | category | flops | bytes accessed | tf_op | source)
XLA Modules:
  0.0 3324.4 jit_solution(9850159751055328947)
XLA Ops:
  7.2 0.7 broadcast_multiply_fusion
  7.9 0.8 copy.43
  8.7 1.0 fusion.60
  10.4 0.8 scatter_custom_fusion
  11.3 1.0 fusion.53
  12.3 0.9 gather_fusion
  13.3 0.9 broadcast_select_fusion.1
  14.2 6.6 all-to-all-start
  21.1 8.8 all-to-all-done
  29.9 9.2 fusion.18
  39.2 14.1 multiply_convert_fusion.2
  53.3 9.4 fusion.40
  62.7 1.8 copy.68
  64.5 0.5 broadcast.150
  65.0 4.8 reduce.1
  69.8 1.2 reshape.268
  70.9 4.6 all-to-all-start.1
  75.5 80.2 %psum.42 = f32[16]{0:T(128)S(1)} all-reduce(f32[16]{0:T(128)S(1)} %pad_maximum_fusion), channel_id=1, replica_groups=mesh['dp'=32,'ep'=8] {'dp','ep'}, use_global_device_ids=true, to_apply=%region_10.12 | all-reduce | flops 16 | bytes 128 | tf_op jit(solution)/shard_map/psum | solution.py:39
  155.8 1.0 mul.179
  156.8 1.4 mul.180
  158.3 1.8 reshape.269
  160.1 1.5 copy.66
  161.6 0.7 gather_fusion.2
  163.2 0.9 gather_fusion.1
  164.1 0.9 broadcast_select_fusion
  165.0 4.2 all-to-all-start.2
  169.3 0.7 slice_multiply_fusion
  170.7 0.8 fusion.69
  171.5 6.9 all-to-all-done.2
  178.4 17.7 convolution_bitcast_fusion
  196.2 14.1 multiply_convert_fusion.1
  210.3 11.8 fusion.4
  222.1 18.0 convolution_bitcast_fusion.1
  240.1 18.1 convolution_bitcast_fusion.2
  258.1 12.0 fusion.43
  270.2 0.8 copy.67
  271.0 3.7 reduce.2
  274.7 1.2 reshape.270
  275.9 4.6 all-to-all-start.3
  280.5 2951.9 %all-reduce.5 = (bf16[1,2048,5632]{2,1,0:T(8,128)(2,1)}, bf16[1,2048,5632]{2,1,0:T(8,128)(2,1)}, bf16[1,5632,2048]{2,1,0:T(8,128)(2,1)}) all-reduce(f32[1,2048,5632]{2,1,0:T(8,128)} %convolution_bitcast_fusion.2, f32[1,2048,5632]{2,1,0:T(8,128)} %convolution_bitcast_fusion.1, ...), channel_id=1, replica_groups=mesh['dp'=32,'ep'=8] {'dp'}, use_global_device_ids=true, to_apply=%region_19.21 | all-reduce | flops 34603008 | bytes 207618048 | tf_op jit(solution)/shard_map/psum | solution.py:80
  3232.4 0.5 reshape.271
  3233.3 0.7 gather_fusion.3
  3234.4 0.4 fusion.72
  3234.8 0.5 fusion.59
  3235.6 0.7 multiply_reduce_fusion.1
  3236.3 0.8 fusion.58
  3237.1 77.6 %psum.43 = f32[2048]{0:T(1024)} all-reduce(f32[2048]{0:T(1024)S(1)} %get-tuple-element.9), channel_id=1, replica_groups=mesh['dp'=32,'ep'=8] {'dp','ep'}, use_global_device_ids=true, to_apply=%region_17.19 | all-reduce | flops 2048 | bytes 16384 | tf_op jit(solution)/shard_map/psum | solution.py:79
  3314.7 1.5 copy.76
  (64 shorter events, 3.1 us)
Async XLA Ops:
  7.2 13.6 copy-start
  9.7 1.6 copy-start.10
  14.2 15.7 all-to-all-start
  39.2 14.1 copy-start.1
  62.7 93.1 %copy-start.6 = (bf16[32,2048]{1,0:T(8,128)(2,1)S(1)}, bf16[32,2048]{1,0:T(8,128)(2,1)}, u32[]{:S(2)}) copy-start(bf16[32,2048]{1,0:T(8,128)(2,1)} %param.11) | copy-start | bytes 393220
  70.9 87.4 %all-to-all-start.1 = ((bf16[8,2,16384]{2,1,0:T(2,128)(2,1)}), bf16[8,2,16384]{2,1,0:T(2,128)(2,1)S(1)}, u32[]{:S(2)}, u32[]{:S(2)}) async-start(bf16[8,2,16384]{2,1,0:T(2,128)(2,1)} %reshape.268), calls=%async_computation.1 | async-start | bytes 1048576 | tf_op jit(solution)/shard_map/all_to_all | solution.py:53
  158.3 4.5 copy-start.9
  162.4 1.7 copy-start.2
  165.0 13.4 all-to-all-start.2
  169.3 3145.4 %all-reduce.4.cloned.1.call-start = ((), (), s32[]{:S(2)}) async-start(), calls=%async_computation.4 | async-start | bytes 131072 | tf_op jit(solution)/shard_map/psum | solution.py:79
  178.4 17.8 copy-start.4
  275.9 2956.5 %all-to-all-start.3 = ((bf16[8,2,16384]{2,1,0:T(2,128)(2,1)}), bf16[8,2,16384]{2,1,0:T(2,128)(2,1)S(1)}, u32[]{:S(2)}, u32[]{:S(2)}) async-start(bf16[8,2,16384]{2,1,0:T(2,128)(2,1)} %reshape.270), calls=%async_computation.3 | async-start | bytes 1048576 | tf_op jit(solution)/shard_map/all_to_all | solution.py:70
  3232.4 1.6 copy-start.3
  3233.2 1.5 copy-start.5
  3233.3 1.5 copy-start.8
  3233.3 1.5 copy-start.11
  3234.0 2.3 copy-start.7
Sparse Core Ops, SparseCore 0:
  176.1 352.4 all-reduce.3
where the time goes:
time: 3330 us; the launch traced here: 3320 us
  blocking collectives  3110 us (93%)
  matrix products  126 us (4%)
    psum x1, blocking collectives, local_step(): big_grads = lax.psum((g_gate, g_up, g_down), 'dp')  2950 us
    psum x1, blocking collectives, local_step(): lax.psum(jnp.concatenate([loads.astype(jnp.float32), jnp.sum(router_probs...  80.2 us
    psum x1, blocking collectives, local_step(): lax.psum((jnp.sum(d_xnorm * x_hat, axis=0), jnp.einsum('td,te->de', xn_f3...  77.6 us
  transfers between devices with their start and end apart: 5, of which 2 were waited for; matrix products, arithmetic and copies ran while one was open for 3% of the time, Pallas kernels for 0%

commit v1 on v0

v1 whole, which is shorter than its diff:
```python
import functools
import jax
import jax.numpy as jnp
from jax import lax
from jax.experimental import pallas as pl
from jax.experimental.pallas import tpu as pltpu
from jax.sharding import PartitionSpec as P

EPS = 1e-6
AUX_COEF = 0.001
LANES = 128
GROUP = 256
ALIGN = 16
CAP_SMALL = 256
F32 = jnp.float32
BF16 = jnp.bfloat16


def route_tables(expert_ids, n_exp, capacity):
    flat_ids = expert_ids.reshape(-1)
    n_choice = flat_ids.shape[0]
    one_hot = (flat_ids[:, None] == jnp.arange(n_exp, dtype=jnp.int32)[None, :]).astype(jnp.int32)
    running = jnp.cumsum(one_hot, axis=0) - 1
    dest_rows = flat_ids * capacity + jnp.sum(running * one_hot, axis=1)
    slot_owner = jnp.full((n_exp * capacity,), n_choice, jnp.int32).at[dest_rows].set(jnp.arange(n_choice, dtype=jnp.int32))
    return dest_rows, slot_owner, jnp.sum(one_hot, axis=0)


def peers(n_y, n_z, n_ep):
    dp, ep = lax.axis_index("dp"), lax.axis_index("ep")
    y, z = lax.rem(dp, n_y), lax.div(dp, n_y)
    along_ep = [{"dp": dp, "ep": lax.rem(ep + k, n_ep)} for k in range(1, n_ep)]
    along_y = [{"dp": z * n_y + lax.rem(y + k, n_y), "ep": ep} for k in range(1, n_y)]
    along_z = [{"dp": lax.rem(z + k, n_z) * n_y + y, "ep": ep} for k in range(1, n_z)]
    return dp, ep, y, z, along_ep, along_y, along_z


def enter(all_peers):
    barrier = pltpu.get_barrier_semaphore()
    for peer in all_peers:
        pl.semaphore_signal(barrier, inc=1, device_id=peer, device_id_type=pl.DeviceIdType.MESH)
    pl.semaphore_wait(barrier, len(all_peers))


def exchange(targets, make):
    copies = [make(k, target) for k, target in enumerate(targets)]
    for copy in copies:
        copy.start()
    for copy in copies:
        copy.wait()


def remote(src, dst, send_sem, recv_sem, target):
    return pltpu.make_async_remote_copy(src_ref=src, dst_ref=dst, send_sem=send_sem, recv_sem=recv_sem, device_id=target, device_id_type=pl.DeviceIdType.MESH)


def gather_kernel(n_y, n_z, n_ep, row_ref, out_ref, send_sem, recv_sem):
    dp, ep, y, z, along_ep, along_y, along_z = peers(n_y, n_z, n_ep)
    enter(along_ep + along_y + along_z)
    mine = out_ref.at[pl.ds(dp * n_ep + ep, 1)]
    local = pltpu.make_async_copy(row_ref, mine, send_sem.at[0])
    local.start()
    local.wait()
    base = 0
    exchange(along_ep, lambda k, t: remote(row_ref, mine, send_sem.at[base + k], recv_sem.at[base + k], t))
    base = len(along_ep)
    rows_y = out_ref.at[pl.ds(dp * n_ep, n_ep)]
    exchange(along_y, lambda k, t: remote(rows_y, rows_y, send_sem.at[base + k], recv_sem.at[base + k], t))
    base += len(along_y)
    rows_z = out_ref.at[pl.ds(z * n_y * n_ep, n_y * n_ep)]
    exchange(along_z, lambda k, t: remote(rows_z, rows_z, send_sem.at[base + k], recv_sem.at[base + k], t))


def gather_rows(row, n_y, n_z, n_ep):
    n_dev = n_y * n_z * n_ep
    n_sem = n_ep + n_y + n_z - 3
    return pl.pallas_call(
        functools.partial(gather_kernel, n_y, n_z, n_ep),
        out_shape=jax.ShapeDtypeStruct((n_dev, 1, LANES), F32),
        in_specs=[pl.BlockSpec(memory_space=pltpu.VMEM)],
        out_specs=pl.BlockSpec(memory_space=pltpu.VMEM),
        scratch_shapes=[pltpu.SemaphoreType.DMA((n_sem,)), pltpu.SemaphoreType.DMA((n_sem,))],
        compiler_params=pltpu.CompilerParams(collective_id=1, has_side_effects=True),
        name="gather_rows",
    )(row)


def reduce_kernel(n_y, n_z, n_ep, in_ref, out_ref, got_ep, got_y, got_z, send_sem, recv_sem):
    dp, ep, y, z, along_ep, along_y, along_z = peers(n_y, n_z, n_ep)
    enter(along_ep + along_y + along_z)
    base = 0
    got_ep[ep] = in_ref[ep]
    exchange(along_ep, lambda k, t: remote(in_ref.at[t["ep"]], got_ep.at[ep], send_sem.at[base + k], recv_sem.at[base + k], t))
    total = got_ep[0]
    for k in range(1, n_ep):
        total = total + got_ep[k]
    got_y[y] = total
    base = len(along_ep)
    exchange(along_y, lambda k, t: remote(got_y.at[y], got_y.at[y], send_sem.at[base + k], recv_sem.at[base + k], t))
    total = got_y[0]
    for k in range(1, n_y):
        total = total + got_y[k]
    got_z[z] = total
    base += len(along_y)
    exchange(along_z, lambda k, t: remote(got_z.at[z], got_z.at[z], send_sem.at[base + k], recv_sem.at[base + k], t))
    total = got_z[0]
    for k in range(1, n_z):
        total = total + got_z[k]
    out_ref[ep] = total
    base += len(along_z)
    exchange(along_ep, lambda k, t: remote(out_ref.at[ep], out_ref.at[ep], send_sem.at[base + k], recv_sem.at[base + k], t))


def reduce_rows(parts, n_y, n_z, n_ep):
    n_sem = 2 * n_ep + n_y + n_z - 4
    chunk = parts.shape[1:]
    return pl.pallas_call(
        functools.partial(reduce_kernel, n_y, n_z, n_ep),
        out_shape=jax.ShapeDtypeStruct(parts.shape, F32),
        in_specs=[pl.BlockSpec(memory_space=pltpu.VMEM)],
        out_specs=pl.BlockSpec(memory_space=pltpu.VMEM),
        scratch_shapes=[pltpu.VMEM((n_ep, *chunk), F32), pltpu.VMEM((n_y, *chunk), F32), pltpu.VMEM((n_z, *chunk), F32), pltpu.SemaphoreType.DMA((n_sem,)), pltpu.SemaphoreType.DMA((n_sem,))],
        compiler_params=pltpu.CompilerParams(collective_id=2, has_side_effects=True),
        name="reduce_rows",
    )(parts)


def dot(a, b, dims):
    return lax.dot_general(a, b, (dims, ((), ())), preferred_element_type=F32)


def expert_math(hg, hu, da):
    gate = hg.astype(BF16).astype(F32)
    up = hu.astype(BF16).astype(F32)
    d_act = da.astype(BF16).astype(F32)
    sig = jax.nn.sigmoid(gate)
    silu = gate * sig
    act = (silu * up).astype(BF16)
    d_up = (d_act * silu).astype(BF16)
    d_gate = (d_act * up * sig * (1.0 + gate * (1.0 - sig))).astype(BF16)
    return act, d_gate, d_up


def ffn_kernel(rows_ref, wg_ref, wu_ref, wd_ref, out_ref, o_acc, d_acc):
    step = pl.program_id(0)
    width = wg_ref.shape[0]
    xn, dp = rows_ref[:, :width], rows_ref[:, width:]
    wg, wu, wd = wg_ref[...], wu_ref[...], wd_ref[...]
    act, d_gate, d_up = expert_math(dot(xn, wg, ((1,), (0,))), dot(xn, wu, ((1,), (0,))), dot(dp, wd, ((1,), (1,))))

    @pl.when(step == 0)
    def _():
        o_acc[...] = jnp.zeros_like(o_acc)
        d_acc[...] = jnp.zeros_like(d_acc)

    o_acc[...] += dot(act, wd, ((1,), (0,)))
    d_acc[...] += dot(d_gate, wg, ((1,), (1,))) + dot(d_up, wu, ((1,), (1,)))

    @pl.when(step == pl.num_programs(0) - 1)
    def _():
        out_ref[:, :width] = o_acc[...].astype(BF16)
        out_ref[:, width:] = d_acc[...].astype(BF16)


def local_ffn(rows, wg, wu, wd, block):
    n, width = rows.shape[0], wg.shape[0]
    ff = wg.shape[1]
    whole = pl.BlockSpec((n, 2 * width), lambda j: (0, 0))
    col = pl.BlockSpec((width, block), lambda j: (0, j))
    row = pl.BlockSpec((block, width), lambda j: (j, 0))
    return pl.pallas_call(
        ffn_kernel,
        grid=(ff // block,),
        out_shape=jax.ShapeDtypeStruct((n, 2 * width), BF16),
        in_specs=[whole, col, col, row],
        out_specs=whole,
        scratch_shapes=[pltpu.VMEM((n, width), F32), pltpu.VMEM((n, width), F32)],
        compiler_params=pltpu.CompilerParams(dimension_semantics=("arbitrary",), vmem_limit_bytes=40 * 2**20),
        cost_estimate=pl.CostEstimate(flops=12 * n * width * ff, bytes_accessed=6 * width * ff, transcendentals=0),
        name="local_ffn",
    )(rows, wg, wu, wd)


def pack_kernel(cap, off_ref, first_ref, rows_ref, pos_ref, gate_ref, xn_out, dp_out, xn_buf, dp_buf, sem):
    g = pl.program_id(0)
    width = xn_buf.shape[1]
    tile = xn_buf.shape[0] - cap
    off = off_ref[g] - first_ref[0]
    base = pl.multiple_of(jnp.clip(lax.div(off, ALIGN) * ALIGN, 0, cap), ALIGN)

    @pl.when(g == 0)
    def _():
        xn_buf[...] = jnp.zeros_like(xn_buf)
        dp_buf[...] = jnp.zeros_like(dp_buf)

    row_id = lax.broadcasted_iota(jnp.int32, (tile, GROUP), 0) + base
    hit = row_id == pos_ref[0] - first_ref[0]
    pick = hit.astype(F32).astype(BF16)
    gate = jnp.sum(jnp.where(hit, gate_ref[0], 0.0), axis=1, keepdims=True)
    xn = dot(pick, rows_ref[:, :width], ((1,), (0,))).astype(BF16)
    dp = (dot(pick, rows_ref[:, width:], ((1,), (0,))) * gate).astype(BF16)
    keep = lax.broadcasted_iota(jnp.int32, (ALIGN, width), 0) + base < off
    for buf, new in ((xn_buf, xn), (dp_buf, dp)):
        head = pl.ds(base, ALIGN)
        buf[head, :] = jnp.where(keep, buf[head, :].astype(F32), new[:ALIGN].astype(F32)).astype(BF16)
        buf[pl.ds(pl.multiple_of(base + ALIGN, ALIGN), tile - ALIGN), :] = new[ALIGN:]

    @pl.when(g == pl.num_programs(0) - 1)
    def _():
        copies = [pltpu.make_async_copy(xn_buf.at[pl.ds(0, cap)], xn_out, sem.at[0]), pltpu.make_async_copy(dp_buf.at[pl.ds(0, cap)], dp_out, sem.at[1])]
        for copy in copies:
            copy.start()
        for copy in copies:
            copy.wait()


def pack_rows(rows, offsets, first, pos, gates, cap, most):
    total, width = rows.shape[0], rows.shape[1] // 2
    n_group = total // GROUP
    tile = most + ALIGN
    small = pl.BlockSpec((1, 1, GROUP), lambda g, *_: (g, 0, 0))
    return pl.pallas_call(
        functools.partial(pack_kernel, cap),
        grid_spec=pltpu.PrefetchScalarGridSpec(
            num_scalar_prefetch=2,
            grid=(n_group,),
            in_specs=[pl.BlockSpec((GROUP, 2 * width), lambda g, *_: (g, 0)), small, small],
            out_specs=[pl.BlockSpec(memory_space=pl.ANY), pl.BlockSpec(memory_space=pl.ANY)],
            scratch_shapes=[pltpu.VMEM((cap + tile, width), BF16), pltpu.VMEM((cap + tile, width), BF16), pltpu.SemaphoreType.DMA((2,))],
        ),
        out_shape=[jax.ShapeDtypeStruct((cap, width), BF16)] * 2,
        compiler_params=pltpu.CompilerParams(dimension_semantics=("arbitrary",), vmem_limit_bytes=50 * 2**20),
        cost_estimate=pl.CostEstimate(flops=4 * tile * total * width, bytes_accessed=4 * total * width, transcendentals=0),
        name="pack_rows",
    )(offsets, first, rows, pos, gates)


def solution(mesh):
    n_ep = mesh.shape["ep"]
    n_dp = mesh.shape["dp"]
    n_y = 4 if n_dp == 32 else 2
    n_z = n_dp // n_y
    n_dev = n_dp * n_ep
    all_axes = ("dp", "ep")

    def local_step(hidden, grad_out, expert_ids, norm_gain, w_router, w_gate, w_up, w_down):
        n_tok, width = hidden.shape
        n_exp = w_router.shape[1]
        capacity = 4 * n_tok // n_exp
        total_tok = n_tok * n_dev
        cap = min(2432, total_tok) if n_dp == 32 else CAP_SMALL
        dest_rows, slot_owner, loads = route_tables(expert_ids, n_exp, capacity)
        choice_hot = (expert_ids[:, :, None] == jnp.arange(n_exp, dtype=jnp.int32)).astype(F32)

        x_f32 = hidden.astype(F32)
        inv_rms = lax.rsqrt(jnp.mean(x_f32 * x_f32, axis=-1, keepdims=True) + EPS)
        x_hat = x_f32 * inv_rms
        x_norm = (x_hat * norm_gain).astype(BF16)
        rows_all = lax.all_gather(jnp.concatenate([x_norm, grad_out], axis=1), all_axes, axis=0, tiled=True)
        xn_f32 = x_norm.astype(F32)
        router_probs = jax.nn.softmax(jnp.dot(xn_f32, w_router, preferred_element_type=F32), axis=-1)
        gate_vals = jnp.sum(router_probs[:, None, :] * choice_hot, axis=-1)

        meta = jnp.concatenate([gate_vals.T.reshape(1, -1), expert_ids.T.astype(F32).reshape(1, -1)], axis=1)
        meta = jnp.pad(meta, ((0, 0), (0, LANES - meta.shape[1])))
        meta_all = gather_rows(meta[None], n_y, n_z, n_ep).reshape(n_dev, LANES)
        ids_all = meta_all[:, 2 * n_tok:4 * n_tok].astype(jnp.int32).reshape(n_dev, 2, n_tok)
        gates_all = meta_all[:, :2 * n_tok].reshape(n_dev, 2, n_tok)
        all_loads = jnp.sum((ids_all[..., None] == jnp.arange(n_exp, dtype=jnp.int32)).astype(F32), axis=(0, 1, 2))
        load_frac = all_loads / (2 * total_tok)

        dy_f32 = grad_out.astype(F32)
        d_picked = (dy_f32[:, None, :] * gate_vals[:, :, None]).astype(BF16).reshape(n_tok * 2, width)
        send = jnp.concatenate([
            jnp.take(x_norm, slot_owner // 2, axis=0, mode="fill", fill_value=0),
            jnp.take(d_picked, slot_owner, axis=0, mode="fill", fill_value=0)], axis=1)
        recv = lax.all_to_all(send.reshape(n_exp, capacity, 2 * width), "ep", 0, 0, tiled=True).reshape(n_exp * capacity, 2 * width)
        wg, wu, wd = w_gate[0], w_up[0], w_down[0]
        done = local_ffn(recv, wg, wu, wd, 256)
        back = lax.all_to_all(done.reshape(n_exp, capacity, 2 * width), "ep", 0, 0, tiled=True).reshape(n_exp * capacity, 2 * width)
        both = jnp.take(back, dest_rows, axis=0).reshape(n_tok, 2, 2 * width)
        picked, d_xn_exp = both[..., :width], both[..., width:]
        out_hidden = (x_f32 + jnp.sum(gate_vals[:, :, None] * picked, axis=1)).astype(BF16)
        d_gates = jnp.sum(dy_f32[:, None, :] * picked, axis=-1)

        d_probs = jnp.sum(d_gates[:, :, None] * choice_hot, axis=1) + (AUX_COEF * n_exp / total_tok) * load_frac
        d_logits = router_probs * (d_probs - jnp.sum(router_probs * d_probs, axis=-1, keepdims=True))
        d_xnorm = jnp.einsum("te,de->td", d_logits, w_router) + d_xn_exp[:, 0].astype(F32) + d_xn_exp[:, 1].astype(F32)
        d_xnorm = d_xnorm.astype(BF16).astype(F32)
        value_a6 = d_xnorm * norm_gain
        grad_hidden = (inv_rms * (value_a6 - x_hat * jnp.mean(value_a6 * x_hat, axis=-1, keepdims=True)) + dy_f32).astype(BF16)

        part_router = jnp.einsum("te,td->ed", d_logits, xn_f32).reshape(-1)
        part_gain = jnp.sum(d_xnorm * x_hat, axis=0)
        flat = jnp.concatenate([part_router, part_gain, jnp.sum(router_probs, axis=0)])
        unit = n_ep * 8 * LANES
        size = -(-flat.shape[0] // unit) * unit
        summed = reduce_rows(jnp.pad(flat, (0, size - flat.shape[0])).reshape(n_ep, -1, LANES), n_y, n_z, n_ep).reshape(-1)
        grad_router = summed[:n_exp * width].reshape(n_exp, width).T
        grad_gain = summed[n_exp * width:(n_exp + 1) * width]
        prob_sum = summed[(n_exp + 1) * width:(n_exp + 1) * width + n_exp]
        aux_loss = AUX_COEF * n_exp * jnp.sum(load_frac * prob_sum / total_tok)

        me = lax.axis_index("ep")
        mine = ids_all == me
        member = jnp.any(mine, axis=1).reshape(-1, GROUP)
        gate_me = jnp.sum(jnp.where(mine, gates_all, 0.0), axis=1).reshape(-1, 1, GROUP)
        rank = jnp.cumsum(member.astype(jnp.int32), axis=1)
        counts = rank[:, -1]
        offsets = jnp.cumsum(counts) - counts
        n_rows = offsets[-1] + counts[-1]
        pos = jnp.where(member, offsets[:, None] + rank - 1, -(2**24)).reshape(-1, 1, GROUP)

        def one_pass(first):
            xn, dp = pack_rows(rows_all, offsets, jnp.full((1,), first, jnp.int32), pos, gate_me, cap, GROUP // n_tok * capacity)
            act, d_gate, d_up = expert_math(dot(xn, wg, ((1,), (0,))), dot(xn, wu, ((1,), (0,))), dot(dp, wd, ((1,), (1,))))
            return dot(xn, d_gate, ((0,), (0,))), dot(xn, d_up, ((0,), (0,))), dot(act, dp, ((0,), (0,)))

        def few():
            return tuple(g.astype(BF16)[None] for g in one_pass(0))

        def many():
            return tuple((a + b).astype(BF16)[None] for a, b in zip(one_pass(0), one_pass(cap)))

        g_gate, g_up, g_down = lax.cond(n_rows <= cap, few, many)
        return out_hidden, aux_loss, grad_hidden, grad_gain, grad_router, g_gate, g_up, g_down

    tok_spec = P(all_axes, None)
    w_spec = P("ep", None, None)
    return jax.shard_map(local_step, mesh=mesh, in_specs=(tok_spec, tok_spec, tok_spec, P(), P(), w_spec, w_spec, w_spec), out_specs=(tok_spec, P(), tok_spec, P(), P(), w_spec, w_spec, w_spec), check_vma=False)
```

time: 3330 us -> 725 us (0.22)
  blocking collectives: 3110 us -> 0 us
  matrix products: 126 us -> 411 us
  Pallas kernels: 0 us -> 156 us
  waiting for transfers between devices: 15.7 us -> 85.9 us
    psum x3 -> x0, blocking collectives: 3110 us -> none  [the longest x1 2950 us: local_step(): big_grads = lax.psum((g_gate, g_up, g_down), 'dp')]
    dot_general x12 -> x9, matrix products: 126 us -> 411 us  [the longest x6 410 us: dot(): return lax.dot_general(a, b, (dims, ((), ())), preferred_element_type=F32)]
    pallas_call x0 -> x4, Pallas kernels: none -> 156 us  [the longest x1 51.7 us: local_ffn(): pl.pallas_call(ffn_kernel, grid=(ff // block,), out_shape=jax.ShapeDtypeS...]
    all_gather x0 -> x1, waiting for transfers between devices: none -> 62.9 us  [local_step(): lax.all_gather(jnp.concatenate([x_norm, grad_out], axis=1), all_axes, axi...]
  transfers between devices with their start and end apart: 5 -> 3, of which waited for: 2 -> 2; matrix products, arithmetic and copies ran while one was open for 3% -> 3% of each run, Pallas kernels for 0% -> 15%
where the time goes in v1:
time: 725 us; the launch traced here: 718 us
  matrix products  411 us (57%)
  Pallas kernels  156 us (22%)
  waiting for transfers between devices  85.9 us (12%)
  between operations  18 us (2%)
  other arithmetic  13.6 us (2%)
  local copies, waits for them, and re-layouts  13.2 us (2%)
  starting transfers between devices  11.3 us (2%)
  loops' own time  8.92 us (1%)
    dot_general x6, matrix products, dot(): return lax.dot_general(a, b, (dims, ((), ())), preferred_element_type=F32)  410 us
    all_gather x1, waiting for transfers between devices, local_step(): lax.all_gather(jnp.concatenate([x_norm, grad_out], axis=1), all_axes, axi...  62.9 us
    pallas_call x1, Pallas kernels, local_ffn(): pl.pallas_call(ffn_kernel, grid=(ff // block,), out_shape=jax.ShapeDtypeS...  51.7 us
    pallas_call x1, Pallas kernels, pack_rows(): pl.pallas_call(functools.partial(pack_kernel, cap), grid_spec=pltpu.Prefe...  46 us
    pallas_call x1, Pallas kernels, gather_rows(): pl.pallas_call(functools.partial(gather_kernel, n_y, n_z, n_ep), out_shap...  32 us
    pallas_call x1, Pallas kernels, reduce_rows(): pl.pallas_call(functools.partial(reduce_kernel, n_y, n_z, n_ep), out_shap...  26.4 us
    all_to_all x1, waiting for transfers between devices, local_step(): lax.all_to_all(done.reshape(n_exp, capacity, 2 * width), 'ep', 0, 0, tile...  22.9 us
  transfers between devices with their start and end apart: 3, of which 2 were waited for; matrix products, arithmetic and copies ran while one was open for 3% of the time, Pallas kernels for 15%

profile of v1, /device:TPU:1, one launch (start us, length us, event | category | flops | bytes accessed | tf_op | source)
XLA Modules:
  0.0 717.7 jit_solution(2106521674430616442)
XLA Ops:
  7.2 1.0 fusion.86
  8.3 1.0 fusion.79
  9.3 1.6 pad_maximum_fusion.1
  10.9 0.8 copy.80
  11.7 0.8 convert_bitcast_fusion.3
  12.9 0.2 select_reduce_fusion.1
  13.1 0.8 scatter_custom_fusion
  14.3 0.7 select_reduce_fusion.3
  15.3 0.9 gather_fusion
  16.2 1.1 mul.208.clone
  17.3 0.4 mul.209
  17.8 0.9 gather_fusion.1
  18.9 1.1 pad_maximum_fusion
  20.0 6.6 all-to-all-start
  26.8 0.6 maximum_bitcast_fusion.row_ref
  27.4 32.0 %gather_rows.1 = f32[256,1,128]{2,1,0:T(1,128)} custom-call(f32[1,1,128]{2,1,0:T(1,128)} %maximum_bitcast_fusion.row_ref), custom_call_target="tpu_custom_call" | custom-call | tf_op jit(solution)/shard_map/gather_rows/pallas_call | solution.py:77
  59.4 1.1 fusion.97
  60.9 0.6 reduce-window.10
  61.5 0.2 slice_reduce_fusion
  62.0 0.2 fusion.96
  62.3 51.7 %local_ffn.1 = bf16[128,4096]{1,0:T(8,128)(2,1)} custom-call(bf16[128,4096]{1,0:T(8,128)(2,1)S(1)} %bitcast.105, bf16[2048,5632]{1,0:T(8,128)(2,1)} %bitcast.107, bf16[2048,5632]{1,0:T(8,128)(2,1)} %bitcast.112, bf16[5632,2048]{1,0:T(8,128)(2,1)} %bitcast.115), custom_call_target="tpu_custom_call" | custom-call | flops 17716740096 | bytes 69206016 | tf_op jit(solution)/shard_map/local_ffn/pallas_call | solution.py:171
  114.0 4.6 all-to-all-start.1
  118.9 0.6 slice.78
  119.8 0.5 slice.77
  121.8 0.2 convert_reduce_fusion
  122.1 22.9 %all-to-all-done.1 = bf16[8,16,4096]{2,1,0:T(8,128)(2,1)S(1)} async-done(((bf16[8,16,4096]{2,1,0:T(8,128)(2,1)}), bf16[8,16,4096]{2,1,0:T(8,128)(2,1)S(1)}, u32[]{:S(2)}, u32[]{:S(2)}) %all-to-all-start.1) | async-done | bytes 1048608 | tf_op jit(solution)/shard_map/all_to_all | solution.py:280
  145.0 0.9 gather_fusion.2
  145.9 0.3 gather.23
  146.2 0.6 copy_select_fusion
  147.2 0.2 convolution_bitcast_fusion
  147.4 0.5 fusion.81
  147.9 0.7 select_maximum_fusion
  148.6 26.4 %reduce_rows.1 = f32[8,24,128]{2,1,0:T(8,128)} custom-call(f32[8,24,128]{2,1,0:T(8,128)} %bitcast.126), custom_call_target="tpu_custom_call" | custom-call | tf_op jit(solution)/shard_map/reduce_rows/pallas_call | solution.py:117
  175.0 0.9 slice.54
  175.9 1.3 slice.73
  177.2 1.3 fusion.93
  179.2 0.6 slice_bitcast_fusion.2
  179.8 0.8 fusion.85
  180.6 62.9 %all-gather.2.cloned.1.call-done = bf16[8192,4096]{1,0:T(8,128)(2,1)} async-done(((bf16[32,4096]{1,0:T(8,128)(2,1)}), bf16[8192,4096]{1,0:T(8,128)(2,1)}) %all-gather.2.cloned.1.call-update) | async-done | bytes 67108880 | tf_op jit(solution)/shard_map/all_gather | solution.py:259
  243.5 464.9 %conditional.1 = (bf16[1,2048,5632]{2,1,0:T(8,128)(2,1)}, bf16[1,2048,5632]{2,1,0:T(8,128)(2,1)}, bf16[1,5632,2048]{2,1,0:T(8,128)(2,1)}) conditional(s32[]{:T(128)} %bitcast.26, (s32[32]{0:T(128)S(1)}, bf16[8192,4096]{1,0:T(8,128)(2,1)}, s32[32,1,256]{2,0,1:T(8,128)S(1)}, f32[32,1,256]{2,0,1:T(8,128)S(1)}, bf16[5632,2048]{1,0:T(8,128)(2,1)}, ...), branch_computations={%region_21.22_spmd, %region_22.23_spmd} | conditional | flops 693509292032 | bytes 1447690496 | solution.py:325
  252.2 46.0 %pack_rows.5 = (bf16[2432,2048]{1,0:T(8,128)(2,1)}, bf16[2432,2048]{1,0:T(8,128)(2,1)}) custom-call(s32[32]{0:T(128)S(1)} %get-tuple-element.39.off_ref, s32[1]{0:T(128)} %constant.74.clone.first_ref, bf16[8192,4096]{1,0:T(8,128)(2,1)} %get-tuple-element.40.rows_ref, s32[32,1,256]{2,1,0:T(1,128)S(1)} %copy.96.pos_ref, f32[32,1,256]{2,1,0:T(1,128)S(1)} %copy.97.gate_ref), custom_call_target="tpu_custom_call" | custom-call | flops 9663676416 | bytes 67108864 | tf_op jit(solution)/shard_map/cond/branch_1_fun/pack_rows/pallas_call | solution.py:222
  298.2 65.1 %convolution_convert_fusion.6 = bf16[2432,5632]{1,0:T(8,128)(2,1)} fusion(bf16[2432,2048]{1,0:T(8,128)(2,1)} %get-tuple-element.43, bf16[2048,5632]{1,0:T(8,128)(2,1)} %get-tuple-element.47), kind=kOutput, calls=%fused_computation.72 | convolution fusion | flops 56116707328 | bytes 60424192 | tf_op jit(solution)/shard_map/cond/branch_1_fun/dot_general | solution.py:129
  363.4 62.2 %convolution_convert_fusion.8 = bf16[2432,5632]{1,0:T(8,128)(2,1)} fusion(bf16[2432,2048]{1,0:T(8,128)(2,1)} %get-tuple-element.44, bf16[5632,2048]{1,0:T(8,128)(2,1)S(1)} %bitcast.119), kind=kOutput, calls=%fused_computation.74 | convolution fusion | flops 56116707328 | bytes 60424192 | tf_op jit(solution)/shard_map/cond/branch_1_fun/dot_general | solution.py:129
  425.5 71.0 %convert_bitcast_fusion.1 = bf16[1,2048,5632]{2,1,0:T(8,128)(2,1)} fusion(bf16[2432,2048]{1,0:T(8,128)(2,1)} %get-tuple-element.43, bf16[2432,5632]{1,0:T(8,128)(2,1)} %convolution_convert_fusion.8, bf16[2432,5632]{1,0:T(8,128)(2,1)} %convolution_convert_fusion.6), kind=kOutput, calls=%fused_computation.79 | convolution fusion | flops 56224120832 | bytes 87818240 | tf_op jit(solution)/shard_map/cond/branch_1_fun/dot_general | solution.py:129
  496.6 61.3 %convolution_convert_fusion.7 = bf16[2432,5632]{1,0:T(8,128)(2,1)} fusion(bf16[2432,2048]{1,0:T(8,128)(2,1)} %get-tuple-element.43, bf16[2048,5632]{1,0:T(8,128)(2,1)S(1)} %copy-done.3), kind=kOutput, calls=%fused_computation.73 | convolution fusion | flops 56116707328 | bytes 60424192 | tf_op jit(solution)/shard_map/cond/branch_1_fun/dot_general | solution.py:129
  557.9 73.6 %convert_bitcast_fusion.2 = bf16[1,2048,5632]{2,1,0:T(8,128)(2,1)} fusion(bf16[2432,2048]{1,0:T(8,128)(2,1)} %get-tuple-element.43, bf16[2432,5632]{1,0:T(8,128)(2,1)} %convolution_convert_fusion.7, bf16[2432,5632]{1,0:T(8,128)(2,1)} %convolution_convert_fusion.8, bf16[2432,5632]{1,0:T(8,128)(2,1)} %convolution_convert_fusion.6), kind=kOutput, calls=%fused_computation.80 | convolution fusion | flops 56292605952 | bytes 115212288 | tf_op jit(solution)/shard_map/cond/branch_1_fun/dot_general | solution.py:129
  631.6 76.6 %convert_bitcast_fusion = bf16[1,5632,2048]{2,1,0:T(8,128)(2,1)} fusion(bf16[2432,2048]{1,0:T(8,128)(2,1)S(1)} %copy-done.8, bf16[2432,5632]{1,0:T(8,128)(2,1)} %convolution_convert_fusion.7, bf16[2432,5632]{1,0:T(8,128)(2,1)} %convolution_convert_fusion.6), kind=kOutput, calls=%fused_computation.78 | convolution fusion | flops 56224120832 | bytes 87818240 | tf_op jit(solution)/shard_map/cond/branch_1_fun/dot_general | solution.py:129
  708.4 0.8 copy-done.1
  (89 shorter events, 3.5 us)
Async XLA Ops:
  7.2 7.0 copy-start
  7.2 236.3 %all-gather.2.cloned.1.call-start = ((), (), s32[]{:S(2)}) async-start(), calls=%async_computation.2 | async-start | bytes 67371008 | tf_op jit(solution)/shard_map/all_gather | solution.py:259
  20.0 42.3 %all-to-all-start = ((bf16[8,16,4096]{2,1,0:T(8,128)(2,1)}), bf16[8,16,4096]{2,1,0:T(8,128)(2,1)S(1)}, u32[]{:S(2)}, u32[]{:S(2)}) async-start(bf16[8,16,4096]{2,1,0:T(8,128)(2,1)} %pad_maximum_fusion), calls=%async_computation | async-start | bytes 2097152 | tf_op jit(solution)/shard_map/all_to_all | solution.py:277
  62.3 57.2 %copy-start.4 = (bf16[32,2048]{1,0:T(8,128)(2,1)S(1)}, bf16[32,2048]{1,0:T(8,128)(2,1)}, u32[]{:S(2)}) copy-start(bf16[32,2048]{1,0:T(8,128)(2,1)} %param.11) | copy-start | bytes 393220
  62.3 59.8 %copy-start.7 = (s32[32,2]{0,1:T(2,128)S(1)}, s32[32,2]{0,1:T(2,128)}, u32[]{:S(2)}) copy-start(s32[32,2]{0,1:T(2,128)} %param.12) | copy-start | bytes 772
  62.3 85.1 %copy-start.5 = (bf16[32,2048]{1,0:T(8,128)(2,1)S(1)}, bf16[32,2048]{1,0:T(8,128)(2,1)}, u32[]{:S(2)}) copy-start(bf16[32,2048]{1,0:T(8,128)(2,1)} %param.10) | copy-start | bytes 393220
  62.3 85.1 %copy-start.6 = (f32[2048]{0:T(1024)S(1)}, f32[2048]{0:T(1024)}, u32[]{:S(2)}) copy-start(f32[2048]{0:T(1024)} %param.13) | copy-start | bytes 24580
  114.0 31.0 %all-to-all-start.1 = ((bf16[8,16,4096]{2,1,0:T(8,128)(2,1)}), bf16[8,16,4096]{2,1,0:T(8,128)(2,1)S(1)}, u32[]{:S(2)}, u32[]{:S(2)}) async-start(bf16[8,16,4096]{2,1,0:T(8,128)(2,1)} %bitcast.14), calls=%async_computation.1 | async-start | bytes 2097152 | tf_op jit(solution)/shard_map/all_to_all | solution.py:280
  252.2 111.2 %slice-start.6 = ((s8[23068672]{0:T(1024)(128)(4,1)}), s8[2097152]{0:T(1024)(128)(4,1)S(1)}, s32[]{:S(2)}) async-start(s8[23068672]{0:T(1024)(128)(4,1)} %bitcast.118), calls=%async_computation.9 | async-start | bytes 4194304 | tf_op jit(solution)/shard_map/cond
  298.1 65.2 %slice-start.7 = ((s8[23068672]{0:T(1024)(128)(4,1)}), s8[4194304]{0:T(1024)(128)(4,1)S(1)}, s32[]{:S(2)}) async-start(s8[23068672]{0:T(1024)(128)(4,1)} %bitcast.118), calls=%async_computation.10 | async-start | bytes 8388608 | tf_op jit(solution)/shard_map/cond
  298.1 65.2 %slice-start.8 = ((s8[23068672]{0:T(1024)(128)(4,1)}), s8[4194304]{0:T(1024)(128)(4,1)S(1)}, s32[]{:S(2)}) async-start(s8[23068672]{0:T(1024)(128)(4,1)} %bitcast.118), calls=%async_computation.11 | async-start | bytes 8388608 | tf_op jit(solution)/shard_map/cond
  298.1 65.2 %slice-start.9 = ((s8[23068672]{0:T(1024)(128)(4,1)}), s8[4194304]{0:T(1024)(128)(4,1)S(1)}, s32[]{:S(2)}) async-start(s8[23068672]{0:T(1024)(128)(4,1)} %bitcast.118), calls=%async_computation.12 | async-start | bytes 8388608 | tf_op jit(solution)/shard_map/cond
  298.2 65.2 %slice-start.10 = ((s8[23068672]{0:T(1024)(128)(4,1)}), s8[4194304]{0:T(1024)(128)(4,1)S(1)}, s32[]{:S(2)}) async-start(s8[23068672]{0:T(1024)(128)(4,1)} %bitcast.118), calls=%async_computation.13 | async-start | bytes 8388608 | tf_op jit(solution)/shard_map/cond
  298.2 65.2 %slice-start.11 = ((s8[23068672]{0:T(1024)(128)(4,1)}), s8[4194304]{0:T(1024)(128)(4,1)S(1)}, s32[]{:S(2)}) async-start(s8[23068672]{0:T(1024)(128)(4,1)} %bitcast.118), calls=%async_computation.14 | async-start | bytes 8388608 | tf_op jit(solution)/shard_map/cond
  425.5 71.0 %copy-start.3 = (bf16[2048,5632]{1,0:T(8,128)(2,1)S(1)}, bf16[2048,5632]{1,0:T(8,128)(2,1)}, u32[]{:S(2)}) copy-start(bf16[2048,5632]{1,0:T(8,128)(2,1)} %get-tuple-element.46) | copy-start | bytes 69206016 | tf_op jit(solution)/shard_map/cond
  557.9 73.6 %copy-start.8 = (bf16[2432,2048]{1,0:T(8,128)(2,1)S(1)}, bf16[2432,2048]{1,0:T(8,128)(2,1)}, u32[]{:S(2)}) copy-start(bf16[2432,2048]{1,0:T(8,128)(2,1)} %get-tuple-element.44) | copy-start | bytes 29884420 | tf_op jit(solution)/shard_map/cond
  708.4 0.8 copy-start.1
Sparse Core Ops, SparseCore 0:
  12.2 231.3 all-gather.1

commit v2 on v1

--- a/solution.py
+++ b/solution.py
@@ -11,7 +11,9 @@
 LANES = 128
 GROUP = 256
 ALIGN = 16
-CAP_SMALL = 256
+TILE = 256
+FIRST_ROWS = 1024
+LAST_ROWS = 1280
 F32 = jnp.float32
 BF16 = jnp.bfloat16
 
@@ -144,17 +146,19 @@
 def ffn_kernel(rows_ref, wg_ref, wu_ref, wd_ref, out_ref, o_acc, d_acc):
     step = pl.program_id(0)
     width = wg_ref.shape[0]
+    half = wg_ref.shape[1] // 2
     xn, dp = rows_ref[:, :width], rows_ref[:, width:]
-    wg, wu, wd = wg_ref[...], wu_ref[...], wd_ref[...]
-    act, d_gate, d_up = expert_math(dot(xn, wg, ((1,), (0,))), dot(xn, wu, ((1,), (0,))), dot(dp, wd, ((1,), (1,))))
 
     @pl.when(step == 0)
     def _():
         o_acc[...] = jnp.zeros_like(o_acc)
         d_acc[...] = jnp.zeros_like(d_acc)
 
-    o_acc[...] += dot(act, wd, ((1,), (0,)))
-    d_acc[...] += dot(d_gate, wg, ((1,), (1,))) + dot(d_up, wu, ((1,), (1,)))
+    cols = [slice(0, half), slice(half, 2 * half)]
+    mid = [expert_math(dot(xn, wg_ref[:, c], ((1,), (0,))), dot(xn, wu_ref[:, c], ((1,), (0,))), dot(dp, wd_ref[c, :], ((1,), (1,)))) for c in cols]
+    act, d_gate, d_up = (jnp.concatenate(parts, axis=1) for parts in zip(*mid))
+    o_acc[...] += dot(act, wd_ref[...], ((1,), (0,)))
+    d_acc[...] += dot(d_gate, wg_ref[...], ((1,), (1,))) + dot(d_up, wu_ref[...], ((1,), (1,)))
 
     @pl.when(step == pl.num_programs(0) - 1)
     def _():
@@ -181,11 +185,12 @@
     )(rows, wg, wu, wd)
 
 
-def pack_kernel(cap, off_ref, first_ref, rows_ref, pos_ref, gate_ref, xn_out, dp_out, xn_buf, dp_buf, sem):
+def pack_kernel(cap, n_early, info_ref, off_ref, early_ref, late_ref, pos_ref, gate_ref, xn_out, dp_out, xn_buf, dp_buf, sem):
     g = pl.program_id(0)
+    first = info_ref[0]
     width = xn_buf.shape[1]
     tile = xn_buf.shape[0] - cap
-    off = off_ref[g] - first_ref[0]
+    off = off_ref[g] - first
     base = pl.multiple_of(jnp.clip(lax.div(off, ALIGN) * ALIGN, 0, cap), ALIGN)
 
     @pl.when(g == 0)
@@ -193,17 +198,26 @@
         xn_buf[...] = jnp.zeros_like(xn_buf)
         dp_buf[...] = jnp.zeros_like(dp_buf)
 
-    row_id = lax.broadcasted_iota(jnp.int32, (tile, GROUP), 0) + base
-    hit = row_id == pos_ref[0] - first_ref[0]
-    pick = hit.astype(F32).astype(BF16)
-    gate = jnp.sum(jnp.where(hit, gate_ref[0], 0.0), axis=1, keepdims=True)
-    xn = dot(pick, rows_ref[:, :width], ((1,), (0,))).astype(BF16)
-    dp = (dot(pick, rows_ref[:, width:], ((1,), (0,))) * gate).astype(BF16)
-    keep = lax.broadcasted_iota(jnp.int32, (ALIGN, width), 0) + base < off
-    for buf, new in ((xn_buf, xn), (dp_buf, dp)):
-        head = pl.ds(base, ALIGN)
-        buf[head, :] = jnp.where(keep, buf[head, :].astype(F32), new[:ALIGN].astype(F32)).astype(BF16)
-        buf[pl.ds(pl.multiple_of(base + ALIGN, ALIGN), tile - ALIGN), :] = new[ALIGN:]
+    def add(rows_ref):
+        row_id = lax.broadcasted_iota(jnp.int32, (tile, GROUP), 0) + base
+        hit = row_id == pos_ref[0] - first
+        pick = hit.astype(F32).astype(BF16)
+        gate = jnp.sum(jnp.where(hit, gate_ref[0], 0.0), axis=1, keepdims=True)
+        xn = dot(pick, rows_ref[:, :width], ((1,), (0,))).astype(BF16)
+        dp = (dot(pick, rows_ref[:, width:], ((1,), (0,))) * gate).astype(BF16)
+        keep = lax.broadcasted_iota(jnp.int32, (ALIGN, width), 0) + base < off
+        for buf, new in ((xn_buf, xn), (dp_buf, dp)):
+            head = pl.ds(base, ALIGN)
+            buf[head, :] = jnp.where(keep, buf[head, :].astype(F32), new[:ALIGN].astype(F32)).astype(BF16)
+            buf[pl.ds(pl.multiple_of(base + ALIGN, ALIGN), tile - ALIGN), :] = new[ALIGN:]
+
+    @pl.when(jnp.logical_and(g >= info_ref[1], g < n_early))
+    def _():
+        add(early_ref)
+
+    @pl.when(jnp.logical_and(g >= info_ref[1], g >= n_early))
+    def _():
+        add(late_ref)
 
     @pl.when(g == pl.num_programs(0) - 1)
     def _():
@@ -214,25 +228,95 @@
             copy.wait()
 
 
-def pack_rows(rows, offsets, first, pos, gates, cap, most):
-    total, width = rows.shape[0], rows.shape[1] // 2
-    n_group = total // GROUP
-    tile = most + ALIGN
-    small = pl.BlockSpec((1, 1, GROUP), lambda g, *_: (g, 0, 0))
+def pack_rows(early, late, offsets, first, start, n_group, pos, gates, cap):
+    width = early.shape[1] // 2
+    n_early, n_late = early.shape[0] // GROUP, late.shape[0] // GROUP
+    tile = GROUP + ALIGN
+    small = pl.BlockSpec((1, 1, GROUP), lambda g, info, off: (jnp.maximum(g, info[1]), 0, 0))
     return pl.pallas_call(
-        functools.partial(pack_kernel, cap),
+        functools.partial(pack_kernel, cap, n_early),
         grid_spec=pltpu.PrefetchScalarGridSpec(
             num_scalar_prefetch=2,
             grid=(n_group,),
-            in_specs=[pl.BlockSpec((GROUP, 2 * width), lambda g, *_: (g, 0)), small, small],
+            in_specs=[
+                pl.BlockSpec((GROUP, 2 * width), lambda g, info, off: (jnp.minimum(jnp.maximum(g, info[1]), n_early - 1), 0)),
+                pl.BlockSpec((GROUP, 2 * width), lambda g, info, off: (jnp.clip(g - n_early, 0, n_late - 1), 0)),
+                small, small],
             out_specs=[pl.BlockSpec(memory_space=pl.ANY), pl.BlockSpec(memory_space=pl.ANY)],
             scratch_shapes=[pltpu.VMEM((cap + tile, width), BF16), pltpu.VMEM((cap + tile, width), BF16), pltpu.SemaphoreType.DMA((2,))],
         ),
         out_shape=[jax.ShapeDtypeStruct((cap, width), BF16)] * 2,
         compiler_params=pltpu.CompilerParams(dimension_semantics=("arbitrary",), vmem_limit_bytes=50 * 2**20),
-        cost_estimate=pl.CostEstimate(flops=4 * tile * total * width, bytes_accessed=4 * total * width, transcendentals=0),
+        cost_estimate=pl.CostEstimate(flops=64 * tile * GROUP * width, bytes_accessed=64 * GROUP * width, transcendentals=0),
         name="pack_rows",
-    )(offsets, first, rows, pos, gates)
+    )(jnp.stack([jnp.asarray(first, jnp.int32), jnp.asarray(start, jnp.int32)]), offsets, early, late, pos, gates)
+
+
+def grads_kernel(n_part, xn_hbm, dp_hbm, wg_ref, wu_ref, wd_ref, *refs):
+    parts, (gg_ref, gu_ref, gd_ref, xn, xt, dp, act_t, d_gate, d_up, sem) = refs[:n_part], refs[n_part:]
+    rows, width = xn.shape
+    tiles = [slice(r, r + TILE) for r in range(0, rows, TILE)]
+
+    @pl.when(pl.program_id(0) == 0)
+    def _():
+        copies = [[pltpu.make_async_copy(src.at[pl.ds(t.start, TILE)], dst.at[pl.ds(t.start, TILE)], sem.at[k, i]) for i, t in enumerate(tiles)] for k, (src, dst) in enumerate(((xn_hbm, xn), (dp_hbm, dp)))]
+        for copy in copies[0] + copies[1]:
+            copy.start()
+        for copy, t in zip(copies[0], tiles):
+            copy.wait()
+            xt[:, t] = xn[t, :].T
+        for copy in copies[1]:
+            copy.wait()
+
+    wg, wu, wd = wg_ref[...], wu_ref[...], wd_ref[...]
+    for t in tiles:
+        act, d_gate[t, :], d_up[t, :] = expert_math(dot(xn[t, :], wg, ((1,), (0,))), dot(xn[t, :], wu, ((1,), (0,))), dot(dp[t, :], wd, ((1,), (1,))))
+        act_t[:, t] = act.T
+
+    def put(out, index, k, value):
+        if n_part:
+            value = value + parts[k][(0, *index)]
+        if out.dtype == F32:
+            out[(0, *index)] = value
+        else:
+            out[index] = value.astype(out.dtype)
+
+    wide = 2 * TILE if width % (2 * TILE) == 0 else TILE
+    for c in range(0, width, wide):
+        cut = slice(c, c + wide)
+        put(gg_ref, (cut, slice(None)), 0, dot(xt[cut, :], d_gate[...], ((1,), (0,))))
+        put(gu_ref, (cut, slice(None)), 1, dot(xt[cut, :], d_up[...], ((1,), (0,))))
+    for c in range(0, width, wide):
+        cut = slice(c, c + wide)
+        put(gd_ref, (slice(None), cut), 2, dot(act_t[...], dp[:, cut], ((1,), (0,))))
+
+
+def expert_grads(xn, dp, wg, wu, wd, parts, last):
+    rows, width = xn.shape
+    ff = wg.shape[1]
+    n_block = ff // TILE
+    hbm = pl.BlockSpec(memory_space=pl.ANY)
+    col = pl.BlockSpec((width, TILE), lambda j: (0, j))
+    row = pl.BlockSpec((TILE, width), lambda j: (j, 0))
+    col_part = pl.BlockSpec((1, width, TILE), lambda j: (j, 0, 0))
+    row_part = pl.BlockSpec((1, TILE, width), lambda j: (j, 0, 0))
+    part_specs = [col_part, col_part, row_part]
+    if last:
+        outs = [jax.ShapeDtypeStruct((width, ff), BF16)] * 2 + [jax.ShapeDtypeStruct((ff, width), BF16)]
+    else:
+        outs = [jax.ShapeDtypeStruct((n_block, width, TILE), F32)] * 2 + [jax.ShapeDtypeStruct((n_block, TILE, width), F32)]
+    return pl.pallas_call(
+        functools.partial(grads_kernel, len(parts)),
+        grid=(n_block,),
+        in_specs=[hbm, hbm, col, col, row] + part_specs[:len(parts)],
+        out_specs=[col, col, row] if last else part_specs,
+        out_shape=outs,
+        scratch_shapes=[pltpu.VMEM((rows, width), BF16), pltpu.VMEM((width, rows), BF16), pltpu.VMEM((rows, width), BF16), pltpu.VMEM((TILE, rows), BF16), pltpu.VMEM((rows, TILE), BF16), pltpu.VMEM((rows, TILE), BF16), pltpu.SemaphoreType.DMA((2, rows // TILE))],
+        input_output_aliases={} if last or not parts else {5: 0, 6: 1, 7: 2},
+        compiler_params=pltpu.CompilerParams(dimension_semantics=("arbitrary",), vmem_limit_bytes=62 * 2**20),
+        cost_estimate=pl.CostEstimate(flops=12 * rows * width * ff, bytes_accessed=12 * width * ff, transcendentals=0),
+        name="expert_grads",
+    )(xn, dp, wg, wu, wd, *parts)
 
 
 def solution(mesh):
@@ -248,7 +332,6 @@
         n_exp = w_router.shape[1]
         capacity = 4 * n_tok // n_exp
         total_tok = n_tok * n_dev
-        cap = min(2432, total_tok) if n_dp == 32 else CAP_SMALL
         dest_rows, slot_owner, loads = route_tables(expert_ids, n_exp, capacity)
         choice_hot = (expert_ids[:, :, None] == jnp.arange(n_exp, dtype=jnp.int32)).astype(F32)
 
@@ -256,7 +339,10 @@
         inv_rms = lax.rsqrt(jnp.mean(x_f32 * x_f32, axis=-1, keepdims=True) + EPS)
         x_hat = x_f32 * inv_rms
         x_norm = (x_hat * norm_gain).astype(BF16)
-        rows_all = lax.all_gather(jnp.concatenate([x_norm, grad_out], axis=1), all_axes, axis=0, tiled=True)
+        rows = jnp.concatenate([x_norm, grad_out], axis=1)
+        half = n_tok // 2
+        early = lax.all_gather(rows[:half], all_axes, axis=0, tiled=True)
+        late = lax.all_gather(rows[half:], all_axes, axis=0, tiled=True)
         xn_f32 = x_norm.astype(F32)
         router_probs = jax.nn.softmax(jnp.dot(xn_f32, w_router, preferred_element_type=F32), axis=-1)
         gate_vals = jnp.sum(router_probs[:, None, :] * choice_hot, axis=-1)
@@ -276,7 +362,7 @@
             jnp.take(d_picked, slot_owner, axis=0, mode="fill", fill_value=0)], axis=1)
         recv = lax.all_to_all(send.reshape(n_exp, capacity, 2 * width), "ep", 0, 0, tiled=True).reshape(n_exp * capacity, 2 * width)
         wg, wu, wd = w_gate[0], w_up[0], w_down[0]
-        done = local_ffn(recv, wg, wu, wd, 256)
+        done = local_ffn(recv, wg, wu, wd, 2 * TILE)
         back = lax.all_to_all(done.reshape(n_exp, capacity, 2 * width), "ep", 0, 0, tiled=True).reshape(n_exp * capacity, 2 * width)
         both = jnp.take(back, dest_rows, axis=0).reshape(n_tok, 2, 2 * width)
         picked, d_xn_exp = both[..., :width], both[..., width:]
@@ -303,26 +389,35 @@
 
         me = lax.axis_index("ep")
         mine = ids_all == me
-        member = jnp.any(mine, axis=1).reshape(-1, GROUP)
-        gate_me = jnp.sum(jnp.where(mine, gates_all, 0.0), axis=1).reshape(-1, 1, GROUP)
-        rank = jnp.cumsum(member.astype(jnp.int32), axis=1)
+        member = jnp.any(mine, axis=1)
+        gate_me = jnp.sum(jnp.where(mine, gates_all, 0.0), axis=1)
+
+        def by_group(a):
+            return jnp.concatenate([a[:, :half].reshape(-1, GROUP), a[:, half:].reshape(-1, GROUP)], axis=0)
+
+        rank = jnp.cumsum(by_group(member.astype(jnp.int32)), axis=1)
         counts = rank[:, -1]
         offsets = jnp.cumsum(counts) - counts
         n_rows = offsets[-1] + counts[-1]
-        pos = jnp.where(member, offsets[:, None] + rank - 1, -(2**24)).reshape(-1, 1, GROUP)
-
-        def one_pass(first):
-            xn, dp = pack_rows(rows_all, offsets, jnp.full((1,), first, jnp.int32), pos, gate_me, cap, GROUP // n_tok * capacity)
-            act, d_gate, d_up = expert_math(dot(xn, wg, ((1,), (0,))), dot(xn, wu, ((1,), (0,))), dot(dp, wd, ((1,), (1,))))
-            return dot(xn, d_gate, ((0,), (0,))), dot(xn, d_up, ((0,), (0,))), dot(act, dp, ((0,), (0,)))
-
-        def few():
-            return tuple(g.astype(BF16)[None] for g in one_pass(0))
-
-        def many():
-            return tuple((a + b).astype(BF16)[None] for a, b in zip(one_pass(0), one_pass(cap)))
-
-        g_gate, g_up, g_down = lax.cond(n_rows <= cap, few, many)
+        pos = jnp.where(by_group(member), offsets[:, None] + rank - 1, -(2**24))[:, None]
+        gate_me = by_group(gate_me)[:, None]
+        n_group, n_early = pos.shape[0], n_dev * half // GROUP
+        in_early = jnp.sum(counts[:n_early])
+        split = jnp.minimum(in_early, FIRST_ROWS)
+        extra = jnp.maximum(n_rows - split - LAST_ROWS + FIRST_ROWS - 1, 0) // FIRST_ROWS
+        pos, gate_me, offsets, split, grad_router = lax.optimization_barrier((pos, gate_me, offsets, split, grad_router))
+
+        parts = expert_grads(*pack_rows(early, early, offsets[:n_early], 0, 0, n_early, pos, gate_me, FIRST_ROWS), wg, wu, wd, (), False)
+
+        def more(k, parts):
+            xn, dp = pack_rows(early, late, offsets, split + k * FIRST_ROWS, 0, n_group, pos, gate_me, FIRST_ROWS)
+            return tuple(expert_grads(xn, dp, wg, wu, wd, tuple(parts), False))
+
+        parts = lax.fori_loop(0, extra, more, tuple(parts))
+        split = split + extra * FIRST_ROWS
+        start = jnp.minimum(jnp.sum((offsets + counts <= split).astype(jnp.int32)), n_group - 1)
+        grads = expert_grads(*pack_rows(early, late, offsets, split, start, n_group, pos, gate_me, LAST_ROWS), wg, wu, wd, parts, True)
+        g_gate, g_up, g_down = (g[None] for g in grads)
         return out_hidden, aux_loss, grad_hidden, grad_gain, grad_router, g_gate, g_up, g_down
 
     tok_spec = P(all_axes, None)

time: 725 us -> 621 us (0.86)
  matrix products: 411 us -> 0.81 us
  Pallas kernels: 156 us -> 511 us
  waiting for transfers between devices: 85.9 us -> 34.8 us
    dot_general x6 -> x0, matrix products: 410 us -> none  [dot(): return lax.dot_general(a, b, (dims, ((), ())), preferred_element_type=F32)]
    pallas_call x1 -> x4, Pallas kernels: 46 us -> 419 us  [the longest x2 362 us: expert_grads(): pl.pallas_call(functools.partial(grads_kernel, len(parts)), grid=(n_block...]
    all_gather x1 -> x2, waiting for transfers between devices: 62.9 us -> 13.8 us  [the longest x1 13.8 us: local_step(): early = lax.all_gather(rows[:half], all_axes, axis=0, tiled=True)]
    pallas_call x1, Pallas kernels: 51.7 us -> 36.8 us  [local_ffn(): pl.pallas_call(ffn_kernel, grid=(ff // block,), out_shape=jax.ShapeDtypeS...]
  transfers between devices with their start and end apart: 3 -> 4, of which waited for: 2 -> 2; matrix products, arithmetic and copies ran while one was open for 3% -> 4% of each run, Pallas kernels for 15% -> 45%
where the time goes in v2:
time: 621 us; the launch traced here: 614 us
  Pallas kernels  511 us (82%)
  waiting for transfers between devices  34.8 us (6%)
  between operations  19.4 us (3%)
  other arithmetic  15.1 us (2%)
  local copies, waits for them, and re-layouts  13 us (2%)
  starting transfers between devices  11.9 us (2%)
  loops' own time  8.39 us (1%)
    pallas_call x2, Pallas kernels, expert_grads(): pl.pallas_call(functools.partial(grads_kernel, len(parts)), grid=(n_block...  362 us
    pallas_call x2, Pallas kernels, pack_rows(): pl.pallas_call(functools.partial(pack_kernel, cap, n_early), grid_spec=pl...  56.4 us
    pallas_call x1, Pallas kernels, local_ffn(): pl.pallas_call(ffn_kernel, grid=(ff // block,), out_shape=jax.ShapeDtypeS...  36.8 us
    pallas_call x1, Pallas kernels, gather_rows(): pl.pallas_call(functools.partial(gather_kernel, n_y, n_z, n_ep), out_shap...  30.5 us
    pallas_call x1, Pallas kernels, reduce_rows(): pl.pallas_call(functools.partial(reduce_kernel, n_y, n_z, n_ep), out_shap...  25.2 us
    all_to_all x1, waiting for transfers between devices, local_step(): lax.all_to_all(done.reshape(n_exp, capacity, 2 * width), 'ep', 0, 0, tile...  20.3 us
    all_gather x1, waiting for transfers between devices, local_step(): early = lax.all_gather(rows[:half], all_axes, axis=0, tiled=True)  13.8 us
  transfers between devices with their start and end apart: 4, of which 2 were waited for; matrix products, arithmetic and copies ran while one was open for 4% of the time, Pallas kernels for 45%

profile of v2, /device:TPU:1, one launch (start us, length us, event | category | flops | bytes accessed | tf_op | source)
XLA Modules:
  0.0 614.4 jit_solution(5793417234752578073)
XLA Ops:
  7.2 1.0 fusion.16
  8.3 1.0 fusion.9
  9.3 1.6 pad_maximum_fusion.1
  11.0 0.7 all-gather.5.cloned.1.call-update
  11.7 0.8 copy.82
  12.6 0.7 select_reduce_fusion.3
  13.5 1.1 mul.151.clone
  14.7 0.4 mul.152
  15.2 0.8 convert_bitcast_fusion
  16.3 0.2 select_reduce_fusion.1
  16.5 0.8 scatter_custom_fusion
  17.3 0.9 gather_fusion
  18.5 0.9 gather_fusion.1
  19.6 1.1 pad_maximum_fusion
  20.7 6.6 %all-to-all-start = ((bf16[8,16,4096]{2,1,0:T(8,128)(2,1)}), bf16[8,16,4096]{2,1,0:T(8,128)(2,1)S(1)}, u32[]{:S(2)}, u32[]{:S(2)}) async-start(bf16[8,16,4096]{2,1,0:T(8,128)(2,1)} %pad_maximum_fusion), calls=%async_computation | async-start | bytes 2097152 | tf_op jit(solution)/shard_map/all_to_all | solution.py:363
  27.5 0.6 maximum_bitcast_fusion.row_ref
  28.1 30.5 %gather_rows.1 = f32[256,1,128]{2,1,0:T(1,128)} custom-call(f32[1,1,128]{2,1,0:T(1,128)} %maximum_bitcast_fusion.row_ref), custom_call_target="tpu_custom_call" | custom-call | tf_op jit(solution)/shard_map/gather_rows/pallas_call | solution.py:79
  58.6 1.1 fusion.28
  60.3 0.6 reduce-window.10
  60.9 0.2 slice_reduce_fusion
  61.9 0.7 slice_reduce_fusion.1
  62.6 0.2 slice_reduce_fusion.2
  62.9 36.8 %local_ffn.1 = bf16[128,4096]{1,0:T(8,128)(2,1)} custom-call(bf16[128,4096]{1,0:T(8,128)(2,1)S(1)} %bitcast.61, bf16[2048,5632]{1,0:T(8,128)(2,1)} %bitcast.63, bf16[2048,5632]{1,0:T(8,128)(2,1)} %bitcast.66, bf16[5632,2048]{1,0:T(8,128)(2,1)} %bitcast.69), custom_call_target="tpu_custom_call" | custom-call | flops 17716740096 | bytes 69206016 | tf_op jit(solution)/shard_map/local_ffn/pallas_call | solution.py:175
  99.7 5.2 all-to-all-start.1
  105.1 0.6 slice.126
  106.3 0.6 slice.98
  108.8 0.2 convert_reduce_fusion
  109.2 20.3 %all-to-all-done.1 = bf16[8,16,4096]{2,1,0:T(8,128)(2,1)S(1)} async-done(((bf16[8,16,4096]{2,1,0:T(8,128)(2,1)}), bf16[8,16,4096]{2,1,0:T(8,128)(2,1)S(1)}, u32[]{:S(2)}, u32[]{:S(2)}) %all-to-all-start.1) | async-done | bytes 1048608 | tf_op jit(solution)/shard_map/all_to_all | solution.py:366
  129.5 0.9 gather_fusion.2
  130.4 0.3 gather.23
  130.7 0.6 copy_select_fusion
  131.4 0.2 fusion.4
  131.7 0.2 convolution_bitcast_fusion
  131.9 0.5 fusion.11
  132.4 0.7 select_maximum_fusion
  133.1 25.2 %reduce_rows.1 = f32[8,24,128]{2,1,0:T(8,128)} custom-call(f32[8,24,128]{2,1,0:T(8,128)} %bitcast.78), custom_call_target="tpu_custom_call" | custom-call | tf_op jit(solution)/shard_map/reduce_rows/pallas_call | solution.py:119
  158.3 0.9 slice.96
  159.2 0.6 slice_bitcast_fusion.2
  159.8 1.3 slice.114
  161.1 0.6 fusion.22
  162.4 1.3 fusion.25
  164.4 0.8 fusion.15
  165.2 13.8 %all-gather.3.cloned.1.call-done.early_ref.late_ref = bf16[4096,4096]{1,0:T(8,128)(2,1)} async-done(((bf16[16,4096]{1,0:T(8,128)(2,1)}), bf16[4096,4096]{1,0:T(8,128)(2,1)}) %all-gather.3.cloned.1.call-update) | async-done | bytes 33554448 | tf_op jit(solution)/shard_map/all_gather | solution.py:344
  179.0 27.4 %pack_rows.4 = (bf16[1024,2048]{1,0:T(8,128)(2,1)}, bf16[1024,2048]{1,0:T(8,128)(2,1)}) custom-call(s32[2]{0:T(128)S(1)} %broadcast_5_info_ref.2.info_ref, s32[16]{0:T(128)S(1)} %bitcast.82, bf16[4096,4096]{1,0:T(8,128)(2,1)} %all-gather.3.cloned.1.call-done.early_ref.late_ref, bf16[4096,4096]{1,0:T(8,128)(2,1)} %all-gather.3.cloned.1.call-done.early_ref.late_ref, ...), custom_call_target="tpu_custom_call" | custom-call | flops 9126805504 | bytes 33554432 | tf_op jit(solution)/shard_map/pack_rows/pallas_call | solution.py:236
  206.4 158.4 %expert_grads.3 = (f32[22,2048,256]{2,1,0:T(8,128)}, f32[22,2048,256]{2,1,0:T(8,128)}, f32[22,256,2048]{2,1,0:T(8,128)}) custom-call(bf16[1024,2048]{1,0:T(8,128)(2,1)} %get-tuple-element.110.xn_hbm, bf16[1024,2048]{1,0:T(8,128)(2,1)} %get-tuple-element.111.dp_hbm, bf16[2048,5632]{1,0:T(8,128)(2,1)} %bitcast.64, bf16[2048,5632]{1,0:T(8,128)(2,1)} %bitcast.67, ...), custom_call_target="tpu_custom_call" | custom-call | flops 141733920768 | bytes 138412032 | tf_op jit(solution)/shard_map/expert_grads/pallas_call | solution.py:308
  364.8 8.4 %while.14 = (s32[]{:T(128)}, f32[22,2048,256]{2,1,0:T(8,128)}, f32[22,2048,256]{2,1,0:T(8,128)}, f32[22,256,2048]{2,1,0:T(8,128)}, s32[]{:T(128)}, /*index=5*/s3...) while((s32[]{:T(128)}, f32[22,2048,256]{2,1,0:T(8,128)}, ...), condition=%wide.region_24.25_spmd, body=%wide.region_23.24_spmd.sunk | while | flops 150860726272 | bytes 171966672 | solution.py:416
  373.2 29.0 %pack_rows.3 = (bf16[1280,2048]{1,0:T(8,128)(2,1)}, bf16[1280,2048]{1,0:T(8,128)(2,1)}) custom-call(s32[2]{0:T(128)S(1)} %pad_add_fusion.3.info_ref, s32[32]{0:T(128)S(1)} %get-tuple-element.344, bf16[4096,4096]{1,0:T(8,128)(2,1)} %get-tuple-element.331, bf16[4096,4096]{1,0:T(8,128)(2,1)} %get-tuple-element.333, s32[32,1,256]{2,1,0:T(1,128)S(1)} %get-tuple-element.339, ...), custom_call_target="tpu_custom_call" | custom-call | flops 9126805504 | bytes 33554432 | tf_op jit(solution)/shard_map/pack_rows/pallas_call | solution.py:236
  402.3 203.8 %expert_grads.4 = (bf16[2048,5632]{1,0:T(8,128)(2,1)}, bf16[2048,5632]{1,0:T(8,128)(2,1)}, bf16[5632,2048]{1,0:T(8,128)(2,1)}) custom-call(bf16[1280,2048]{1,0:T(8,128)(2,1)} %get-tuple-element.108.xn_hbm, bf16[1280,2048]{1,0:T(8,128)(2,1)} %get-tuple-element.109.dp_hbm, bf16[2048,5632]{1,0:T(8,128)(2,1)} %get-tuple-element.335, ...), custom_call_target="tpu_custom_call" | custom-call | flops 177167400960 | bytes 138412032 | tf_op jit(solution)/shard_map/expert_grads/pallas_call | solution.py:308
  (87 shorter events, 4.1 us)
Async XLA Ops:
  7.2 5.3 copy-start
  7.2 171.8 %all-gather.3.cloned.1.call-start = ((), (), s32[]{:S(2)}) async-start(), calls=%async_computation.2 | async-start | bytes 33685504 | tf_op jit(solution)/shard_map/all_gather | solution.py:344
  10.9 353.9 %all-gather.5.cloned.1.call-start = ((), (), s32[]{:S(2)}) async-start(), calls=%async_computation.3 | async-start | bytes 33685504 | tf_op jit(solution)/shard_map/all_gather | solution.py:345
  20.7 42.2 %all-to-all-start = ((bf16[8,16,4096]{2,1,0:T(8,128)(2,1)}), bf16[8,16,4096]{2,1,0:T(8,128)(2,1)S(1)}, u32[]{:S(2)}, u32[]{:S(2)}) async-start(bf16[8,16,4096]{2,1,0:T(8,128)(2,1)} %pad_maximum_fusion), calls=%async_computation | async-start | bytes 2097152 | tf_op jit(solution)/shard_map/all_to_all | solution.py:363
  62.9 42.1 %copy-start.2 = (bf16[32,2048]{1,0:T(8,128)(2,1)S(1)}, bf16[32,2048]{1,0:T(8,128)(2,1)}, u32[]{:S(2)}) copy-start(bf16[32,2048]{1,0:T(8,128)(2,1)} %param.11) | copy-start | bytes 393220
  62.9 46.2 %copy-start.5 = (s32[32,2]{0,1:T(2,128)S(1)}, s32[32,2]{0,1:T(2,128)}, u32[]{:S(2)}) copy-start(s32[32,2]{0,1:T(2,128)} %param.12) | copy-start | bytes 772
  62.9 69.0 %copy-start.3 = (bf16[32,2048]{1,0:T(8,128)(2,1)S(1)}, bf16[32,2048]{1,0:T(8,128)(2,1)}, u32[]{:S(2)}) copy-start(bf16[32,2048]{1,0:T(8,128)(2,1)} %param.10) | copy-start | bytes 393220
  62.9 69.0 %copy-start.4 = (f32[2048]{0:T(1024)S(1)}, f32[2048]{0:T(1024)}, u32[]{:S(2)}) copy-start(f32[2048]{0:T(1024)} %param.13) | copy-start | bytes 24580
  99.7 29.8 %all-to-all-start.1 = ((bf16[8,16,4096]{2,1,0:T(8,128)(2,1)}), bf16[8,16,4096]{2,1,0:T(8,128)(2,1)S(1)}, u32[]{:S(2)}, u32[]{:S(2)}) async-start(bf16[8,16,4096]{2,1,0:T(8,128)(2,1)} %bitcast.9), calls=%async_computation.1 | async-start | bytes 2097152 | tf_op jit(solution)/shard_map/all_to_all | solution.py:366
  402.2 203.8 %copy-start.1 = (f32[2048,8]{0,1:T(8,128)S(1)}, f32[2048,8]{0,1:T(8,128)}, u32[]{:S(2)}) copy-start(f32[2048,8]{0,1:T(8,128)} %param.14) | copy-start | bytes 196612
Sparse Core Ops, SparseCore 0:
  12.3 166.6 all-gather.2
  183.3 148.2 all-gather.4

commit v3 on v1

--- a/solution.py
+++ b/solution.py
@@ -10,8 +10,11 @@
 AUX_COEF = 0.001
 LANES = 128
 GROUP = 256
+MOST_PER_GROUP = 128
 ALIGN = 16
-CAP_SMALL = 256
+TILE = 256
+USUAL_ROWS = 2304
+QUARTERS = 4
 F32 = jnp.float32
 BF16 = jnp.bfloat16
 
@@ -144,17 +147,19 @@
 def ffn_kernel(rows_ref, wg_ref, wu_ref, wd_ref, out_ref, o_acc, d_acc):
     step = pl.program_id(0)
     width = wg_ref.shape[0]
+    half = wg_ref.shape[1] // 2
     xn, dp = rows_ref[:, :width], rows_ref[:, width:]
-    wg, wu, wd = wg_ref[...], wu_ref[...], wd_ref[...]
-    act, d_gate, d_up = expert_math(dot(xn, wg, ((1,), (0,))), dot(xn, wu, ((1,), (0,))), dot(dp, wd, ((1,), (1,))))
 
     @pl.when(step == 0)
     def _():
         o_acc[...] = jnp.zeros_like(o_acc)
         d_acc[...] = jnp.zeros_like(d_acc)
 
-    o_acc[...] += dot(act, wd, ((1,), (0,)))
-    d_acc[...] += dot(d_gate, wg, ((1,), (1,))) + dot(d_up, wu, ((1,), (1,)))
+    cols = [slice(0, half), slice(half, 2 * half)]
+    mid = [expert_math(dot(xn, wg_ref[:, c], ((1,), (0,))), dot(xn, wu_ref[:, c], ((1,), (0,))), dot(dp, wd_ref[c, :], ((1,), (1,)))) for c in cols]
+    act, d_gate, d_up = (jnp.concatenate(parts, axis=1) for parts in zip(*mid))
+    o_acc[...] += dot(act, wd_ref[...], ((1,), (0,)))
+    d_acc[...] += dot(d_gate, wg_ref[...], ((1,), (1,))) + dot(d_up, wu_ref[...], ((1,), (1,)))
 
     @pl.when(step == pl.num_programs(0) - 1)
     def _():
@@ -181,20 +186,15 @@
     )(rows, wg, wu, wd)
 
 
-def pack_kernel(cap, off_ref, first_ref, rows_ref, pos_ref, gate_ref, xn_out, dp_out, xn_buf, dp_buf, sem):
+def pack_kernel(off_ref, rows_ref, pos_ref, gate_ref, xn_out, dp_out, xn_buf, dp_buf, sem):
     g = pl.program_id(0)
+    n_group = pl.num_programs(0)
     width = xn_buf.shape[1]
-    tile = xn_buf.shape[0] - cap
-    off = off_ref[g] - first_ref[0]
-    base = pl.multiple_of(jnp.clip(lax.div(off, ALIGN) * ALIGN, 0, cap), ALIGN)
-
-    @pl.when(g == 0)
-    def _():
-        xn_buf[...] = jnp.zeros_like(xn_buf)
-        dp_buf[...] = jnp.zeros_like(dp_buf)
-
+    tile = MOST_PER_GROUP + ALIGN
+    off = off_ref[g]
+    base = pl.multiple_of(lax.div(off, ALIGN) * ALIGN, ALIGN)
     row_id = lax.broadcasted_iota(jnp.int32, (tile, GROUP), 0) + base
-    hit = row_id == pos_ref[0] - first_ref[0]
+    hit = row_id == pos_ref[0]
     pick = hit.astype(F32).astype(BF16)
     gate = jnp.sum(jnp.where(hit, gate_ref[0], 0.0), axis=1, keepdims=True)
     xn = dot(pick, rows_ref[:, :width], ((1,), (0,))).astype(BF16)
@@ -205,34 +205,196 @@
         buf[head, :] = jnp.where(keep, buf[head, :].astype(F32), new[:ALIGN].astype(F32)).astype(BF16)
         buf[pl.ds(pl.multiple_of(base + ALIGN, ALIGN), tile - ALIGN), :] = new[ALIGN:]
 
-    @pl.when(g == pl.num_programs(0) - 1)
+    @pl.when(g == n_group - 1)
     def _():
-        copies = [pltpu.make_async_copy(xn_buf.at[pl.ds(0, cap)], xn_out, sem.at[0]), pltpu.make_async_copy(dp_buf.at[pl.ds(0, cap)], dp_out, sem.at[1])]
-        for copy in copies:
-            copy.start()
-        for copy in copies:
-            copy.wait()
-
-
-def pack_rows(rows, offsets, first, pos, gates, cap, most):
+        usual = USUAL_ROWS // TILE
+        zeros = jnp.zeros((TILE, width), BF16)
+        tail = pl.ds(pl.multiple_of(base + tile, ALIGN), TILE)
+        xn_buf[tail, :] = zeros
+        dp_buf[tail, :] = zeros
+        used = lax.div(off_ref[n_group] + TILE - 1, TILE)
+
+        def clear(t, carry):
+            rows = pl.ds(pl.multiple_of(t * TILE, TILE), TILE)
+            xn_buf[rows, :] = zeros
+            dp_buf[rows, :] = zeros
+            return carry
+
+        lax.fori_loop(used, usual, clear, 0)
+
+        def copies(t):
+            rows = pl.ds(pl.multiple_of(t * TILE, TILE), TILE)
+            return [pltpu.make_async_copy(buf.at[rows], out.at[rows], sem.at[k]) for k, (buf, out) in enumerate(((xn_buf, xn_out), (dp_buf, dp_out)))]
+
+        def begin(t, carry):
+            for copy in copies(t):
+                copy.start()
+            return carry
+
+        def end(t, carry):
+            for copy in copies(t):
+                copy.wait()
+            return carry
+
+        lax.fori_loop(0, jnp.maximum(used, usual), begin, 0)
+        lax.fori_loop(0, jnp.maximum(used, usual), end, 0)
+
+
+def pack_rows(rows, offsets, pos, gates, most):
     total, width = rows.shape[0], rows.shape[1] // 2
     n_group = total // GROUP
-    tile = most + ALIGN
-    small = pl.BlockSpec((1, 1, GROUP), lambda g, *_: (g, 0, 0))
-    return pl.pallas_call(
-        functools.partial(pack_kernel, cap),
+    small = pl.BlockSpec((1, 1, GROUP), lambda g, off: (g, 0, 0))
+    whole = pl.BlockSpec(memory_space=pl.ANY)
+    buf = pltpu.VMEM((max(most, USUAL_ROWS) + 2 * TILE + ALIGN, width), BF16)
+    out = jax.ShapeDtypeStruct((max(most, USUAL_ROWS), width), BF16)
+    return pl.pallas_call(
+        pack_kernel,
         grid_spec=pltpu.PrefetchScalarGridSpec(
-            num_scalar_prefetch=2,
+            num_scalar_prefetch=1,
             grid=(n_group,),
-            in_specs=[pl.BlockSpec((GROUP, 2 * width), lambda g, *_: (g, 0)), small, small],
-            out_specs=[pl.BlockSpec(memory_space=pl.ANY), pl.BlockSpec(memory_space=pl.ANY)],
-            scratch_shapes=[pltpu.VMEM((cap + tile, width), BF16), pltpu.VMEM((cap + tile, width), BF16), pltpu.SemaphoreType.DMA((2,))],
+            in_specs=[pl.BlockSpec((GROUP, 2 * width), lambda g, off: (g, 0)), small, small],
+            out_specs=[whole, whole],
+            scratch_shapes=[buf, buf, pltpu.SemaphoreType.DMA((2,))],
         ),
-        out_shape=[jax.ShapeDtypeStruct((cap, width), BF16)] * 2,
-        compiler_params=pltpu.CompilerParams(dimension_semantics=("arbitrary",), vmem_limit_bytes=50 * 2**20),
-        cost_estimate=pl.CostEstimate(flops=4 * tile * total * width, bytes_accessed=4 * total * width, transcendentals=0),
+        out_shape=[out, out],
+        compiler_params=pltpu.CompilerParams(dimension_semantics=("arbitrary",), vmem_limit_bytes=60 * 2**20),
+        cost_estimate=pl.CostEstimate(flops=4 * GROUP * total * width, bytes_accessed=4 * total * width, transcendentals=0),
         name="pack_rows",
-    )(offsets, first, rows, pos, gates)
+    )(offsets, rows, pos, gates)
+
+
+def grads_kernel(n_quarter, info_ref, xn_hbm, dp_hbm, wg_ref, wu_ref, wd_ref, *refs):
+    if n_quarter > 1:
+        out_ref, xn, xt, dp, act_t, d_gate, d_up, acc_g, acc_u, acc_d, tile_x, tile_p, sem = refs
+    else:
+        gg_ref, gu_ref, gd_ref, xn, xt, dp, act_t, d_gate, d_up, acc_g, acc_u, acc_d, tile_x, tile_p, sem = refs
+    rows, width = xn.shape
+    part = width // n_quarter
+    low = pl.multiple_of(info_ref[2] * part, part)
+    tiles = [slice(r, r + TILE) for r in range(0, rows, TILE)]
+
+    @pl.when(pl.program_id(0) == 0)
+    def _():
+        copies = [[pltpu.make_async_copy(src.at[pl.ds(t.start, TILE)], dst.at[pl.ds(t.start, TILE)], sem.at[k, i]) for i, t in enumerate(tiles)] for k, (src, dst) in enumerate(((xn_hbm, xn), (dp_hbm, dp)))]
+        for copy in copies[0] + copies[1]:
+            copy.start()
+        for acc in (acc_g, acc_u, acc_d):
+            acc[...] = jnp.zeros_like(acc)
+        for copy, t in zip(copies[0], tiles):
+            copy.wait()
+            xt[:, t] = xn[t, pl.ds(low, part)].T
+        for copy in copies[1]:
+            copy.wait()
+
+    wg, wu, wd = wg_ref[...], wu_ref[...], wd_ref[...]
+
+    def hidden_rows(x, p):
+        return expert_math(dot(x, wg, ((1,), (0,))), dot(x, wu, ((1,), (0,))), dot(p, wd, ((1,), (1,))))
+
+    @pl.when(info_ref[0] > rows // TILE)
+    def _():
+        for acc in (acc_g, acc_u, acc_d):
+            acc[...] = jnp.zeros_like(acc)
+
+        def more(t, carry):
+            at = pl.ds(pl.multiple_of(t * TILE, TILE), TILE)
+            copies = [pltpu.make_async_copy(xn_hbm.at[at], tile_x, sem.at[0, 0]), pltpu.make_async_copy(dp_hbm.at[at], tile_p, sem.at[1, 0])]
+            for copy in copies:
+                copy.start()
+            for copy in copies:
+                copy.wait()
+            act, dg, du = hidden_rows(tile_x[...], tile_p[...])
+            x, p = tile_x[:, pl.ds(low, part)], tile_p[:, pl.ds(low, part)]
+            acc_g[...] += dot(x, dg, ((0,), (0,)))
+            acc_u[...] += dot(x, du, ((0,), (0,)))
+            acc_d[...] += dot(act, p, ((0,), (0,)))
+            return carry
+
+        lax.fori_loop(rows // TILE, info_ref[0], more, 0)
+
+    for t in tiles:
+        act, d_gate[t, :], d_up[t, :] = hidden_rows(xn[t, :], dp[t, :])
+        act_t[:, t] = act.T
+
+    wide = 2 * TILE if part % (2 * TILE) == 0 else TILE
+    for c in range(0, part, wide):
+        cut = slice(c, c + wide)
+        new_g = (dot(xt[cut, :], d_gate[...], ((1,), (0,))) + acc_g[cut, :]).astype(BF16)
+        new_u = (dot(xt[cut, :], d_up[...], ((1,), (0,))) + acc_u[cut, :]).astype(BF16)
+        if n_quarter > 1:
+            out_ref[0, cut, :], out_ref[1, cut, :] = new_g, new_u
+        else:
+            gg_ref[cut, :], gu_ref[cut, :] = new_g, new_u
+    for c in range(0, part, wide):
+        cut = slice(c, c + wide)
+        if n_quarter > 1:
+            new_d = (dot(act_t[...], dp[:, pl.ds(pl.multiple_of(low + c, wide), wide)], ((1,), (0,))) + acc_d[:, cut]).astype(BF16)
+            for k in range(0, wide, TILE):
+                out_ref[2, slice(c + k, c + k + TILE), :] = new_d[:, k:k + TILE]
+        else:
+            gd_ref[:, cut] = (dot(act_t[...], dp[:, cut], ((1,), (0,))) + acc_d[:, cut]).astype(BF16)
+
+
+def expert_grads(info, xn, dp, wg, wu, wd, n_block, n_quarter):
+    width, ff = wg.shape
+    rows = USUAL_ROWS
+    part = width // n_quarter
+    hbm = pl.BlockSpec(memory_space=pl.ANY)
+    if n_quarter > 1:
+        col = pl.BlockSpec((width, TILE), lambda j, info: (0, info[1]))
+        row = pl.BlockSpec((TILE, width), lambda j, info: (info[1], 0))
+        out_specs = [pl.BlockSpec((3, part, TILE), lambda j, info: (0, 0, 0))]
+        outs = [jax.ShapeDtypeStruct((3, part, TILE), BF16)]
+    else:
+        col = pl.BlockSpec((width, TILE), lambda j, info: (0, j))
+        row = pl.BlockSpec((TILE, width), lambda j, info: (j, 0))
+        out_specs = [col, col, row]
+        outs = [jax.ShapeDtypeStruct((width, ff), BF16)] * 2 + [jax.ShapeDtypeStruct((ff, width), BF16)]
+    return pl.pallas_call(
+        functools.partial(grads_kernel, n_quarter),
+        grid_spec=pltpu.PrefetchScalarGridSpec(
+            num_scalar_prefetch=1,
+            grid=(n_block,),
+            in_specs=[hbm, hbm, col, col, row],
+            out_specs=out_specs,
+            scratch_shapes=[
+                pltpu.VMEM((rows, width), BF16), pltpu.VMEM((part, rows), BF16), pltpu.VMEM((rows, width), BF16),
+                pltpu.VMEM((TILE, rows), BF16), pltpu.VMEM((rows, TILE), BF16), pltpu.VMEM((rows, TILE), BF16),
+                pltpu.VMEM((part, TILE), F32), pltpu.VMEM((part, TILE), F32), pltpu.VMEM((TILE, part), F32),
+                pltpu.VMEM((TILE, width), BF16), pltpu.VMEM((TILE, width), BF16), pltpu.SemaphoreType.DMA((2, rows // TILE))],
+        ),
+        out_shape=outs,
+        compiler_params=pltpu.CompilerParams(dimension_semantics=("arbitrary",), vmem_limit_bytes=63 * 2**20),
+        cost_estimate=pl.CostEstimate(flops=12 * rows * width * TILE * n_block, bytes_accessed=12 * width * TILE * n_block, transcendentals=0),
+        name="expert_grads" if n_quarter == 1 else "expert_slices",
+    )(info, xn, dp, wg, wu, wd)
+
+
+def place_kernel(slices_ref, gg_in, gu_in, gd_in, gg_ref, gu_ref, gd_ref):
+    gg_ref[...] = slices_ref[0]
+    gu_ref[...] = slices_ref[1]
+    part = gg_ref.shape[0]
+    for k in range(0, part, TILE):
+        gd_ref[:, k:k + TILE] = slices_ref[2, k:k + TILE, :]
+
+
+def place_slices(slices, grads, first, n_quarter):
+    width, ff = grads[0].shape
+    part = width // n_quarter
+    hbm = pl.BlockSpec(memory_space=pl.ANY)
+    col = pl.BlockSpec((part, TILE), lambda i: (i % n_quarter, first + i // n_quarter))
+    row = pl.BlockSpec((TILE, part), lambda i: (first + i // n_quarter, i % n_quarter))
+    return pl.pallas_call(
+        place_kernel,
+        grid=(slices.shape[0] // 3,),
+        in_specs=[pl.BlockSpec((3, part, TILE), lambda i: (i, 0, 0)), hbm, hbm, hbm],
+        out_specs=[col, col, row],
+        out_shape=[jax.ShapeDtypeStruct(g.shape, g.dtype) for g in grads],
+        input_output_aliases={1: 0, 2: 1, 3: 2},
+        compiler_params=pltpu.CompilerParams(dimension_semantics=("arbitrary",)),
+        cost_estimate=pl.CostEstimate(flops=0, bytes_accessed=4 * slices.size, transcendentals=0),
+        name="place_slices",
+    )(slices, *grads)
 
 
 def solution(mesh):
@@ -248,7 +410,6 @@
         n_exp = w_router.shape[1]
         capacity = 4 * n_tok // n_exp
         total_tok = n_tok * n_dev
-        cap = min(2432, total_tok) if n_dp == 32 else CAP_SMALL
         dest_rows, slot_owner, loads = route_tables(expert_ids, n_exp, capacity)
         choice_hot = (expert_ids[:, :, None] == jnp.arange(n_exp, dtype=jnp.int32)).astype(F32)
 
@@ -276,7 +437,7 @@
             jnp.take(d_picked, slot_owner, axis=0, mode="fill", fill_value=0)], axis=1)
         recv = lax.all_to_all(send.reshape(n_exp, capacity, 2 * width), "ep", 0, 0, tiled=True).reshape(n_exp * capacity, 2 * width)
         wg, wu, wd = w_gate[0], w_up[0], w_down[0]
-        done = local_ffn(recv, wg, wu, wd, 256)
+        done = local_ffn(recv, wg, wu, wd, 2 * TILE)
         back = lax.all_to_all(done.reshape(n_exp, capacity, 2 * width), "ep", 0, 0, tiled=True).reshape(n_exp * capacity, 2 * width)
         both = jnp.take(back, dest_rows, axis=0).reshape(n_tok, 2, 2 * width)
         picked, d_xn_exp = both[..., :width], both[..., width:]
@@ -307,22 +468,20 @@
         gate_me = jnp.sum(jnp.where(mine, gates_all, 0.0), axis=1).reshape(-1, 1, GROUP)
         rank = jnp.cumsum(member.astype(jnp.int32), axis=1)
         counts = rank[:, -1]
-        offsets = jnp.cumsum(counts) - counts
-        n_rows = offsets[-1] + counts[-1]
-        pos = jnp.where(member, offsets[:, None] + rank - 1, -(2**24)).reshape(-1, 1, GROUP)
-
-        def one_pass(first):
-            xn, dp = pack_rows(rows_all, offsets, jnp.full((1,), first, jnp.int32), pos, gate_me, cap, GROUP // n_tok * capacity)
-            act, d_gate, d_up = expert_math(dot(xn, wg, ((1,), (0,))), dot(xn, wu, ((1,), (0,))), dot(dp, wd, ((1,), (1,))))
-            return dot(xn, d_gate, ((0,), (0,))), dot(xn, d_up, ((0,), (0,))), dot(act, dp, ((0,), (0,)))
-
-        def few():
-            return tuple(g.astype(BF16)[None] for g in one_pass(0))
-
-        def many():
-            return tuple((a + b).astype(BF16)[None] for a, b in zip(one_pass(0), one_pass(cap)))
-
-        g_gate, g_up, g_down = lax.cond(n_rows <= cap, few, many)
+        ends = jnp.cumsum(counts)
+        offsets = jnp.concatenate([jnp.zeros((1,), jnp.int32), ends])
+        pos = jnp.where(member, offsets[:-1, None] + rank - 1, -(2**24))[:, None]
+        pos, gate_me, offsets, grad_router = lax.optimization_barrier((pos, gate_me, offsets, grad_router))
+        xn, dp = pack_rows(rows_all, offsets, pos, gate_me, capacity * n_dev)
+        n_block = w_gate.shape[2] // TILE
+        own = n_block - n_dp // QUARTERS
+        place = lax.axis_index("dp")
+        info = jnp.stack([(offsets[-1] + TILE - 1) // TILE, own + place // QUARTERS, place % QUARTERS]).astype(jnp.int32)
+        slices = expert_grads(info, xn, dp, wg, wu, wd, 1, QUARTERS)[0]
+        whole_info = info * jnp.array([1, 0, 0], jnp.int32)
+        slices_all = lax.all_gather(slices, "dp", axis=0, tiled=True)
+        grads = expert_grads(whole_info, xn, dp, wg, wu, wd, own, 1)
+        g_gate, g_up, g_down = (g[None] for g in place_slices(slices_all, grads, own, QUARTERS))
         return out_hidden, aux_loss, grad_hidden, grad_gain, grad_router, g_gate, g_up, g_down
 
     tok_spec = P(all_axes, None)

time: 725 us -> 584 us (0.81)
  matrix products: 411 us -> 1.52 us
  Pallas kernels: 156 us -> 429 us
  loops' own time: 8.92 us -> 0 us
    dot_general x6 -> x0, matrix products: 410 us -> none  [dot(): return lax.dot_general(a, b, (dims, ((), ())), preferred_element_type=F32)]
    pallas_call x1 -> x4, Pallas kernels: 46 us -> 334 us  [the longest x2 259 us: expert_grads(): pl.pallas_call(functools.partial(grads_kernel, n_quarter), grid_spec=pltp...]
    pallas_call x1, Pallas kernels: 51.7 us -> 36.8 us  [local_ffn(): pl.pallas_call(ffn_kernel, grid=(ff // block,), out_shape=jax.ShapeDtypeS...]
    all_gather x1, waiting for transfers between devices: 62.9 us -> 74.6 us  [local_step(): lax.all_gather(jnp.concatenate([x_norm, grad_out], axis=1), all_axes, axi...]
    another operation x1 -> x0, loops' own time: 8.92 us -> none  [local_step(): g_gate, g_up, g_down = lax.cond(n_rows <= cap, few, many)]
    all_to_all x1, waiting for transfers between devices: 22.9 us -> 15.5 us  [local_step(): lax.all_to_all(done.reshape(n_exp, capacity, 2 * width), 'ep', 0, 0, tile...]
  transfers between devices with their start and end apart: 3 -> 4, of which waited for: 2 -> 2; matrix products, arithmetic and copies ran while one was open for 3% -> 5% of each run, Pallas kernels for 15% -> 58%
where the time goes in v3:
time: 584 us; the launch traced here: 579 us
  Pallas kernels  429 us (73%)
  waiting for transfers between devices  90.2 us (15%)
  between operations  17.2 us (3%)
  other arithmetic  16.8 us (3%)
  local copies, waits for them, and re-layouts  13.5 us (2%)
  starting transfers between devices  11.3 us (2%)
    pallas_call x2, Pallas kernels, expert_grads(): pl.pallas_call(functools.partial(grads_kernel, n_quarter), grid_spec=pltp...  259 us
    all_gather x1, waiting for transfers between devices, local_step(): lax.all_gather(jnp.concatenate([x_norm, grad_out], axis=1), all_axes, axi...  74.6 us
    pallas_call x1, Pallas kernels, pack_rows(): pl.pallas_call(pack_kernel, grid_spec=pltpu.PrefetchScalarGridSpec(num_sc...  45 us
    pallas_call x1, Pallas kernels, local_ffn(): pl.pallas_call(ffn_kernel, grid=(ff // block,), out_shape=jax.ShapeDtypeS...  36.8 us
    pallas_call x1, Pallas kernels, gather_rows(): pl.pallas_call(functools.partial(gather_kernel, n_y, n_z, n_ep), out_shap...  32 us
    pallas_call x1, Pallas kernels, place_slices(): pl.pallas_call(place_kernel, grid=(slices.shape[0] // 3,), in_specs=[pl.B...  29.7 us
    pallas_call x1, Pallas kernels, reduce_rows(): pl.pallas_call(functools.partial(reduce_kernel, n_y, n_z, n_ep), out_shap...  26.3 us
    all_to_all x1, waiting for transfers between devices, local_step(): lax.all_to_all(done.reshape(n_exp, capacity, 2 * width), 'ep', 0, 0, tile...  15.5 us
  transfers between devices with their start and end apart: 4, of which 2 were waited for; matrix products, arithmetic and copies ran while one was open for 5% of the time, Pallas kernels for 58%

profile of v3, /device:TPU:1, one launch (start us, length us, event | category | flops | bytes accessed | tf_op | source)
XLA Modules:
  0.0 579.1 jit_solution(1539416124078987791)
XLA Ops:
  7.2 1.0 fusion.16
  8.3 0.5 add_rsqrt_fusion
  8.8 1.0 fusion.9
  9.8 1.6 pad_maximum_fusion.1
  11.5 0.8 copy.79
  12.2 0.8 convert_bitcast_fusion
  13.5 0.2 select_reduce_fusion.1
  13.7 0.8 scatter_custom_fusion
  14.7 0.2 fusion.28
  14.9 0.7 select_reduce_fusion.3
  15.8 0.9 gather_fusion
  16.7 1.1 mul.148.clone
  17.9 0.4 mul.149
  18.4 0.9 gather_fusion.1
  19.5 1.1 pad_maximum_fusion
  20.5 6.6 %all-to-all-start = ((bf16[8,16,4096]{2,1,0:T(8,128)(2,1)}), bf16[8,16,4096]{2,1,0:T(8,128)(2,1)S(1)}, u32[]{:S(2)}, u32[]{:S(2)}) async-start(bf16[8,16,4096]{2,1,0:T(8,128)(2,1)} %pad_maximum_fusion), calls=%async_computation | async-start | bytes 2097152 | tf_op jit(solution)/shard_map/all_to_all | solution.py:438
  27.3 0.6 maximum_bitcast_fusion.row_ref
  27.9 32.0 %gather_rows.1 = f32[256,1,128]{2,1,0:T(1,128)} custom-call(f32[1,1,128]{2,1,0:T(1,128)} %maximum_bitcast_fusion.row_ref), custom_call_target="tpu_custom_call" | custom-call | tf_op jit(solution)/shard_map/gather_rows/pallas_call | solution.py:80
  59.9 1.1 fusion.27
  61.5 0.6 reduce-window.19
  62.1 0.2 slice_reduce_fusion
  62.8 36.8 %local_ffn.1 = bf16[128,4096]{1,0:T(8,128)(2,1)} custom-call(bf16[128,4096]{1,0:T(8,128)(2,1)S(1)} %bitcast.59, bf16[2048,5632]{1,0:T(8,128)(2,1)} %bitcast.60, bf16[2048,5632]{1,0:T(8,128)(2,1)} %bitcast.63, bf16[5632,2048]{1,0:T(8,128)(2,1)} %bitcast.66), custom_call_target="tpu_custom_call" | custom-call | flops 17716740096 | bytes 69206016 | tf_op jit(solution)/shard_map/local_ffn/pallas_call | solution.py:176
  99.5 4.6 all-to-all-start.1
  104.9 0.2 convert_reduce_fusion
  105.2 0.5 copy-done.7
  105.7 0.7 add_select_fusion.pos_ref
  106.4 15.5 %all-to-all-done.1 = bf16[8,16,4096]{2,1,0:T(8,128)(2,1)S(1)} async-done(((bf16[8,16,4096]{2,1,0:T(8,128)(2,1)}), bf16[8,16,4096]{2,1,0:T(8,128)(2,1)S(1)}, u32[]{:S(2)}, u32[]{:S(2)}) %all-to-all-start.1) | async-done | bytes 1048608 | tf_op jit(solution)/shard_map/all_to_all | solution.py:441
  122.0 0.9 gather_fusion.2
  122.8 0.3 gather.23
  123.2 0.6 copy_select_fusion
  123.8 0.2 fusion.4
  124.1 0.2 convolution_bitcast_fusion
  124.4 1.2 fusion.11
  125.5 0.7 select_maximum_fusion
  126.2 26.3 %reduce_rows.1 = f32[8,24,128]{2,1,0:T(8,128)} custom-call(f32[8,24,128]{2,1,0:T(8,128)} %bitcast.79), custom_call_target="tpu_custom_call" | custom-call | tf_op jit(solution)/shard_map/reduce_rows/pallas_call | solution.py:120
  152.5 0.9 slice.56
  153.4 0.6 slice_bitcast_fusion.2
  154.1 1.2 slice.58
  155.9 0.6 copy.94.gate_ref
  156.6 1.3 fusion.26
  157.8 74.6 %all-gather.3.cloned.1.call-done.rows_ref = bf16[8192,4096]{1,0:T(8,128)(2,1)} async-done(((bf16[32,4096]{1,0:T(8,128)(2,1)}), bf16[8192,4096]{1,0:T(8,128)(2,1)}) %all-gather.3.cloned.1.call-update) | async-done | bytes 67108880 | tf_op jit(solution)/shard_map/all_gather | solution.py:420
  232.5 45.0 %pack_rows.1 = (bf16[4096,2048]{1,0:T(8,128)(2,1)}, bf16[4096,2048]{1,0:T(8,128)(2,1)}) custom-call(s32[33]{0:T(128)} %copy-done.6, bf16[8192,4096]{1,0:T(8,128)(2,1)} %all-gather.3.cloned.1.call-done.rows_ref, s32[32,1,256]{2,1,0:T(1,128)} %add_select_fusion.pos_ref, f32[32,1,256]{2,1,0:T(1,128)} %copy.94.gate_ref), custom_call_target="tpu_custom_call" | custom-call | flops 17179869184 | bytes 67108864 | tf_op jit(solution)/shard_map/pack_rows/pallas_call | solution.py:250
  277.5 20.3 %expert_slices.1 = bf16[3,512,256]{2,1,0:T(8,128)(2,1)} custom-call(s32[3]{0:T(128)} %get-tuple-element.39.info_ref, bf16[4096,2048]{1,0:T(8,128)(2,1)} %get-tuple-element.24.xn_hbm, bf16[4096,2048]{1,0:T(8,128)(2,1)} %get-tuple-element.25.dp_hbm, bf16[2048,5632]{1,0:T(8,128)(2,1)} %bitcast.61, bf16[2048,5632]{1,0:T(8,128)(2,1)} %bitcast.64, ...), custom_call_target="tpu_custom_call" | custom-call | flops 14495514624 | bytes 6291456 | tf_op jit(solution)/shard_map/expert_slices/pallas_call | solution.py:353
  297.9 1.3 slice.70
  299.2 1.3 fusion.23
  301.1 1.4 fusion.15
  302.6 238.7 %expert_grads.1 = (bf16[2048,5632]{1,0:T(8,128)(2,1)}, bf16[2048,5632]{1,0:T(8,128)(2,1)}, bf16[5632,2048]{1,0:T(8,128)(2,1)}) custom-call(s32[3]{0:T(128)} %get-tuple-element.38.info_ref, bf16[4096,2048]{1,0:T(8,128)(2,1)} %get-tuple-element.24.xn_hbm, bf16[4096,2048]{1,0:T(8,128)(2,1)} %get-tuple-element.25.dp_hbm, bf16[2048,5632]{1,0:T(8,128)(2,1)} %bitcast.62, ...), custom_call_target="tpu_custom_call" | custom-call | flops 202937204736 | bytes 88080384 | tf_op jit(solution)/shard_map/expert_grads/pallas_call | solution.py:353
  541.3 29.7 %place_slices.1 = (bf16[2048,5632]{1,0:T(8,128)(2,1)}, bf16[2048,5632]{1,0:T(8,128)(2,1)}, bf16[5632,2048]{1,0:T(8,128)(2,1)}) custom-call(bf16[96,512,256]{2,1,0:T(8,128)(2,1)} %all-gather.5.cloned.1.call-done.slices_ref, bf16[2048,5632]{1,0:T(8,128)(2,1)} %get-tuple-element.26.gg_in, ...), custom_call_target="tpu_custom_call", output_to_operand_aliasing={{0}: (1, {}), {1}: (2, {}), {2}: (3, {})} | custom-call | bytes 50331648 | tf_op jit(solution)/shard_map/place_slices/pallas_call | solution.py:387
  (76 shorter events, 3.2 us)
Async XLA Ops:
  7.2 7.5 %copy-start = (f32[2048,8]{0,1:T(8,128)S(1)}, f32[2048,8]{0,1:T(8,128)}, u32[]{:S(2)}) copy-start(f32[2048,8]{0,1:T(8,128)} %param.13) | copy-start | bytes 196612
  7.2 225.3 %all-gather.3.cloned.1.call-start = ((), (), s32[]{:S(2)}) async-start(), calls=%async_computation.2 | async-start | bytes 67371008 | tf_op jit(solution)/shard_map/all_gather | solution.py:420
  20.5 42.2 %all-to-all-start = ((bf16[8,16,4096]{2,1,0:T(8,128)(2,1)}), bf16[8,16,4096]{2,1,0:T(8,128)(2,1)S(1)}, u32[]{:S(2)}, u32[]{:S(2)}) async-start(bf16[8,16,4096]{2,1,0:T(8,128)(2,1)} %pad_maximum_fusion), calls=%async_computation | async-start | bytes 2097152 | tf_op jit(solution)/shard_map/all_to_all | solution.py:438
  62.7 41.7 %copy-start.2 = (bf16[32,2048]{1,0:T(8,128)(2,1)S(1)}, bf16[32,2048]{1,0:T(8,128)(2,1)}, u32[]{:S(2)}) copy-start(bf16[32,2048]{1,0:T(8,128)(2,1)} %param.10) | copy-start | bytes 393220
  62.7 43.0 %copy-start.5 = (s32[32,2]{0,1:T(2,128)S(1)}, s32[32,2]{0,1:T(2,128)}, u32[]{:S(2)}) copy-start(s32[32,2]{0,1:T(2,128)} %param.11) | copy-start | bytes 772
  62.7 61.6 %copy-start.3 = (bf16[32,2048]{1,0:T(8,128)(2,1)S(1)}, bf16[32,2048]{1,0:T(8,128)(2,1)}, u32[]{:S(2)}) copy-start(bf16[32,2048]{1,0:T(8,128)(2,1)} %param.9) | copy-start | bytes 393220
  99.5 22.4 %all-to-all-start.1 = ((bf16[8,16,4096]{2,1,0:T(8,128)(2,1)}), bf16[8,16,4096]{2,1,0:T(8,128)(2,1)S(1)}, u32[]{:S(2)}, u32[]{:S(2)}) async-start(bf16[8,16,4096]{2,1,0:T(8,128)(2,1)} %bitcast.8), calls=%async_computation.1 | async-start | bytes 2097152 | tf_op jit(solution)/shard_map/all_to_all | solution.py:441
  104.1 437.1 %all-gather.5.cloned.1.call-start = ((), (), s32[]{:S(2)}) async-start(), calls=%async_computation.3 | async-start | bytes 25952256 | tf_op jit(solution)/shard_map/all_gather | solution.py:482
  104.2 17.8 %copy-start.6 = (s32[33]{0:T(128)}, s32[33]{0:T(128)S(1)}, u32[]{:S(2)}) copy-start(s32[33]{0:T(128)S(1)} %pad_add_fusion.off_ref) | copy-start | bytes 400
  105.2 0.5 copy-start.7
  277.5 21.7 %copy-start.8 = (f32[8]{0:T(128)S(1)}, f32[8]{0:T(128)}, u32[]{:S(2)}) copy-start(f32[8]{0:T(128)} %copy-done.7) | copy-start | bytes 100
  277.5 23.6 %copy-start.4 = (f32[2048]{0:T(1024)S(1)}, f32[2048]{0:T(1024)}, u32[]{:S(2)}) copy-start(f32[2048]{0:T(1024)} %param.12) | copy-start | bytes 24580
  541.3 29.7 %copy-start.1 = (f32[2048,8]{0,1:T(8,128)S(1)}, f32[2048,8]{0,1:T(8,128)}, u32[]{:S(2)}) copy-start(f32[2048,8]{0,1:T(8,128)} %param.13) | copy-start | bytes 196612
Sparse Core Ops, SparseCore 0:
  12.2 220.2 all-gather.2
  298.0 178.3 all-gather.4

commit v4 on v3

--- a/solution.py
+++ b/solution.py
@@ -57,35 +57,286 @@
     return pltpu.make_async_remote_copy(src_ref=src, dst_ref=dst, send_sem=send_sem, recv_sem=recv_sem, device_id=target, device_id_type=pl.DeviceIdType.MESH)
 
 
-def gather_kernel(n_y, n_z, n_ep, row_ref, out_ref, send_sem, recv_sem):
-    dp, ep, y, z, along_ep, along_y, along_z = peers(n_y, n_z, n_ep)
-    enter(along_ep + along_y + along_z)
-    mine = out_ref.at[pl.ds(dp * n_ep + ep, 1)]
-    local = pltpu.make_async_copy(row_ref, mine, send_sem.at[0])
-    local.start()
-    local.wait()
-    base = 0
-    exchange(along_ep, lambda k, t: remote(row_ref, mine, send_sem.at[base + k], recv_sem.at[base + k], t))
-    base = len(along_ep)
-    rows_y = out_ref.at[pl.ds(dp * n_ep, n_ep)]
-    exchange(along_y, lambda k, t: remote(rows_y, rows_y, send_sem.at[base + k], recv_sem.at[base + k], t))
-    base += len(along_y)
-    rows_z = out_ref.at[pl.ds(z * n_y * n_ep, n_y * n_ep)]
-    exchange(along_z, lambda k, t: remote(rows_z, rows_z, send_sem.at[base + k], recv_sem.at[base + k], t))
-
-
-def gather_rows(row, n_y, n_z, n_ep):
+def dot(a, b, dims):
+    return lax.dot_general(a, b, (dims, ((), ())), preferred_element_type=F32)
+
+
+def expert_math(hg, hu, da):
+    gate = hg.astype(BF16).astype(F32)
+    up = hu.astype(BF16).astype(F32)
+    d_act = da.astype(BF16).astype(F32)
+    sig = jax.nn.sigmoid(gate)
+    silu = gate * sig
+    act = (silu * up).astype(BF16)
+    d_up = (d_act * silu).astype(BF16)
+    d_gate = (d_act * up * sig * (1.0 + gate * (1.0 - sig))).astype(BF16)
+    return act, d_gate, d_up
+
+
+LINK_RATE, HOP_US, FFN_US, FFN_FROM_US = 46e3, 3.0, 3.5, 24.0
+PIECES = (
+    (0, None, "xyz"), (3, 0, "zxy"), (3, 1, "zyx"), (1, None, "yzx"), (2, None, "xzy"))
+
+
+def due(left, sizes):
+    ready = []
+    for piece in range(len(PIECES)):
+        for phase in (1, 2):
+            if (piece, phase) not in left and left.get((piece, phase - 1)) == 0:
+                if (piece, phase) != (0, 2) or all(left.get((other, 1)) == 0 for other in (3, 4)):
+                    ready.append((piece, phase))
+    return ready
+
+
+def plan(sizes, tile_bytes, n_ffn):
+    free, arrive, order, left = {}, [], [], {}
+    ffn, now = 0, 8.0
+
+    def issue(hop, when):
+        piece, phase, sign, step = hop
+        _, half, axes = PIECES[piece]
+        size = tile_bytes // (1 if half is None else 2)
+        for axis in axes[:phase]:
+            size *= sizes[axis]
+        size //= 2 if step == sizes[axes[phase]] // 2 else 1
+        link = (axes[phase], sign)
+        free[link] = max(when, free.get(link, 0.0)) + size / LINK_RATE
+        arrive.append((free[link] + HOP_US, hop))
+
+    def begin(piece, phase, when):
+        left[piece, phase] = 2 * (sizes[PIECES[piece][2][phase]] // 2)
+        for sign in (1, -1):
+            issue((piece, phase, sign, 1), when)
+
+    for piece in range(len(PIECES)):
+        begin(piece, 0, now)
+    while arrive:
+        arrive.sort()
+        when, hop = arrive[0]
+        if ffn < n_ffn and now >= FFN_FROM_US and when > now + 0.4 * FFN_US:
+            order.append("ffn")
+            ffn, now = ffn + 1, now + FFN_US
+            continue
+        arrive.pop(0)
+        now = max(now, when)
+        order.append(hop)
+        piece, phase, sign, step = hop
+        if step < sizes[PIECES[piece][2][phase]] // 2:
+            issue((piece, phase, sign, step + 1), now)
+        left[piece, phase] -= 1
+        for other in due(left, sizes):
+            begin(*other, now)
+    return order + ["ffn"] * (n_ffn - ffn), now
+
+
+class Copies:
+    def __init__(self, send_sem, recv_sem):
+        self.sems, self.made = (send_sem, recv_sem), {}
+
+    def start(self, name, ends):
+        k = len(self.made)
+        self.made[name] = lambda: remote(*ends()[:2], self.sems[0].at[k], self.sems[1].at[k], ends()[2])
+        self.made[name]().start()
+
+    def wait_recv(self, name):
+        self.made[name]().wait_recv()
+
+
+def gather_kernel(n_y, n_z, n_ep, order, rows_in, send_in, meta_in, wg_ref, wu_ref, wd_ref, rows_out, back_out, meta_out, got, result, o_acc, d_acc, send_sem, recv_sem, own_sem):
+    step = pl.program_id(0)
+    n_x = n_ep // 2
+    dp, ep = lax.axis_index("dp"), lax.axis_index("ep")
+    at = {"x": lax.div(ep, 2), "y": lax.rem(dp, n_y), "z": lax.div(dp, n_y)}
+    core = lax.rem(ep, 2)
+    sizes = {"x": n_x, "y": n_y, "z": n_z}
+    width = wg_ref.shape[0]
+    wide = rows_in.shape[2]
+
+    def shifted(axis, by):
+        return lax.rem(at[axis] + by + 2 * sizes[axis], sizes[axis])
+
+    def neighbour(axis, by):
+        place = {**at, axis: shifted(axis, by)}
+        return {"dp": place["z"] * n_y + place["y"], "ep": place["x"] * 2 + core}
+
+    partner = {"dp": dp, "ep": at["x"] * 2 + (1 - core)}
+    along_ep = [{"dp": dp, "ep": lax.rem(ep + k, n_ep)} for k in range(1, n_ep)]
+    along_y = [{"dp": at["z"] * n_y + lax.rem(at["y"] + k, n_y), "ep": ep} for k in range(1, n_y)]
+    along_z = [{"dp": lax.rem(at["z"] + k, n_z) * n_y + at["y"], "ep": ep} for k in range(1, n_z)]
+    copies = Copies(send_sem, recv_sem)
+
+    def columns(piece, half):
+        low, high = 0, wide
+        for part in (PIECES[piece][1], half):
+            if part is not None:
+                middle = (low + high) // 2
+                low, high = ((low, middle), (middle, high))[part]
+        return pl.ds(low, high - low)
+
+    def region(piece, phase, index, half):
+        tile, _, axes = PIECES[piece]
+        pick = {axis: slice(None) if k < phase else index if k == phase else at[axis] for k, axis in enumerate(axes)}
+        return rows_out.at[pick["z"], pick["y"], pick["x"], core, tile, :, columns(piece, half)]
+
+    def send(piece, phase, sign, hop):
+        axis = PIECES[piece][2][phase]
+        half = None if hop < sizes[axis] // 2 else (0 if sign == 1 else 1)
+
+        def ends():
+            dst = region(piece, phase, shifted(axis, -sign * (hop - 1)), half)
+            src = rows_in.at[PIECES[piece][0], :, columns(piece, half)] if (phase, hop) == (0, 1) else dst
+            return src, dst, neighbour(axis, sign)
+
+        copies.start((piece, phase, sign, hop), ends)
+
+    def to_partner(name, block):
+        copies.start(("pair", *name), lambda: (block(), block(), partner))
+
+    left = {}
+
+    def arrived(piece, phase, sign, hop):
+        axes = PIECES[piece][2]
+        copies.wait_recv((piece, phase, sign, hop))
+        last = sizes[axes[phase]] // 2
+        if hop < last:
+            send(piece, phase, sign, hop + 1)
+        if phase == 2:
+            half = None if hop < last else (0 if sign == 1 else 1)
+            to_partner((piece, phase, sign, hop), lambda: region(piece, phase, shifted(axes[phase], -sign * hop), half))
+        left[piece, phase] = left.get((piece, phase), 2 * last) - 1
+        if not left[piece, phase] and phase == 1:
+            to_partner((piece, phase), lambda: region(piece, 2, at[axes[2]], None))
+        for other, later in due(left, sizes):
+            left[other, later] = 2 * (sizes[PIECES[other][2][later]] // 2)
+            for way in (1, -1):
+                send(other, later, way, 1)
+
+    def exchange_results(name, src, dst):
+        for k, target in enumerate(along_ep):
+            copies.start((name, k), lambda target=target: (src.at[target["ep"]], dst.at[ep], target))
+
+    def spread(name, targets, block):
+        for k, target in enumerate(targets):
+            copies.start((name, k), lambda target=target: (block(), block(), target))
+
+    def all_in(name, n):
+        for k in range(n):
+            copies.wait_recv((name, k))
+
+    def own_copies():
+        return [
+            pltpu.make_async_copy(rows_in, rows_out.at[at["z"], at["y"], at["x"], core], own_sem.at[0]),
+            pltpu.make_async_copy(send_in.at[ep], got.at[ep], own_sem.at[1]),
+            pltpu.make_async_copy(meta_in, meta_out.at[pl.ds(dp * n_ep + ep, 1)], own_sem.at[2])]
+
+    def prologue():
+        enter(along_ep + [neighbour("y", 1), neighbour("y", -1), neighbour("z", 1), neighbour("z", -1)] + along_y + along_z)
+        mine = own_copies()
+        for copy in mine:
+            copy.start()
+        for piece in range(len(PIECES)):
+            left[piece, 0] = 2 * (sizes[PIECES[piece][2][0]] // 2)
+            for sign in (1, -1):
+                send(piece, 0, sign, 1)
+        exchange_results("dispatch", send_in, got)
+        for copy in mine:
+            copy.wait()
+        spread("meta_ep", along_ep, lambda: meta_out.at[pl.ds(dp * n_ep + ep, 1)])
+
+    def ready():
+        all_in("dispatch", n_ep - 1)
+        all_in("meta_ep", n_ep - 1)
+        spread("meta_y", along_y, lambda: meta_out.at[pl.ds(dp * n_ep, n_ep)])
+
+    runs, current = [], []
+    for entry in order:
+        if entry == "ffn":
+            runs.append(current)
+            current = []
+        else:
+            current.append(entry)
+    runs.append(current)
+    n_ffn = len(runs) - 1
+
+    @pl.when(step == 0)
+    def _():
+        prologue()
+        for hop in runs[0]:
+            arrived(*hop)
+        ready()
+        o_acc[...] = jnp.zeros_like(o_acc)
+        d_acc[...] = jnp.zeros_like(d_acc)
+
+    @pl.when(step < n_ffn)
+    def _():
+        n_row = got.shape[0] * got.shape[1]
+        half = wg_ref.shape[1] // 2
+        xn = got[:, :, :width].reshape(n_row, width)
+        dy = got[:, :, width:].reshape(n_row, width)
+        cuts = [slice(0, half), slice(half, 2 * half)]
+        mid = [expert_math(dot(xn, wg_ref[:, c], ((1,), (0,))), dot(xn, wu_ref[:, c], ((1,), (0,))), dot(dy, wd_ref[c, :], ((1,), (1,)))) for c in cuts]
+        act, d_gate, d_up = (jnp.concatenate(parts, axis=1) for parts in zip(*mid))
+        o_acc[...] += dot(act, wd_ref[...], ((1,), (0,)))
+        d_acc[...] += dot(d_gate, wg_ref[...], ((1,), (1,))) + dot(d_up, wu_ref[...], ((1,), (1,)))
+
+    @pl.when(step == n_ffn - 1)
+    def _():
+        result[:, :, :width] = o_acc[...].astype(BF16).reshape(*result.shape[:2], width)
+        result[:, :, width:] = d_acc[...].astype(BF16).reshape(*result.shape[:2], width)
+
+    for k in range(1, n_ffn + 1):
+        @pl.when(step == (k - 1 if k < n_ffn else n_ffn))
+        def _():
+            if k == 2:
+                all_in("meta_y", n_y - 1)
+                spread("meta_z", along_z, lambda: meta_out.at[pl.ds(at["z"] * n_y * n_ep, n_y * n_ep)])
+            if k == n_ffn:
+                own = pltpu.make_async_copy(result.at[ep], back_out.at[ep], own_sem.at[1])
+                own.start()
+                own.wait()
+                exchange_results("back", result, back_out)
+            for hop in runs[k]:
+                arrived(*hop)
+            if k == n_ffn:
+                all_in("meta_z", n_z - 1)
+                all_in("back", n_ep - 1)
+                for name in copies.made:
+                    if name[0] == "pair":
+                        copies.wait_recv(name)
+                for copy in copies.made.values():
+                    copy().wait_send()
+
+
+def gather_rows(rows, send, meta, wg, wu, wd, n_y, n_z, n_ep, block):
+    n_tok, wide = rows.shape
     n_dev = n_y * n_z * n_ep
-    n_sem = n_ep + n_y + n_z - 3
-    return pl.pallas_call(
-        functools.partial(gather_kernel, n_y, n_z, n_ep),
-        out_shape=jax.ShapeDtypeStruct((n_dev, 1, LANES), F32),
-        in_specs=[pl.BlockSpec(memory_space=pltpu.VMEM)],
-        out_specs=pl.BlockSpec(memory_space=pltpu.VMEM),
-        scratch_shapes=[pltpu.SemaphoreType.DMA((n_sem,)), pltpu.SemaphoreType.DMA((n_sem,))],
-        compiler_params=pltpu.CompilerParams(collective_id=1, has_side_effects=True),
+    capacity = send.shape[1]
+    width, ff = wg.shape
+    n_ffn = ff // block
+    tiles = n_tok // 8
+    order, _ = plan({"x": n_ep // 2, "y": n_y, "z": n_z}, 8 * wide * 2, n_ffn)
+    n_sem = len([e for e in order if e != "ffn"])
+    n_sem += sum(1 for e in order if e != "ffn" and e[1] == 2) + len(PIECES) + 2 * (n_ep - 1) + n_ep + n_y + n_z - 3
+    vmem, hbm = pl.BlockSpec(memory_space=pltpu.VMEM), pl.BlockSpec(memory_space=pl.ANY)
+    col = pl.BlockSpec((width, block), lambda j: (0, jnp.minimum(j, n_ffn - 1)))
+    row = pl.BlockSpec((block, width), lambda j: (jnp.minimum(j, n_ffn - 1), 0))
+    slots = pltpu.VMEM((n_ep, capacity, wide), BF16)
+    out, back, meta_all = pl.pallas_call(
+        functools.partial(gather_kernel, n_y, n_z, n_ep, order),
+        grid=(n_ffn + 1,),
+        in_specs=[vmem, vmem, vmem, col, col, row],
+        out_specs=[hbm, hbm, hbm],
+        out_shape=[
+            jax.ShapeDtypeStruct((n_z, n_y, n_ep // 2, 2, tiles, 8, wide), BF16),
+            jax.ShapeDtypeStruct((n_ep, capacity, wide), BF16),
+            jax.ShapeDtypeStruct((n_dev, 1, LANES), F32)],
+        scratch_shapes=[slots, slots, pltpu.VMEM((n_ep * capacity, width), F32), pltpu.VMEM((n_ep * capacity, width), F32),
+                        pltpu.SemaphoreType.DMA((n_sem,)), pltpu.SemaphoreType.DMA((n_sem,)), pltpu.SemaphoreType.DMA((3,))],
+        compiler_params=pltpu.CompilerParams(collective_id=1, has_side_effects=True, dimension_semantics=("arbitrary",), vmem_limit_bytes=50 * 2**20),
+        cost_estimate=pl.CostEstimate(flops=12 * n_ep * capacity * width * ff, bytes_accessed=6 * width * ff, transcendentals=0),
         name="gather_rows",
-    )(row)
+    )(rows.reshape(tiles, 8, wide), send, meta, wg, wu, wd)
+    return out.reshape(n_dev * n_tok, wide), back.reshape(n_ep * capacity, wide), meta_all
 
 
 def reduce_kernel(n_y, n_z, n_ep, in_ref, out_ref, got_ep, got_y, got_z, send_sem, recv_sem):
@@ -126,64 +377,6 @@
         compiler_params=pltpu.CompilerParams(collective_id=2, has_side_effects=True),
         name="reduce_rows",
     )(parts)
-
-
-def dot(a, b, dims):
-    return lax.dot_general(a, b, (dims, ((), ())), preferred_element_type=F32)
-
-
-def expert_math(hg, hu, da):
-    gate = hg.astype(BF16).astype(F32)
-    up = hu.astype(BF16).astype(F32)
-    d_act = da.astype(BF16).astype(F32)
-    sig = jax.nn.sigmoid(gate)
-    silu = gate * sig
-    act = (silu * up).astype(BF16)
-    d_up = (d_act * silu).astype(BF16)
-    d_gate = (d_act * up * sig * (1.0 + gate * (1.0 - sig))).astype(BF16)
-    return act, d_gate, d_up
-
-
-def ffn_kernel(rows_ref, wg_ref, wu_ref, wd_ref, out_ref, o_acc, d_acc):
-    step = pl.program_id(0)
-    width = wg_ref.shape[0]
-    half = wg_ref.shape[1] // 2
-    xn, dp = rows_ref[:, :width], rows_ref[:, width:]
-
-    @pl.when(step == 0)
-    def _():
-        o_acc[...] = jnp.zeros_like(o_acc)
-        d_acc[...] = jnp.zeros_like(d_acc)
-
-    cols = [slice(0, half), slice(half, 2 * half)]
-    mid = [expert_math(dot(xn, wg_ref[:, c], ((1,), (0,))), dot(xn, wu_ref[:, c], ((1,), (0,))), dot(dp, wd_ref[c, :], ((1,), (1,)))) for c in cols]
-    act, d_gate, d_up = (jnp.concatenate(parts, axis=1) for parts in zip(*mid))
-    o_acc[...] += dot(act, wd_ref[...], ((1,), (0,)))
-    d_acc[...] += dot(d_gate, wg_ref[...], ((1,), (1,))) + dot(d_up, wu_ref[...], ((1,), (1,)))
-
-    @pl.when(step == pl.num_programs(0) - 1)
-    def _():
-        out_ref[:, :width] = o_acc[...].astype(BF16)
-        out_ref[:, width:] = d_acc[...].astype(BF16)
-
-
-def local_ffn(rows, wg, wu, wd, block):
-    n, width = rows.shape[0], wg.shape[0]
-    ff = wg.shape[1]
-    whole = pl.BlockSpec((n, 2 * width), lambda j: (0, 0))
-    col = pl.BlockSpec((width, block), lambda j: (0, j))
-    row = pl.BlockSpec((block, width), lambda j: (j, 0))
-    return pl.pallas_call(
-        ffn_kernel,
-        grid=(ff // block,),
-        out_shape=jax.ShapeDtypeStruct((n, 2 * width), BF16),
-        in_specs=[whole, col, col, row],
-        out_specs=whole,
-        scratch_shapes=[pltpu.VMEM((n, width), F32), pltpu.VMEM((n, width), F32)],
-        compiler_params=pltpu.CompilerParams(dimension_semantics=("arbitrary",), vmem_limit_bytes=40 * 2**20),
-        cost_estimate=pl.CostEstimate(flops=12 * n * width * ff, bytes_accessed=6 * width * ff, transcendentals=0),
-        name="local_ffn",
-    )(rows, wg, wu, wd)
 
 
 def pack_kernel(off_ref, rows_ref, pos_ref, gate_ref, xn_out, dp_out, xn_buf, dp_buf, sem):
@@ -371,23 +564,25 @@
 
 
 def place_kernel(slices_ref, gg_in, gu_in, gd_in, gg_ref, gu_ref, gd_ref):
-    gg_ref[...] = slices_ref[0]
-    gu_ref[...] = slices_ref[1]
-    part = gg_ref.shape[0]
-    for k in range(0, part, TILE):
-        gd_ref[:, k:k + TILE] = slices_ref[2, k:k + TILE, :]
+    part = slices_ref.shape[1]
+    for q in range(slices_ref.shape[0] // 3):
+        rows = slice(q * part, (q + 1) * part)
+        gg_ref[rows, :] = slices_ref[3 * q]
+        gu_ref[rows, :] = slices_ref[3 * q + 1]
+        for k in range(0, part, TILE):
+            gd_ref[:, q * part + k:q * part + k + TILE] = slices_ref[3 * q + 2, k:k + TILE, :]
 
 
 def place_slices(slices, grads, first, n_quarter):
     width, ff = grads[0].shape
     part = width // n_quarter
     hbm = pl.BlockSpec(memory_space=pl.ANY)
-    col = pl.BlockSpec((part, TILE), lambda i: (i % n_quarter, first + i // n_quarter))
-    row = pl.BlockSpec((TILE, part), lambda i: (first + i // n_quarter, i % n_quarter))
+    col = pl.BlockSpec((width, TILE), lambda i: (0, first + i))
+    row = pl.BlockSpec((TILE, width), lambda i: (first + i, 0))
     return pl.pallas_call(
         place_kernel,
-        grid=(slices.shape[0] // 3,),
-        in_specs=[pl.BlockSpec((3, part, TILE), lambda i: (i, 0, 0)), hbm, hbm, hbm],
+        grid=(slices.shape[0] // (3 * n_quarter),),
+        in_specs=[pl.BlockSpec((3 * n_quarter, part, TILE), lambda i: (i, 0, 0)), hbm, hbm, hbm],
         out_specs=[col, col, row],
         out_shape=[jax.ShapeDtypeStruct(g.shape, g.dtype) for g in grads],
         input_output_aliases={1: 0, 2: 1, 3: 2},
@@ -417,28 +612,25 @@
         inv_rms = lax.rsqrt(jnp.mean(x_f32 * x_f32, axis=-1, keepdims=True) + EPS)
         x_hat = x_f32 * inv_rms
         x_norm = (x_hat * norm_gain).astype(BF16)
-        rows_all = lax.all_gather(jnp.concatenate([x_norm, grad_out], axis=1), all_axes, axis=0, tiled=True)
         xn_f32 = x_norm.astype(F32)
         router_probs = jax.nn.softmax(jnp.dot(xn_f32, w_router, preferred_element_type=F32), axis=-1)
         gate_vals = jnp.sum(router_probs[:, None, :] * choice_hot, axis=-1)
 
         meta = jnp.concatenate([gate_vals.T.reshape(1, -1), expert_ids.T.astype(F32).reshape(1, -1)], axis=1)
         meta = jnp.pad(meta, ((0, 0), (0, LANES - meta.shape[1])))
-        meta_all = gather_rows(meta[None], n_y, n_z, n_ep).reshape(n_dev, LANES)
-        ids_all = meta_all[:, 2 * n_tok:4 * n_tok].astype(jnp.int32).reshape(n_dev, 2, n_tok)
-        gates_all = meta_all[:, :2 * n_tok].reshape(n_dev, 2, n_tok)
-        all_loads = jnp.sum((ids_all[..., None] == jnp.arange(n_exp, dtype=jnp.int32)).astype(F32), axis=(0, 1, 2))
-        load_frac = all_loads / (2 * total_tok)
-
         dy_f32 = grad_out.astype(F32)
         d_picked = (dy_f32[:, None, :] * gate_vals[:, :, None]).astype(BF16).reshape(n_tok * 2, width)
         send = jnp.concatenate([
             jnp.take(x_norm, slot_owner // 2, axis=0, mode="fill", fill_value=0),
             jnp.take(d_picked, slot_owner, axis=0, mode="fill", fill_value=0)], axis=1)
-        recv = lax.all_to_all(send.reshape(n_exp, capacity, 2 * width), "ep", 0, 0, tiled=True).reshape(n_exp * capacity, 2 * width)
         wg, wu, wd = w_gate[0], w_up[0], w_down[0]
-        done = local_ffn(recv, wg, wu, wd, 2 * TILE)
-        back = lax.all_to_all(done.reshape(n_exp, capacity, 2 * width), "ep", 0, 0, tiled=True).reshape(n_exp * capacity, 2 * width)
+        rows_all, back, meta_all = gather_rows(jnp.concatenate([x_norm, grad_out], axis=1), send.reshape(n_exp, capacity, 2 * width), meta[None], wg, wu, wd, n_y, n_z, n_ep, 2 * TILE)
+        meta_all = meta_all.reshape(n_dev, LANES)
+        ids_all = meta_all[:, 2 * n_tok:4 * n_tok].astype(jnp.int32).reshape(n_dev, 2, n_tok)
+        gates_all = meta_all[:, :2 * n_tok].reshape(n_dev, 2, n_tok)
+        all_loads = jnp.sum((ids_all[..., None] == jnp.arange(n_exp, dtype=jnp.int32)).astype(F32), axis=(0, 1, 2))
+        load_frac = all_loads / (2 * total_tok)
+
         both = jnp.take(back, dest_rows, axis=0).reshape(n_tok, 2, 2 * width)
         picked, d_xn_exp = both[..., :width], both[..., width:]
         out_hidden = (x_f32 + jnp.sum(gate_vals[:, :, None] * picked, axis=1)).astype(BF16)

time: 584 us -> 579 us (level)
  Pallas kernels: 429 us -> 531 us
  waiting for transfers between devices: 90.2 us -> 0.04 us
  starting transfers between devices: 11.3 us -> 0.04 us
    pallas_call x3 -> x2, Pallas kernels: 98.5 us -> 203 us  [the longest x1 185 us: gather_rows(): pl.pallas_call(functools.partial(gather_kernel, n_y, n_z, n_ep, order), g...]
    all_gather x1 -> x0, waiting for transfers between devices: 74.6 us -> none  [local_step(): lax.all_gather(jnp.concatenate([x_norm, grad_out], axis=1), all_axes, axi...]
    all_to_all x2 -> x0, waiting for transfers between devices: 15.5 us -> none  [the longest x1 15.5 us: local_step(): lax.all_to_all(done.reshape(n_exp, capacity, 2 * width), 'ep', 0, 0, tile...]
    all_to_all x2 -> x0, starting transfers between devices: 11.2 us -> none  [the longest x1 6.64 us: local_step(): lax.all_to_all(send.reshape(n_exp, capacity, 2 * width), 'ep', 0, 0, tile...]
  transfers between devices with their start and end apart: 4 -> 1, of which waited for: 2 -> 0; matrix products, arithmetic and copies ran while one was open for 5% -> 1% of each run, Pallas kernels for 58% -> 42%
where the time goes in v4:
time: 579 us; the launch traced here: 575 us
  Pallas kernels  531 us (92%)
  between operations  17.1 us (3%)
  other arithmetic  13.3 us (2%)
  local copies, waits for them, and re-layouts  12.3 us (2%)
    pallas_call x2, Pallas kernels, expert_grads(): pl.pallas_call(functools.partial(grads_kernel, n_quarter), grid_spec=pltp...  259 us
    pallas_call x1, Pallas kernels, gather_rows(): pl.pallas_call(functools.partial(gather_kernel, n_y, n_z, n_ep, order), g...  185 us
    pallas_call x1, Pallas kernels, pack_rows(): pl.pallas_call(pack_kernel, grid_spec=pltpu.PrefetchScalarGridSpec(num_sc...  45.1 us
    pallas_call x1, Pallas kernels, reduce_rows(): pl.pallas_call(functools.partial(reduce_kernel, n_y, n_z, n_ep), out_shap...  23.6 us
    pallas_call x1, Pallas kernels, place_slices(): pl.pallas_call(place_kernel, grid=(slices.shape[0] // (3 * n_quarter),),...  18.4 us
  transfers between devices with their start and end apart: 1, of which 0 were waited for; matrix products, arithmetic and copies ran while one was open for 1% of the time, Pallas kernels for 42%

profile of v4, /device:TPU:1, one launch (start us, length us, event | category | flops | bytes accessed | tf_op | source)
XLA Modules:
  0.0 574.9 jit_solution(13215416201348201283)
XLA Ops:
  7.2 0.8 convert_bitcast_fusion
  8.0 0.8 copy.79
  8.8 0.1 mul.147
  9.0 0.1 reshape.245
  9.2 0.2 select_reduce_fusion.1
  9.4 0.8 scatter_custom_fusion
  10.4 1.0 fusion.16
  11.8 0.7 compare_and_fusion.2
  12.5 0.9 convert_element_type.70
  13.4 1.0 fusion.9
  14.4 0.9 maximum_bitcast_fusion.rows_in
  15.4 0.2 fusion.28
  15.6 0.7 select_reduce_fusion.3
  16.5 0.9 gather_fusion
  17.5 1.1 mul.148.clone
  18.6 0.4 mul.149
  19.2 0.9 gather_fusion.1
  20.1 0.1 broadcast_select_fusion
  20.4 184.9 %gather_rows.1 = (bf16[8,4,4,2,4,8,4096]{6,5,4,3,2,1,0:T(8,128)(2,1)}, bf16[8,16,4096]{2,1,0:T(8,128)(2,1)S(1)}, f32[256,1,128]{2,1,0:T(1,128)S(1)}) custom-call(bf16[4,8,4096]{2,1,0:T(8,128)(2,1)S(1)} %maximum_bitcast_fusion.rows_in, bf16[8,16,4096]{2,1,0:T(8,128)(2,1)S(1)} %pad_maximum_fusion.send_in, f32[1,1,128]{2,1,0:T(1,128)S(1)} %maximum_bitcast_fusion.1.meta_in, ...), custom_call_target="tpu_custom_call" | custom-call | flops 17716740096 | bytes 69206016 | tf_op jit(solution)/shard_map/gather_rows/pallas_call | solution.py:324
  205.3 0.9 gather_fusion.2
  206.2 0.3 gather.23
  206.6 0.6 copy_select_fusion
  207.2 0.2 fusion.4
  207.6 0.2 convert_reduce_fusion
  207.8 0.1 multiply_reduce_fusion
  208.0 0.5 fusion.11
  208.5 0.2 convolution_bitcast_fusion
  208.7 0.1 copy.86
  208.9 0.1 reshape.262
  209.1 0.6 reduce-window.19
  209.7 0.2 slice_reduce_fusion
  210.2 0.6 select_maximum_fusion
  210.8 23.6 %reduce_rows.1 = f32[8,24,128]{2,1,0:T(8,128)} custom-call(f32[8,24,128]{2,1,0:T(8,128)} %bitcast.79), custom_call_target="tpu_custom_call" | custom-call | tf_op jit(solution)/shard_map/reduce_rows/pallas_call | solution.py:371
  234.5 0.1 reshape.297
  234.8 0.1 reduce.1
  235.1 0.9 slice.56
  236.0 0.6 slice_bitcast_fusion.2
  236.7 0.7 add_select_fusion.pos_ref
  237.4 0.6 slice.58
  238.7 0.6 copy.94.gate_ref
  239.4 45.1 %pack_rows.1 = (bf16[4096,2048]{1,0:T(8,128)(2,1)}, bf16[4096,2048]{1,0:T(8,128)(2,1)}) custom-call(s32[33]{0:T(128)} %copy-done.6, bf16[8192,4096]{1,0:T(8,128)(2,1)} %bitcast.25.rows_ref, s32[32,1,256]{2,1,0:T(1,128)} %add_select_fusion.pos_ref, f32[32,1,256]{2,1,0:T(1,128)} %copy.94.gate_ref), custom_call_target="tpu_custom_call" | custom-call | flops 17179869184 | bytes 67108864 | tf_op jit(solution)/shard_map/pack_rows/pallas_call | solution.py:443
  284.5 0.6 fusion.26
  285.1 20.3 %expert_slices.1 = bf16[3,512,256]{2,1,0:T(8,128)(2,1)} custom-call(s32[3]{0:T(128)} %get-tuple-element.45.info_ref, bf16[4096,2048]{1,0:T(8,128)(2,1)} %get-tuple-element.30.xn_hbm, bf16[4096,2048]{1,0:T(8,128)(2,1)} %get-tuple-element.31.dp_hbm, bf16[2048,5632]{1,0:T(8,128)(2,1)} %bitcast.63, bf16[2048,5632]{1,0:T(8,128)(2,1)} %bitcast.66, ...), custom_call_target="tpu_custom_call" | custom-call | flops 14495514624 | bytes 6291456 | tf_op jit(solution)/shard_map/expert_slices/pallas_call | solution.py:546
  305.5 1.3 slice.70
  306.8 1.3 fusion.23
  308.7 0.8 fusion.15
  309.5 238.8 %expert_grads.1 = (bf16[2048,5632]{1,0:T(8,128)(2,1)}, bf16[2048,5632]{1,0:T(8,128)(2,1)}, bf16[5632,2048]{1,0:T(8,128)(2,1)}) custom-call(s32[3]{0:T(128)} %get-tuple-element.44.info_ref, bf16[4096,2048]{1,0:T(8,128)(2,1)} %get-tuple-element.30.xn_hbm, bf16[4096,2048]{1,0:T(8,128)(2,1)} %get-tuple-element.31.dp_hbm, bf16[2048,5632]{1,0:T(8,128)(2,1)} %bitcast.64, ...), custom_call_target="tpu_custom_call" | custom-call | flops 202937204736 | bytes 88080384 | tf_op jit(solution)/shard_map/expert_grads/pallas_call | solution.py:546
  548.3 18.4 %place_slices.1 = (bf16[2048,5632]{1,0:T(8,128)(2,1)}, bf16[2048,5632]{1,0:T(8,128)(2,1)}, bf16[5632,2048]{1,0:T(8,128)(2,1)}) custom-call(bf16[96,512,256]{2,1,0:T(8,128)(2,1)} %all-gather.2.cloned.1.call-done.slices_ref, bf16[2048,5632]{1,0:T(8,128)(2,1)} %get-tuple-element.32.gg_in, ...), custom_call_target="tpu_custom_call", output_to_operand_aliasing={{0}: (1, {}), {1}: (2, {}), {2}: (3, {})} | custom-call | bytes 50331648 | tf_op jit(solution)/shard_map/place_slices/pallas_call | solution.py:582
  (66 shorter events, 2.5 us)
Async XLA Ops:
  7.2 8.2 %copy-start = (f32[2048,8]{0,1:T(8,128)S(1)}, f32[2048,8]{0,1:T(8,128)}, u32[]{:S(2)}) copy-start(f32[2048,8]{0,1:T(8,128)} %param.13) | copy-start | bytes 196612
  7.2 541.1 %all-gather.2.cloned.1.call-start = ((), (), s32[]{:S(2)}) async-start(), calls=%async_computation | async-start | bytes 25952256 | tf_op jit(solution)/shard_map/all_gather | solution.py:674
  20.4 187.0 %copy-start.5 = (s32[32,2]{0,1:T(2,128)S(1)}, s32[32,2]{0,1:T(2,128)}, u32[]{:S(2)}) copy-start(s32[32,2]{0,1:T(2,128)} %param.11) | copy-start | bytes 772
  20.4 187.6 %copy-start.3 = (bf16[32,2048]{1,0:T(8,128)(2,1)S(1)}, bf16[32,2048]{1,0:T(8,128)(2,1)}, u32[]{:S(2)}) copy-start(bf16[32,2048]{1,0:T(8,128)(2,1)} %param.9) | copy-start | bytes 393220
  20.4 187.6 %copy-start.4 = (f32[2048]{0:T(1024)S(1)}, f32[2048]{0:T(1024)}, u32[]{:S(2)}) copy-start(f32[2048]{0:T(1024)} %param.12) | copy-start | bytes 24580
  236.7 2.7 copy-start.6
  239.4 45.1 %copy-start.7 = (s32[3]{0:T(128)S(1)}, s32[3]{0:T(128)}, u32[]{:S(2)}) copy-start(s32[3]{0:T(128)} %constant.161.clone) | copy-start | bytes 40
  285.1 23.6 %copy-start.2 = (bf16[32,2048]{1,0:T(8,128)(2,1)S(1)}, bf16[32,2048]{1,0:T(8,128)(2,1)}, u32[]{:S(2)}) copy-start(bf16[32,2048]{1,0:T(8,128)(2,1)} %param.10) | copy-start | bytes 393220
  548.3 18.4 %copy-start.1 = (f32[2048,8]{0,1:T(8,128)S(1)}, f32[2048,8]{0,1:T(8,128)}, u32[]{:S(2)}) copy-start(f32[2048,8]{0,1:T(8,128)} %param.13) | copy-start | bytes 196612
Sparse Core Ops, SparseCore 0:
  305.6 177.4 all-gather.1

commit v5 on v4

v5 whole, which is shorter than its diff:
```python
import functools
import jax
import jax.numpy as jnp
from jax import lax
from jax.experimental import pallas as pl
from jax.experimental.pallas import tpu as pltpu
from jax.sharding import PartitionSpec as P

EPS = 1e-6
AUX_COEF = 0.001
LANES = 128
GROUP = 256
MOST_PER_GROUP = 128
ALIGN = 16
TILE = 256
USUAL_ROWS = 2304
QUARTERS = 4
F32 = jnp.float32
BF16 = jnp.bfloat16


def route_tables(expert_ids, n_exp, capacity):
    flat_ids = expert_ids.reshape(-1)
    n_choice = flat_ids.shape[0]
    one_hot = (flat_ids[:, None] == jnp.arange(n_exp, dtype=jnp.int32)[None, :]).astype(jnp.int32)
    running = jnp.cumsum(one_hot, axis=0) - 1
    dest_rows = flat_ids * capacity + jnp.sum(running * one_hot, axis=1)
    slot_owner = jnp.full((n_exp * capacity,), n_choice, jnp.int32).at[dest_rows].set(jnp.arange(n_choice, dtype=jnp.int32))
    return dest_rows, slot_owner, jnp.sum(one_hot, axis=0)


def peers(n_y, n_z, n_ep):
    dp, ep = lax.axis_index("dp"), lax.axis_index("ep")
    y, z = lax.rem(dp, n_y), lax.div(dp, n_y)
    along_ep = [{"dp": dp, "ep": lax.rem(ep + k, n_ep)} for k in range(1, n_ep)]
    along_y = [{"dp": z * n_y + lax.rem(y + k, n_y), "ep": ep} for k in range(1, n_y)]
    along_z = [{"dp": lax.rem(z + k, n_z) * n_y + y, "ep": ep} for k in range(1, n_z)]
    return dp, ep, y, z, along_ep, along_y, along_z


def enter(all_peers):
    barrier = pltpu.get_barrier_semaphore()
    for peer in all_peers:
        pl.semaphore_signal(barrier, inc=1, device_id=peer, device_id_type=pl.DeviceIdType.MESH)
    pl.semaphore_wait(barrier, len(all_peers))


def exchange(targets, make):
    copies = [make(k, target) for k, target in enumerate(targets)]
    for copy in copies:
        copy.start()
    for copy in copies:
        copy.wait()


def remote(src, dst, send_sem, recv_sem, target):
    return pltpu.make_async_remote_copy(src_ref=src, dst_ref=dst, send_sem=send_sem, recv_sem=recv_sem, device_id=target, device_id_type=pl.DeviceIdType.MESH)


def dot(a, b, dims):
    return lax.dot_general(a, b, (dims, ((), ())), preferred_element_type=F32)


def expert_math(hg, hu, da):
    gate = hg.astype(BF16).astype(F32)
    up = hu.astype(BF16).astype(F32)
    d_act = da.astype(BF16).astype(F32)
    sig = jax.nn.sigmoid(gate)
    silu = gate * sig
    act = (silu * up).astype(BF16)
    d_up = (d_act * silu).astype(BF16)
    d_gate = (d_act * up * sig * (1.0 + gate * (1.0 - sig))).astype(BF16)
    return act, d_gate, d_up


LINK_RATE, HOP_US, FFN_US, FFN_FROM_US = 25e3, 4.0, 3.5, 20.0
PIECES = (
    (0, 0, "zxy"), (0, 1, "zyx"), (1, 0, "xyz"), (1, 1, "yzx"))


def due(left):
    steps = [(piece, phase) for piece in range(len(PIECES)) for phase in (1, 2)]
    return [(piece, phase) for piece, phase in steps if (piece, phase) not in left and left.get((piece, phase - 1)) == 0]


def plan(sizes, tile_bytes, n_ffn):
    free, arrive, order, left = {}, [], [], {}
    tasks = [("ffn", 0.0, FFN_US)] * n_ffn + [("back", 0.0, 0.5), ("final", 12.0, 6.0)] + [(f"sum{k}", 5.0, 0.5) for k in range(4)]
    now, next_at = 8.0, FFN_FROM_US

    def issue(hop, when):
        piece, phase, sign, step = hop
        _, half, axes = PIECES[piece]
        size = tile_bytes // (1 if half is None else 2)
        for axis in axes[:phase]:
            size *= sizes[axis]
        size //= 2 if step == sizes[axes[phase]] // 2 else 1
        link = (axes[phase], sign)
        free[link] = max(when, free.get(link, 0.0)) + size / LINK_RATE
        arrive.append((free[link] + HOP_US, hop))

    def begin(piece, phase, when):
        left[piece, phase] = 2 * (sizes[PIECES[piece][2][phase]] // 2)
        for sign in (1, -1):
            issue((piece, phase, sign, 1), when)

    for piece in range(len(PIECES)):
        begin(piece, 0, now)
    while arrive or tasks:
        arrive.sort()
        when, hop = arrive[0] if arrive else (1e9, None)
        if tasks and max(now, next_at) + 0.6 * tasks[0][2] < max(now, when) + (0.0 if arrive else 1e9):
            name, _, lasts = tasks.pop(0)
            order.append(name)
            now = max(now, next_at) + lasts
            next_at = now + (tasks[0][1] if tasks else 0.0)
            continue
        arrive.pop(0)
        now = max(now, when)
        order.append(hop)
        piece, phase, sign, step = hop
        if step < sizes[PIECES[piece][2][phase]] // 2:
            issue((piece, phase, sign, step + 1), now)
        left[piece, phase] -= 1
        for other in due(left):
            begin(*other, now)
    return order, now


class Copies:
    def __init__(self, send_sem, recv_sem):
        self.sems, self.made = (send_sem, recv_sem), {}

    def start(self, name, ends):
        k = len(self.made)
        self.made[name] = lambda: remote(*ends()[:2], self.sems[0].at[k], self.sems[1].at[k], ends()[2])
        self.made[name]().start()

    def wait_recv(self, name):
        self.made[name]().wait_recv()


def gather_kernel(n_y, n_z, n_ep, order, rows_in, send_in, meta_in, x_ref, tok_ref, gain_ref, router_ref, wg_ref, wu_ref, wd_ref, rows_out, meta_res, y_ref, gh_ref, sum_ref,
                  got, result, back_out, meta_out, parts, got_ep, got_y, got_z, total, o_acc, d_acc, send_sem, recv_sem, own_sem):
    step = pl.program_id(0)
    n_x = n_ep // 2
    dp, ep = lax.axis_index("dp"), lax.axis_index("ep")
    at = {"x": lax.div(ep, 2), "y": lax.rem(dp, n_y), "z": lax.div(dp, n_y)}
    core = lax.rem(ep, 2)
    sizes = {"x": n_x, "y": n_y, "z": n_z}
    width = wg_ref.shape[0]
    wide = rows_in.shape[2]

    def shifted(axis, by):
        return lax.rem(at[axis] + by + 2 * sizes[axis], sizes[axis])

    def neighbour(axis, by):
        place = {**at, axis: shifted(axis, by)}
        return {"dp": place["z"] * n_y + place["y"], "ep": place["x"] * 2 + core}

    partner = {"dp": dp, "ep": at["x"] * 2 + (1 - core)}
    along_ep = [{"dp": dp, "ep": lax.rem(ep + k, n_ep)} for k in range(1, n_ep)]
    along_y = [{"dp": at["z"] * n_y + lax.rem(at["y"] + k, n_y), "ep": ep} for k in range(1, n_y)]
    along_z = [{"dp": lax.rem(at["z"] + k, n_z) * n_y + at["y"], "ep": ep} for k in range(1, n_z)]
    copies = Copies(send_sem, recv_sem)

    def columns(piece, half):
        low, high = 0, wide
        for part in (PIECES[piece][1], half):
            if part is not None:
                middle = (low + high) // 2
                low, high = ((low, middle), (middle, high))[part]
        return pl.ds(low, high - low)

    def region(piece, phase, index, half):
        tile, _, axes = PIECES[piece]
        pick = {axis: slice(None) if k < phase else index if k == phase else at[axis] for k, axis in enumerate(axes)}
        return rows_out.at[pick["z"], pick["y"], pick["x"], core, tile, :, columns(piece, half)]

    def send(piece, phase, sign, hop):
        axis = PIECES[piece][2][phase]
        half = None if hop < sizes[axis] // 2 else (0 if sign == 1 else 1)

        def ends():
            dst = region(piece, phase, shifted(axis, -sign * (hop - 1)), half)
            src = rows_in.at[PIECES[piece][0], :, columns(piece, half)] if (phase, hop) == (0, 1) else dst
            return src, dst, neighbour(axis, sign)

        copies.start((piece, phase, sign, hop), ends)

    def to_partner(name, block):
        copies.start(("pair", *name), lambda: (block(), block(), partner))

    left = {}

    def arrived(piece, phase, sign, hop):
        axes = PIECES[piece][2]
        copies.wait_recv((piece, phase, sign, hop))
        last = sizes[axes[phase]] // 2
        if hop < last:
            send(piece, phase, sign, hop + 1)
        if phase == 2:
            half = None if hop < last else (0 if sign == 1 else 1)
            to_partner((piece, phase, sign, hop), lambda: region(piece, phase, shifted(axes[phase], -sign * hop), half))
        left[piece, phase] = left.get((piece, phase), 2 * last) - 1
        if not left[piece, phase] and phase == 1:
            to_partner((piece, phase), lambda: region(piece, 2, at[axes[2]], None))
        for other, later in due(left):
            left[other, later] = 2 * (sizes[PIECES[other][2][later]] // 2)
            for way in (1, -1):
                send(other, later, way, 1)

    def exchange_results(name, src, dst):
        for k, target in enumerate(along_ep):
            copies.start((name, k), lambda target=target: (src.at[target["ep"]], dst.at[ep], target))

    def spread(name, targets, block):
        for k, target in enumerate(targets):
            copies.start((name, k), lambda target=target: (block(), block(), target))

    def all_in(name, n):
        for k in range(n):
            copies.wait_recv((name, k))

    def own_copies():
        return [
            pltpu.make_async_copy(rows_in.at[pl.ds(0, 2)], rows_out.at[at["z"], at["y"], at["x"], core], own_sem.at[0]),
            pltpu.make_async_copy(send_in.at[ep], got.at[ep], own_sem.at[1]),
            pltpu.make_async_copy(meta_in, meta_out.at[pl.ds(dp * n_ep + ep, 1)], own_sem.at[2])]

    def prologue():
        enter(along_ep + [neighbour("y", 1), neighbour("y", -1), neighbour("z", 1), neighbour("z", -1)] + along_y + along_z)
        mine = own_copies()
        for copy in mine:
            copy.start()
        for piece in range(len(PIECES)):
            left[piece, 0] = 2 * (sizes[PIECES[piece][2][0]] // 2)
            for sign in (1, -1):
                send(piece, 0, sign, 1)
        exchange_results("dispatch", send_in, got)
        for copy in mine:
            copy.wait()
        spread("meta_ep", along_ep, lambda: meta_out.at[pl.ds(dp * n_ep + ep, 1)])

    def ready():
        all_in("dispatch", n_ep - 1)
        all_in("meta_ep", n_ep - 1)
        spread("meta_y", along_y, lambda: meta_out.at[pl.ds(dp * n_ep, n_ep)])

    def finish_tokens():
        all_in("back", n_ep - 1)
        all_in("meta_z", n_z - 1)
        n_tok = x_ref.shape[0]
        n_slot = got.shape[0] * got.shape[1]
        tok = tok_ref[...]
        probs, inv = tok[:, :n_ep], tok[:, n_ep:n_ep + 1]
        gates, slots, experts = ([tok[:, n_ep + k:n_ep + k + 1] for k in (first, first + 1)] for first in (1, 3, 5))
        slot_id = lax.broadcasted_iota(jnp.int32, (n_tok, n_slot), 1).astype(F32)
        expert_id = lax.broadcasted_iota(jnp.int32, (n_tok, n_ep), 1).astype(F32)
        picks = [(slot_id == slot).astype(F32).astype(BF16) for slot in slots]
        hots = [(expert_id == expert).astype(F32) for expert in experts]
        back = back_out[...].reshape(n_slot, wide)
        picked = [dot(pick, back[:, :width], ((1,), (0,))) for pick in picks]
        d_picks = [dot(pick, back[:, width:], ((1,), (0,))) for pick in picks]
        x = x_ref[...].astype(F32)
        x_hat = x * inv
        xn = rows_in[:, :, :width].reshape(n_tok, width).astype(F32)
        dy = rows_in[:, :, width:].reshape(n_tok, width).astype(F32)
        ids = meta_out[...]
        lane = lax.broadcasted_iota(jnp.int32, (1, 1, LANES), 2)
        is_id = jnp.logical_and(lane >= 2 * n_tok, lane < 4 * n_tok)
        expert_lane = lax.broadcasted_iota(jnp.int32, (1, n_ep), 1)
        load_frac = jnp.zeros((1, n_ep), F32)
        for e in range(n_ep):
            named = jnp.sum(jnp.where(jnp.logical_and(is_id, ids == float(e)), 1.0, 0.0), axis=0)
            load_frac += jnp.where(expert_lane == e, jnp.sum(named, axis=1, keepdims=True), 0.0)
        total_tok = n_tok * ids.shape[0]
        load_frac = load_frac / (2 * total_tok)
        d_probs = (AUX_COEF * n_ep / total_tok) * load_frac
        for hot, pick in zip(hots, picked):
            d_probs = d_probs + hot * jnp.sum(dy * pick, axis=1, keepdims=True)
        d_logits = probs * (d_probs - jnp.sum(probs * d_probs, axis=1, keepdims=True))
        d_xn = d_picks[0] + d_picks[1]
        for e in range(n_ep):
            d_xn = d_xn + d_logits[:, e:e + 1] * router_ref[e:e + 1, :]
        d_xn = d_xn.astype(BF16).astype(F32)
        d_gain = jnp.sum(d_xn * x_hat, axis=0, keepdims=True)
        d_probs_sum = jnp.sum(tok, axis=0, keepdims=True)
        share = width // n_ep
        for e in range(n_ep):
            parts[e, :, :width] = jnp.sum(d_logits[:, e:e + 1] * xn, axis=0, keepdims=True)
            parts[e, :, width:width + share] = d_gain[:, e * share:(e + 1) * share]
            parts[e, :, width + share:] = d_probs_sum
        y_ref[...] = (x + (gates[0] * picked[0] + gates[1] * picked[1])).astype(BF16)
        scaled = d_xn * gain_ref[...]
        gh_ref[...] = (inv * (scaled - x_hat * jnp.mean(scaled * x_hat, axis=1, keepdims=True)) + dy).astype(BF16)
        got_ep[ep] = parts[ep]
        exchange_results("sum0", parts, got_ep)

    def added(ref, n):
        value = ref[0]
        for k in range(1, n):
            value = value + ref[k]
        return value

    def sum_up(stage):
        if stage == 0:
            all_in("sum0", n_ep - 1)
            got_y[at["y"]] = added(got_ep, n_ep)
            spread("sum1", along_y, lambda: got_y.at[at["y"]])
        if stage == 1:
            all_in("sum1", n_y - 1)
            got_z[at["z"]] = added(got_y, n_y)
            spread("sum2", along_z, lambda: got_z.at[at["z"]])
        if stage == 2:
            all_in("sum2", n_z - 1)
            total[ep] = added(got_z, n_z)
            spread("sum3", along_ep, lambda: total.at[ep])
        if stage == 3:
            all_in("sum3", n_ep - 1)
            sum_ref[...] = total[...]

    runs, current = [], []
    for entry in order:
        if entry == "ffn":
            runs.append(current)
            current = []
        else:
            current.append(entry)
    runs.append(current)
    n_ffn = len(runs) - 1

    @pl.when(step == 0)
    def _():
        prologue()
        for hop in runs[0]:
            arrived(*hop)
        ready()
        o_acc[...] = jnp.zeros_like(o_acc)
        d_acc[...] = jnp.zeros_like(d_acc)

    @pl.when(step < n_ffn)
    def _():
        n_row = got.shape[0] * got.shape[1]
        half = wg_ref.shape[1] // 2
        xn = got[:, :, :width].reshape(n_row, width)
        dy = got[:, :, width:].reshape(n_row, width)
        cuts = [slice(0, half), slice(half, 2 * half)]
        mid = [expert_math(dot(xn, wg_ref[:, c], ((1,), (0,))), dot(xn, wu_ref[:, c], ((1,), (0,))), dot(dy, wd_ref[c, :], ((1,), (1,)))) for c in cuts]
        act, d_gate, d_up = (jnp.concatenate(parts, axis=1) for parts in zip(*mid))
        o_acc[...] += dot(act, wd_ref[...], ((1,), (0,)))
        d_acc[...] += dot(d_gate, wg_ref[...], ((1,), (1,))) + dot(d_up, wu_ref[...], ((1,), (1,)))

    @pl.when(step == n_ffn - 1)
    def _():
        result[:, :, :width] = o_acc[...].astype(BF16).reshape(*result.shape[:2], width)
        result[:, :, width:] = d_acc[...].astype(BF16).reshape(*result.shape[:2], width)

    for k in range(1, n_ffn):
        @pl.when(step == k - 1)
        def _():
            if k == 2:
                all_in("meta_y", n_y - 1)
                spread("meta_z", along_z, lambda: meta_out.at[pl.ds(at["z"] * n_y * n_ep, n_y * n_ep)])
            for hop in runs[k]:
                arrived(*hop)

    @pl.when(step == n_ffn)
    def _():
        for entry in runs[n_ffn]:
            if entry == "back":
                back_out[ep] = result[ep]
                exchange_results("back", result, back_out)
            elif entry == "final":
                finish_tokens()
            elif entry[:3] == "sum":
                sum_up(int(entry[3:]))
            else:
                arrived(*entry)
        meta_res[...] = meta_out[...]
        for name in copies.made:
            if name[0] == "pair":
                copies.wait_recv(name)
        for copy in copies.made.values():
            copy().wait_send()


def gather_rows(rows, send, meta, x, tok, gain, router, wg, wu, wd, n_y, n_z, n_ep, block):
    n_tok, wide = rows.shape
    n_dev = n_y * n_z * n_ep
    capacity = send.shape[1]
    width, ff = wg.shape
    n_ffn = ff // block
    tiles = n_tok // 8
    order, _ = plan({"x": n_ep // 2, "y": n_y, "z": n_z}, 8 * wide * 2, n_ffn)
    hops = [e for e in order if not isinstance(e, str)]
    n_sem = len(hops) + sum(1 for e in hops if e[1] == 2) + len(PIECES)
    n_sem += 5 * (n_ep - 1) + 2 * (n_y - 1) + 2 * (n_z - 1)
    vmem, hbm = pl.BlockSpec(memory_space=pltpu.VMEM), pl.BlockSpec(memory_space=pl.ANY)
    col = pl.BlockSpec((width, block), lambda j: (0, jnp.minimum(j, n_ffn - 1)))
    row = pl.BlockSpec((block, width), lambda j: (jnp.minimum(j, n_ffn - 1), 0))
    slots = pltpu.VMEM((n_ep, capacity, wide), BF16)
    long = width + width // n_ep + LANES
    out, meta_all, y, gh, sums = pl.pallas_call(
        functools.partial(gather_kernel, n_y, n_z, n_ep, order),
        grid=(n_ffn + 1,),
        in_specs=[vmem] * 7 + [col, col, row],
        out_specs=[hbm] + [vmem] * 4,
        out_shape=[
            jax.ShapeDtypeStruct((n_z, n_y, n_ep // 2, 2, 2, 8, wide), BF16),
            jax.ShapeDtypeStruct((n_dev, 1, LANES), F32),
            jax.ShapeDtypeStruct((n_tok, width), BF16),
            jax.ShapeDtypeStruct((n_tok, width), BF16),
            jax.ShapeDtypeStruct((n_ep, 1, long), F32)],
        scratch_shapes=[
            slots, slots, slots, pltpu.VMEM((n_dev, 1, LANES), F32),
            *(pltpu.VMEM((n, 1, long), F32) for n in (n_ep, n_ep, n_y, n_z, n_ep)),
            pltpu.VMEM((n_ep * capacity, width), F32), pltpu.VMEM((n_ep * capacity, width), F32),
            pltpu.SemaphoreType.DMA((n_sem,)), pltpu.SemaphoreType.DMA((n_sem,)), pltpu.SemaphoreType.DMA((3,))],
        compiler_params=pltpu.CompilerParams(collective_id=1, has_side_effects=True, dimension_semantics=("arbitrary",), vmem_limit_bytes=56 * 2**20),
        cost_estimate=pl.CostEstimate(flops=12 * n_ep * capacity * width * ff, bytes_accessed=6 * width * ff, transcendentals=0),
        name="gather_rows",
    )(rows.reshape(tiles, 8, wide), send, meta, x, tok, gain, router, wg, wu, wd)
    return out.reshape(n_dev * 16, wide), meta_all, y, gh, sums


def pack_kernel(n_quarter, info_ref, off_ref, near_ref, far_ref, pos_ref, gate_ref, wg_ref, wu_ref, wd_ref, xn_out, dp_out, slice_ref, xn_buf, dp_buf, acc_g, acc_u, acc_d, sem):
    g = pl.program_id(0)
    n_group = pl.num_programs(0)
    width = xn_buf.shape[1]
    tile = MOST_PER_GROUP + ALIGN
    off = off_ref[g]
    base = pl.multiple_of(lax.div(off, ALIGN) * ALIGN, ALIGN)
    hit = lax.broadcasted_iota(jnp.int32, (tile, GROUP), 0) + base == pos_ref[0]
    pick = hit.astype(F32).astype(BF16)
    gate = jnp.sum(jnp.where(hit, gate_ref[0], 0.0), axis=1, keepdims=True)
    head, rest = pl.ds(base, ALIGN), pl.ds(pl.multiple_of(base + ALIGN, ALIGN), tile - ALIGN)
    wide = min(2 * TILE, width)
    half = near_ref.shape[0]
    keep = lax.broadcasted_iota(jnp.int32, (ALIGN, wide), 0) + base < off
    for buf, low, scale in ((xn_buf, 0, None), (dp_buf, width, gate)):
        for c in range(0, width, wide):
            cut = slice(c, c + wide)
            columns = slice(low + c, low + c + wide)
            new = dot(pick[:, :half], near_ref[:, columns], ((1,), (0,))) + dot(pick[:, half:], far_ref[:, columns], ((1,), (0,)))
            new = (new if scale is None else new * scale).astype(BF16)
            buf[head, cut] = jnp.where(keep, buf[head, cut].astype(F32), new[:ALIGN].astype(F32)).astype(BF16)
            buf[rest, cut] = new[ALIGN:]

    @pl.when(g == n_group - 1)
    def _():
        usual = USUAL_ROWS // TILE
        zeros = jnp.zeros((TILE, width), BF16)
        tail = pl.ds(pl.multiple_of(base + tile, ALIGN), TILE)
        xn_buf[tail, :] = zeros
        dp_buf[tail, :] = zeros
        used = info_ref[0]

        def at(t):
            return pl.ds(pl.multiple_of(t * TILE, TILE), TILE)

        def clear(t, carry):
            xn_buf[at(t), :] = zeros
            dp_buf[at(t), :] = zeros
            return carry

        lax.fori_loop(used, usual, clear, 0)

        part = width // n_quarter
        low = pl.multiple_of(info_ref[2] * part, part)
        quarter = pl.ds(low, part)
        wg, wu, wd = wg_ref[...], wu_ref[...], wd_ref[...]
        for acc in (acc_g, acc_u, acc_d):
            acc[...] = jnp.zeros_like(acc)

        def hidden_rows(x, p):
            return expert_math(dot(x, wg, ((1,), (0,))), dot(x, wu, ((1,), (0,))), dot(p, wd, ((1,), (1,))))

        def copies(t):
            return [pltpu.make_async_copy(buf.at[at(t)], out.at[at(t)], sem.at[k]) for k, (buf, out) in enumerate(((xn_buf, xn_out), (dp_buf, dp_out)))]

        def begin(t, carry):
            for copy in copies(t):
                copy.start()
            return carry

        def end(t, carry):
            for copy in copies(t):
                copy.wait()
            return carry

        def add(t, carry):
            act, dg, du = hidden_rows(xn_buf[at(t), :], dp_buf[at(t), :])
            acc_g[...] += dot(xn_buf[at(t), quarter], dg, ((0,), (0,)))
            acc_u[...] += dot(xn_buf[at(t), quarter], du, ((0,), (0,)))
            acc_d[...] += dot(act, dp_buf[at(t), quarter], ((0,), (0,)))

            @pl.when(t == 1)
            def _():
                lax.fori_loop(0, jnp.maximum(used, usual), begin, 0)

            return carry

        lax.fori_loop(0, jnp.maximum(used, 2), add, 0)
        slice_ref[0] = acc_g[...].astype(BF16)
        slice_ref[1] = acc_u[...].astype(BF16)
        for k in range(0, part, TILE):
            slice_ref[2, k:k + TILE, :] = acc_d[:, k:k + TILE].astype(BF16)
        lax.fori_loop(0, jnp.maximum(used, usual), end, 0)


def pack_rows(info, near, far, offsets, pos, gates, wg, wu, wd, most, n_quarter):
    total, width = 2 * near.shape[0], near.shape[1] // 2
    n_group = total // GROUP
    half = pl.BlockSpec((GROUP // 2, 2 * width), lambda g, info, off: (g, 0))
    usual, part = USUAL_ROWS, width // n_quarter
    small = pl.BlockSpec((1, 1, GROUP), lambda g, info, off: (g, 0, 0))
    col = pl.BlockSpec((width, TILE), lambda g, info, off: (0, info[1]))
    row = pl.BlockSpec((TILE, width), lambda g, info, off: (info[1], 0))
    whole = pl.BlockSpec(memory_space=pl.ANY)
    buf = pltpu.VMEM((max(most, usual) + 2 * TILE + ALIGN, width), BF16)
    out = jax.ShapeDtypeStruct((max(most, usual), width), BF16)
    return pl.pallas_call(
        functools.partial(pack_kernel, n_quarter),
        grid_spec=pltpu.PrefetchScalarGridSpec(
            num_scalar_prefetch=2,
            grid=(n_group,),
            in_specs=[half, half, small, small, col, col, row],
            out_specs=[whole, whole, pl.BlockSpec((3, part, TILE), lambda g, info, off: (0, 0, 0))],
            scratch_shapes=[
                buf, buf, pltpu.VMEM((part, TILE), F32), pltpu.VMEM((part, TILE), F32), pltpu.VMEM((TILE, part), F32), pltpu.SemaphoreType.DMA((2,))],
        ),
        out_shape=[out, out, jax.ShapeDtypeStruct((3, part, TILE), BF16)],
        compiler_params=pltpu.CompilerParams(dimension_semantics=("arbitrary",), vmem_limit_bytes=63 * 2**20),
        cost_estimate=pl.CostEstimate(flops=4 * GROUP * total * width, bytes_accessed=4 * total * width, transcendentals=0),
        name="pack_rows",
    )(info, offsets, near, far, pos, gates, wg, wu, wd)


def grads_kernel(info_ref, xn_hbm, dp_hbm, wg_ref, wu_ref, wd_ref, gg_ref, gu_ref, gd_ref, xn, xt, dp, act_t, d_gate, d_up, acc_g, acc_u, acc_d, tile_x, tile_p, sem):
    rows, width = xn.shape
    tiles = [slice(r, r + TILE) for r in range(0, rows, TILE)]

    @pl.when(pl.program_id(0) == 0)
    def _():
        def copies(t):
            at = pl.ds(pl.multiple_of(t * TILE, TILE), TILE)
            return [pltpu.make_async_copy(src.at[at], dst.at[at], sem.at[k, t]) for k, (src, dst) in enumerate(((xn_hbm, xn), (dp_hbm, dp)))]

        def begin(t, carry):
            for copy in copies(t):
                copy.start()
            return carry

        def end(t, carry):
            for copy in copies(t):
                copy.wait()
            at = pl.ds(pl.multiple_of(t * TILE, TILE), TILE)
            xt[:, at] = xn[at, :].T
            return carry

        lax.fori_loop(0, len(tiles), begin, 0)
        for acc in (acc_g, acc_u, acc_d):
            acc[...] = jnp.zeros_like(acc)
        lax.fori_loop(0, len(tiles), end, 0)

    wg, wu, wd = wg_ref[...], wu_ref[...], wd_ref[...]

    def hidden_rows(x, p):
        return expert_math(dot(x, wg, ((1,), (0,))), dot(x, wu, ((1,), (0,))), dot(p, wd, ((1,), (1,))))

    @pl.when(info_ref[0] > rows // TILE)
    def _():
        for acc in (acc_g, acc_u, acc_d):
            acc[...] = jnp.zeros_like(acc)

        def more(t, carry):
            at = pl.ds(pl.multiple_of(t * TILE, TILE), TILE)
            copies = [pltpu.make_async_copy(xn_hbm.at[at], tile_x, sem.at[0, 0]), pltpu.make_async_copy(dp_hbm.at[at], tile_p, sem.at[1, 0])]
            for copy in copies:
                copy.start()
            for copy in copies:
                copy.wait()
            act, d_gate[:TILE, :], d_up[:TILE, :] = hidden_rows(tile_x[...], tile_p[...])
            act_t[:, :TILE] = act.T

            def part(c, carry):
                cut = pl.ds(pl.multiple_of(c * TILE, TILE), TILE)
                acc_g[cut, :] += dot(tile_x[:, cut], d_gate[:TILE, :], ((0,), (0,)))
                acc_u[cut, :] += dot(tile_x[:, cut], d_up[:TILE, :], ((0,), (0,)))
                acc_d[:, cut] += dot(act_t[:, :TILE], tile_p[:, cut], ((1,), (0,)))
                return carry

            lax.fori_loop(0, width // TILE, part, 0)
            return carry

        lax.fori_loop(rows // TILE, info_ref[0], more, 0)

    for t in tiles:
        act, d_gate[t, :], d_up[t, :] = hidden_rows(xn[t, :], dp[t, :])
        act_t[:, t] = act.T

    wide = min(2 * TILE, width)
    for c in range(0, width, wide):
        cut = slice(c, c + wide)
        gg_ref[cut, :] = (dot(xt[cut, :], d_gate[...], ((1,), (0,))) + acc_g[cut, :]).astype(BF16)
        gu_ref[cut, :] = (dot(xt[cut, :], d_up[...], ((1,), (0,))) + acc_u[cut, :]).astype(BF16)
    for c in range(0, width, wide):
        cut = slice(c, c + wide)
        gd_ref[:, cut] = (dot(act_t[...], dp[:, cut], ((1,), (0,))) + acc_d[:, cut]).astype(BF16)


def expert_grads(info, xn, dp, wg, wu, wd, n_block):
    width, ff = wg.shape
    rows = USUAL_ROWS
    hbm = pl.BlockSpec(memory_space=pl.ANY)
    col = pl.BlockSpec((width, TILE), lambda j, info: (0, j))
    row = pl.BlockSpec((TILE, width), lambda j, info: (j, 0))
    return pl.pallas_call(
        grads_kernel,
        grid_spec=pltpu.PrefetchScalarGridSpec(
            num_scalar_prefetch=1,
            grid=(n_block,),
            in_specs=[hbm, hbm, col, col, row],
            out_specs=[col, col, row],
            scratch_shapes=[
                pltpu.VMEM((rows, width), BF16), pltpu.VMEM((width, rows), BF16), pltpu.VMEM((rows, width), BF16),
                pltpu.VMEM((TILE, rows), BF16), pltpu.VMEM((rows, TILE), BF16), pltpu.VMEM((rows, TILE), BF16),
                pltpu.VMEM((width, TILE), F32), pltpu.VMEM((width, TILE), F32), pltpu.VMEM((TILE, width), F32),
                pltpu.VMEM((TILE, width), BF16), pltpu.VMEM((TILE, width), BF16), pltpu.SemaphoreType.DMA((2, rows // TILE))],
        ),
        out_shape=[jax.ShapeDtypeStruct((width, ff), BF16)] * 2 + [jax.ShapeDtypeStruct((ff, width), BF16)],
        compiler_params=pltpu.CompilerParams(dimension_semantics=("arbitrary",), vmem_limit_bytes=63 * 2**20),
        cost_estimate=pl.CostEstimate(flops=12 * rows * width * TILE * n_block, bytes_accessed=12 * width * TILE * n_block, transcendentals=0),
        name="expert_grads",
    )(info, xn, dp, wg, wu, wd)


def place_kernel(slices_ref, gg_in, gu_in, gd_in, gg_ref, gu_ref, gd_ref):
    part = slices_ref.shape[1]
    for q in range(slices_ref.shape[0] // 3):
        rows = slice(q * part, (q + 1) * part)
        gg_ref[rows, :] = slices_ref[3 * q]
        gu_ref[rows, :] = slices_ref[3 * q + 1]
        for k in range(0, part, TILE):
            gd_ref[:, q * part + k:q * part + k + TILE] = slices_ref[3 * q + 2, k:k + TILE, :]


def place_slices(slices, grads, first, n_quarter):
    width, ff = grads[0].shape
    part = width // n_quarter
    hbm = pl.BlockSpec(memory_space=pl.ANY)
    col = pl.BlockSpec((width, TILE), lambda i: (0, first + i))
    row = pl.BlockSpec((TILE, width), lambda i: (first + i, 0))
    return pl.pallas_call(
        place_kernel,
        grid=(slices.shape[0] // (3 * n_quarter),),
        in_specs=[pl.BlockSpec((3 * n_quarter, part, TILE), lambda i: (i, 0, 0)), hbm, hbm, hbm],
        out_specs=[col, col, row],
        out_shape=[jax.ShapeDtypeStruct(g.shape, g.dtype) for g in grads],
        input_output_aliases={1: 0, 2: 1, 3: 2},
        compiler_params=pltpu.CompilerParams(dimension_semantics=("arbitrary",)),
        cost_estimate=pl.CostEstimate(flops=0, bytes_accessed=4 * slices.size, transcendentals=0),
        name="place_slices",
    )(slices, *grads)


def solution(mesh):
    n_ep = mesh.shape["ep"]
    n_dp = mesh.shape["dp"]
    n_y = 4 if n_dp == 32 else 2
    n_z = n_dp // n_y
    n_dev = n_dp * n_ep
    all_axes = ("dp", "ep")

    def local_step(hidden, grad_out, expert_ids, norm_gain, w_router, w_gate, w_up, w_down):
        n_tok, width = hidden.shape
        n_exp = w_router.shape[1]
        capacity = 4 * n_tok // n_exp
        total_tok = n_tok * n_dev
        dest_rows, slot_owner, loads = route_tables(expert_ids, n_exp, capacity)
        choice_hot = (expert_ids[:, :, None] == jnp.arange(n_exp, dtype=jnp.int32)).astype(F32)

        x_f32 = hidden.astype(F32)
        inv_rms = lax.rsqrt(jnp.mean(x_f32 * x_f32, axis=-1, keepdims=True) + EPS)
        x_hat = x_f32 * inv_rms
        x_norm = (x_hat * norm_gain).astype(BF16)
        xn_f32 = x_norm.astype(F32)
        router_probs = jax.nn.softmax(jnp.dot(xn_f32, w_router, preferred_element_type=F32), axis=-1)
        gate_vals = jnp.sum(router_probs[:, None, :] * choice_hot, axis=-1)

        meta = jnp.concatenate([gate_vals.T.reshape(1, -1), expert_ids.T.astype(F32).reshape(1, -1)], axis=1)
        meta = jnp.pad(meta, ((0, 0), (0, LANES - meta.shape[1])))
        dy_f32 = grad_out.astype(F32)
        d_picked = (dy_f32[:, None, :] * gate_vals[:, :, None]).astype(BF16).reshape(n_tok * 2, width)
        send = jnp.concatenate([
            jnp.take(x_norm, slot_owner // 2, axis=0, mode="fill", fill_value=0),
            jnp.take(d_picked, slot_owner, axis=0, mode="fill", fill_value=0)], axis=1)
        wg, wu, wd = w_gate[0], w_up[0], w_down[0]
        tok = jnp.concatenate([router_probs, inv_rms, gate_vals, dest_rows.reshape(n_tok, 2).astype(F32), expert_ids.astype(F32)], axis=1)
        tok = jnp.pad(tok, ((0, 0), (0, LANES - tok.shape[1])))
        rows = jnp.concatenate([x_norm, grad_out], axis=1)
        half = n_tok // 2
        far = lax.all_gather(rows[half:], all_axes, axis=0, tiled=True)
        near, meta_all, out_hidden, grad_hidden, sums = gather_rows(
            rows, send.reshape(n_exp, capacity, 2 * width), meta[None], hidden, tok,
            norm_gain[None], w_router.T, wg, wu, wd, n_y, n_z, n_ep, 2 * TILE)
        meta_all = meta_all.reshape(n_dev, LANES)
        ids_all = meta_all[:, 2 * n_tok:4 * n_tok].astype(jnp.int32).reshape(n_dev, 2, n_tok)
        gates_all = meta_all[:, :2 * n_tok].reshape(n_dev, 2, n_tok)
        sums = sums[:, 0]
        share = width // n_exp
        grad_router = sums[:, :width].T
        grad_gain = sums[:, width:width + share].reshape(-1)
        prob_sum = sums[0, width + share:width + share + n_exp]
        all_loads = jnp.sum((ids_all[..., None] == jnp.arange(n_exp, dtype=jnp.int32)).astype(F32), axis=(0, 1, 2))
        load_frac = all_loads / (2 * total_tok)
        aux_loss = AUX_COEF * n_exp * jnp.sum(load_frac * prob_sum / total_tok)

        me = lax.axis_index("ep")
        mine = ids_all == me

        def by_group(a):
            return jnp.concatenate([a[:, :half].reshape(-1, GROUP // 2), a[:, half:].reshape(-1, GROUP // 2)], axis=1)

        member = by_group(jnp.any(mine, axis=1))
        gate_me = by_group(jnp.sum(jnp.where(mine, gates_all, 0.0), axis=1))[:, None]
        rank = jnp.cumsum(member.astype(jnp.int32), axis=1)
        counts = rank[:, -1]
        ends = jnp.cumsum(counts)
        offsets = jnp.concatenate([jnp.zeros((1,), jnp.int32), ends])
        pos = jnp.where(member, offsets[:-1, None] + rank - 1, -(2**24))[:, None]
        n_block = w_gate.shape[2] // TILE
        own = n_block - n_dp // QUARTERS
        place = lax.axis_index("dp")
        info = jnp.stack([(offsets[-1] + TILE - 1) // TILE, own + place // QUARTERS, place % QUARTERS]).astype(jnp.int32)
        xn, dp, slices = pack_rows(info, near, far, offsets, pos, gate_me, wg, wu, wd, capacity * n_dev, QUARTERS)
        slices_all = lax.all_gather(slices, "dp", axis=0, tiled=True)
        grads = expert_grads(info, xn, dp, wg, wu, wd, own)
        g_gate, g_up, g_down = (g[None] for g in place_slices(slices_all, grads, own, QUARTERS))
        return out_hidden, aux_loss, grad_hidden, grad_gain, grad_router, g_gate, g_up, g_down

    tok_spec = P(all_axes, None)
    w_spec = P("ep", None, None)
    return jax.shard_map(local_step, mesh=mesh, in_specs=(tok_spec, tok_spec, tok_spec, P(), P(), w_spec, w_spec, w_spec), out_specs=(tok_spec, P(), tok_spec, P(), P(), w_spec, w_spec, w_spec), check_vma=False)
```

time: 579 us -> 543 us (0.938)
  Pallas kernels: 531 us -> 500 us
    pallas_call x4 -> x2, Pallas kernels: 328 us -> 284 us  [the longest x1 225 us: expert_grads(): pl.pallas_call(grads_kernel, grid_spec=pltpu.PrefetchScalarGridSpec(num_s...]
    pallas_call x1, Pallas kernels: 185 us -> 197 us  [gather_rows(): pl.pallas_call(functools.partial(gather_kernel, n_y, n_z, n_ep, order), g...]
  transfers between devices with their start and end apart: 1 -> 2, of which waited for: 0 -> 0; matrix products, arithmetic and copies ran while one was open for 1% -> 4% of each run, Pallas kernels for 42% -> 78%
where the time goes in v5:
time: 543 us
  Pallas kernels  500 us (92%)
  between operations  16.9 us (3%)
  other arithmetic  12.8 us (2%)
  local copies, waits for them, and re-layouts  11.8 us (2%)
    pallas_call x1, Pallas kernels, expert_grads(): pl.pallas_call(grads_kernel, grid_spec=pltpu.PrefetchScalarGridSpec(num_s...  225 us
    pallas_call x1, Pallas kernels, gather_rows(): pl.pallas_call(functools.partial(gather_kernel, n_y, n_z, n_ep, order), g...  197 us
    pallas_call x1, Pallas kernels, pack_rows(): pl.pallas_call(functools.partial(pack_kernel, n_quarter), grid_spec=pltpu...  59.2 us
    pallas_call x1, Pallas kernels, place_slices(): pl.pallas_call(place_kernel, grid=(slices.shape[0] // (3 * n_quarter),),...  18.4 us
  transfers between devices with their start and end apart: 2, of which 0 were waited for; matrix products, arithmetic and copies ran while one was open for 4% of the time, Pallas kernels for 78%

profile of v5, /device:TPU:1, one launch (start us, length us, event | category | flops | bytes accessed | tf_op | source)
XLA Modules:
  0.0 542.5 jit_solution(3742742525522322715)
XLA Ops:
  7.2 1.0 fusion.1
  8.3 1.0 fusion.3
  9.3 1.5 fusion.4
  11.0 0.8 copy.80
  11.7 0.1 eq.51
  11.9 0.1 reduce_window_sum.43
  12.0 0.2 select_reduce_fusion.1
  12.2 0.1 reduce_sum.72
  12.3 0.1 mul.75
  12.6 0.8 scatter_custom_fusion
  13.6 1.0 fusion.19
  14.6 0.2 fusion.7
  15.0 0.7 select_reduce_fusion.2
  15.9 0.1 mul.81
  16.0 0.9 gather_fusion
  16.9 1.1 mul.77
  18.1 0.4 mul.78
  18.5 0.6 pad.4.tok_ref
  19.3 0.9 gather_fusion.1
  20.2 0.6 maximum_bitcast_fusion.meta_in
  20.8 1.6 fusion.rows_in
  22.4 0.1 broadcast_select_fusion
  22.6 1.1 pad_maximum_fusion.send_in
  23.6 197.4 %gather_rows.1 = (bf16[8,4,4,2,2,8,4096]{6,5,4,3,2,1,0:T(8,128)(2,1)}, f32[256,1,128]{2,1,0:T(1,128)}, bf16[32,2048]{1,0:T(8,128)(2,1)}, bf16[32,2048]{1,0:T(8,128)(2,1)}, f32[8,1,2432]{2,1,0:T(1,128)}) custom-call(bf16[4,8,4096]{2,1,0:T(8,128)(2,1)} %fusion.rows_in, bf16[8,16,4096]{2,1,0:T(8,128)(2,1)} %pad_maximum_fusion.send_in, ...), custom_call_target="tpu_custom_call" | custom-call | flops 17716740096 | bytes 69206016 | tf_op jit(solution)/shard_map/gather_rows/pallas_call | solution.py:404
  221.0 1.1 fusion.15
  222.2 0.1 copy.91
  222.4 0.1 concatenate.40
  222.5 0.1 copy.92
  222.6 0.1 concatenate.41
  222.7 0.6 reduce-window.10
  223.3 0.2 slice_reduce_fusion
  223.8 0.5 slice.73
  225.0 0.1 reduce.1
  225.3 0.1 copy.97
  225.6 0.1 copy.98
  225.7 0.1 reshape.240
  225.8 0.6 broadcast_in_dim.81.gate_ref
  226.5 0.6 pad_add_fusion.1.info_ref
  227.1 0.7 copy_select_fusion.pos_ref
  227.8 59.2 %pack_rows.1 = (bf16[4096,2048]{1,0:T(8,128)(2,1)}, bf16[4096,2048]{1,0:T(8,128)(2,1)}, bf16[3,512,256]{2,1,0:T(8,128)(2,1)}) custom-call(s32[3]{0:T(128)} %pad_add_fusion.1.info_ref, s32[33]{0:T(128)} %copy-done.3, bf16[4096,4096]{1,0:T(8,128)(2,1)} %bitcast.69, bf16[4096,4096]{1,0:T(8,128)(2,1)} %all-gather.3.cloned.1.call-done.far_ref, ...), custom_call_target="tpu_custom_call" | custom-call | flops 17179869184 | bytes 67108864 | tf_op jit(solution)/shard_map/pack_rows/pallas_call | solution.py:523
  287.1 0.6 copy.101
  287.7 0.2 convert_reduce_fusion
  287.9 0.6 fusion.11
  289.2 0.6 slice_bitcast_fusion
  289.8 224.9 %expert_grads.1 = (bf16[2048,5632]{1,0:T(8,128)(2,1)}, bf16[2048,5632]{1,0:T(8,128)(2,1)}, bf16[5632,2048]{1,0:T(8,128)(2,1)}) custom-call(s32[3]{0:T(128)} %pad_add_fusion.1.info_ref, bf16[4096,2048]{1,0:T(8,128)(2,1)} %get-tuple-element.28.xn_hbm, bf16[4096,2048]{1,0:T(8,128)(2,1)} %get-tuple-element.29.dp_hbm, bf16[2048,5632]{1,0:T(8,128)(2,1)} %bitcast.62, ...), custom_call_target="tpu_custom_call" | custom-call | flops 202937204736 | bytes 88080384 | tf_op jit(solution)/shard_map/expert_grads/pallas_call | solution.py:619
  514.8 18.4 %place_slices.1 = (bf16[2048,5632]{1,0:T(8,128)(2,1)}, bf16[2048,5632]{1,0:T(8,128)(2,1)}, bf16[5632,2048]{1,0:T(8,128)(2,1)}) custom-call(bf16[96,512,256]{2,1,0:T(8,128)(2,1)} %all-gather.5.cloned.1.call-done.slices_ref, bf16[2048,5632]{1,0:T(8,128)(2,1)} %get-tuple-element.30.gg_in, ...), custom_call_target="tpu_custom_call", output_to_operand_aliasing={{0}: (1, {}), {1}: (2, {}), {2}: (3, {})} | custom-call | bytes 50331648 | tf_op jit(solution)/shard_map/place_slices/pallas_call | solution.py:655
  533.2 0.7 copy.111
  533.9 0.7 copy.112
  (56 shorter events, 2.0 us)
Async XLA Ops:
  7.2 220.6 %all-gather.3.cloned.1.call-start = ((), (), s32[]{:S(2)}) async-start(), calls=%async_computation | async-start | bytes 33685504 | tf_op jit(solution)/shard_map/all_gather | solution.py:704
  10.8 503.9 %all-gather.5.cloned.1.call-start = ((), (), s32[]{:S(2)}) async-start(), calls=%async_computation.1 | async-start | bytes 25952256 | tf_op jit(solution)/shard_map/all_gather | solution.py:738
  226.5 1.3 copy-start.3
  227.8 59.2 %copy-start.2 = (f32[8,1,2432]{2,1,0:T(1,128)S(1)}, f32[8,1,2432]{2,1,0:T(1,128)}, u32[]{:S(2)}) copy-start(f32[8,1,2432]{2,1,0:T(1,128)} %get-tuple-element.24) | copy-start | bytes 233476
  514.8 18.5 %copy-start.1 = (bf16[32,2048]{1,0:T(8,128)(2,1)S(1)}, bf16[32,2048]{1,0:T(8,128)(2,1)}, u32[]{:S(2)}) copy-start(bf16[32,2048]{1,0:T(8,128)(2,1)} %get-tuple-element.63) | copy-start | bytes 393220
  514.8 19.1 %copy-start = (bf16[32,2048]{1,0:T(8,128)(2,1)S(1)}, bf16[32,2048]{1,0:T(8,128)(2,1)}, u32[]{:S(2)}) copy-start(bf16[32,2048]{1,0:T(8,128)(2,1)} %get-tuple-element.65) | copy-start | bytes 393220
Sparse Core Ops, SparseCore 0:
  12.3 200.7 all-gather.2
  287.2 179.1 all-gather.4

commit v6 on v5

--- a/solution.py
+++ b/solution.py
@@ -79,7 +79,7 @@
 
 
 def due(left):
-    steps = [(piece, phase) for piece in range(len(PIECES)) for phase in (1, 2)]
+    steps = [(piece, phase) for piece in range(len(PIECES)) for phase in (1, 2) if phase == 1 or "local" in left]
     return [(piece, phase) for piece, phase in steps if (piece, phase) not in left and left.get((piece, phase - 1)) == 0]
 
 
@@ -114,6 +114,10 @@
             order.append(name)
             now = max(now, next_at) + lasts
             next_at = now + (tasks[0][1] if tasks else 0.0)
+            if not tasks:
+                left["local"] = 0
+                for other in due(left):
+                    begin(*other, now)
             continue
         arrive.pop(0)
         now = max(now, when)
@@ -205,6 +209,9 @@
         left[piece, phase] = left.get((piece, phase), 2 * last) - 1
         if not left[piece, phase] and phase == 1:
             to_partner((piece, phase), lambda: region(piece, 2, at[axes[2]], None))
+        begin_due()
+
+    def begin_due():
         for other, later in due(left):
             left[other, later] = 2 * (sizes[PIECES[other][2][later]] // 2)
             for way in (1, -1):
@@ -319,6 +326,8 @@
         if stage == 3:
             all_in("sum3", n_ep - 1)
             sum_ref[...] = total[...]
+            left["local"] = 0
+            begin_due()
 
     runs, current = [], []
     for entry in order:

time: 543 us -> 550 us (1.013)
  Pallas kernels: 500 us -> 507 us
    pallas_call x1, Pallas kernels: 197 us -> 206 us  [gather_rows(): pl.pallas_call(functools.partial(gather_kernel, n_y, n_z, n_ep, order), g...]
where the time goes in v6:
time: 550 us; the launch traced here: 549 us
  Pallas kernels  507 us (92%)
  between operations  16.9 us (3%)
  other arithmetic  12.8 us (2%)
  local copies, waits for them, and re-layouts  11.8 us (2%)
    pallas_call x1, Pallas kernels, expert_grads(): pl.pallas_call(grads_kernel, grid_spec=pltpu.PrefetchScalarGridSpec(num_s...  225 us
    pallas_call x1, Pallas kernels, gather_rows(): pl.pallas_call(functools.partial(gather_kernel, n_y, n_z, n_ep, order), g...  206 us
    pallas_call x1, Pallas kernels, pack_rows(): pl.pallas_call(functools.partial(pack_kernel, n_quarter), grid_spec=pltpu...  57.6 us
    pallas_call x1, Pallas kernels, place_slices(): pl.pallas_call(place_kernel, grid=(slices.shape[0] // (3 * n_quarter),),...  18.4 us
  transfers between devices with their start and end apart: 2, of which 0 were waited for; matrix products, arithmetic and copies ran while one was open for 4% of the time, Pallas kernels for 78%

profile of v6, /device:TPU:1, one launch (start us, length us, event | category | flops | bytes accessed | tf_op | source)
XLA Modules:
  0.0 549.3 jit_solution(5382237762252348236)
XLA Ops:
  7.2 1.0 fusion.1
  8.3 1.0 fusion.3
  9.3 1.5 fusion.4
  11.0 0.8 copy.80
  11.7 0.1 eq.51
  11.9 0.1 reduce_window_sum.43
  12.0 0.2 select_reduce_fusion.1
  12.2 0.1 reduce_sum.72
  12.3 0.1 mul.75
  12.6 0.8 scatter_custom_fusion
  13.6 1.0 fusion.19
  14.6 0.2 fusion.7
  15.0 0.7 select_reduce_fusion.2
  15.9 0.1 mul.81
  16.0 0.9 gather_fusion
  16.9 1.1 mul.77
  18.1 0.4 mul.78
  18.5 0.6 pad.4.tok_ref
  19.3 0.9 gather_fusion.1
  20.2 0.6 maximum_bitcast_fusion.meta_in
  20.8 1.6 fusion.rows_in
  22.4 0.1 broadcast_select_fusion
  22.6 1.1 pad_maximum_fusion.send_in
  23.6 205.8 %gather_rows.1 = (bf16[8,4,4,2,2,8,4096]{6,5,4,3,2,1,0:T(8,128)(2,1)}, f32[256,1,128]{2,1,0:T(1,128)}, bf16[32,2048]{1,0:T(8,128)(2,1)}, bf16[32,2048]{1,0:T(8,128)(2,1)}, f32[8,1,2432]{2,1,0:T(1,128)}) custom-call(bf16[4,8,4096]{2,1,0:T(8,128)(2,1)} %fusion.rows_in, bf16[8,16,4096]{2,1,0:T(8,128)(2,1)} %pad_maximum_fusion.send_in, ...), custom_call_target="tpu_custom_call" | custom-call | flops 17716740096 | bytes 69206016 | tf_op jit(solution)/shard_map/gather_rows/pallas_call | solution.py:413
  229.4 1.1 fusion.15
  230.7 0.1 copy.91
  230.8 0.1 concatenate.40
  230.9 0.1 copy.92
  231.0 0.1 concatenate.41
  231.2 0.6 reduce-window.10
  231.8 0.2 slice_reduce_fusion
  232.2 0.5 slice.73
  233.4 0.1 reduce.1
  233.8 0.1 copy.97
  234.0 0.1 copy.98
  234.1 0.1 reshape.240
  234.2 0.6 broadcast_in_dim.81.gate_ref
  234.9 0.6 pad_add_fusion.1.info_ref
  235.5 0.7 copy_select_fusion.pos_ref
  236.2 57.6 %pack_rows.1 = (bf16[4096,2048]{1,0:T(8,128)(2,1)}, bf16[4096,2048]{1,0:T(8,128)(2,1)}, bf16[3,512,256]{2,1,0:T(8,128)(2,1)}) custom-call(s32[3]{0:T(128)} %pad_add_fusion.1.info_ref, s32[33]{0:T(128)} %copy-done.3, bf16[4096,4096]{1,0:T(8,128)(2,1)} %bitcast.69, bf16[4096,4096]{1,0:T(8,128)(2,1)} %all-gather.3.cloned.1.call-done.far_ref, ...), custom_call_target="tpu_custom_call" | custom-call | flops 17179869184 | bytes 67108864 | tf_op jit(solution)/shard_map/pack_rows/pallas_call | solution.py:532
  293.9 0.6 copy.101
  294.5 0.2 convert_reduce_fusion
  294.8 0.6 fusion.11
  296.0 0.6 slice_bitcast_fusion
  296.7 224.9 %expert_grads.1 = (bf16[2048,5632]{1,0:T(8,128)(2,1)}, bf16[2048,5632]{1,0:T(8,128)(2,1)}, bf16[5632,2048]{1,0:T(8,128)(2,1)}) custom-call(s32[3]{0:T(128)} %pad_add_fusion.1.info_ref, bf16[4096,2048]{1,0:T(8,128)(2,1)} %get-tuple-element.28.xn_hbm, bf16[4096,2048]{1,0:T(8,128)(2,1)} %get-tuple-element.29.dp_hbm, bf16[2048,5632]{1,0:T(8,128)(2,1)} %bitcast.62, ...), custom_call_target="tpu_custom_call" | custom-call | flops 202937204736 | bytes 88080384 | tf_op jit(solution)/shard_map/expert_grads/pallas_call | solution.py:628
  521.6 18.4 %place_slices.1 = (bf16[2048,5632]{1,0:T(8,128)(2,1)}, bf16[2048,5632]{1,0:T(8,128)(2,1)}, bf16[5632,2048]{1,0:T(8,128)(2,1)}) custom-call(bf16[96,512,256]{2,1,0:T(8,128)(2,1)} %all-gather.5.cloned.1.call-done.slices_ref, bf16[2048,5632]{1,0:T(8,128)(2,1)} %get-tuple-element.30.gg_in, ...), custom_call_target="tpu_custom_call", output_to_operand_aliasing={{0}: (1, {}), {1}: (2, {}), {2}: (3, {})} | custom-call | bytes 50331648 | tf_op jit(solution)/shard_map/place_slices/pallas_call | solution.py:664
  540.1 0.7 copy.111
  540.7 0.7 copy.112
  (56 shorter events, 2.0 us)
Async XLA Ops:
  7.2 229.1 %all-gather.3.cloned.1.call-start = ((), (), s32[]{:S(2)}) async-start(), calls=%async_computation | async-start | bytes 33685504 | tf_op jit(solution)/shard_map/all_gather | solution.py:713
  10.8 510.8 %all-gather.5.cloned.1.call-start = ((), (), s32[]{:S(2)}) async-start(), calls=%async_computation.1 | async-start | bytes 25952256 | tf_op jit(solution)/shard_map/all_gather | solution.py:747
  234.9 1.3 copy-start.3
  236.2 57.6 %copy-start.2 = (f32[8,1,2432]{2,1,0:T(1,128)S(1)}, f32[8,1,2432]{2,1,0:T(1,128)}, u32[]{:S(2)}) copy-start(f32[8,1,2432]{2,1,0:T(1,128)} %get-tuple-element.24) | copy-start | bytes 233476
  521.6 18.5 %copy-start.1 = (bf16[32,2048]{1,0:T(8,128)(2,1)S(1)}, bf16[32,2048]{1,0:T(8,128)(2,1)}, u32[]{:S(2)}) copy-start(bf16[32,2048]{1,0:T(8,128)(2,1)} %get-tuple-element.63) | copy-start | bytes 393220
  521.6 19.1 %copy-start = (bf16[32,2048]{1,0:T(8,128)(2,1)S(1)}, bf16[32,2048]{1,0:T(8,128)(2,1)}, u32[]{:S(2)}) copy-start(bf16[32,2048]{1,0:T(8,128)(2,1)} %get-tuple-element.65) | copy-start | bytes 393220
Sparse Core Ops, SparseCore 0:
  12.3 194.9 all-gather.2
  294.0 184.0 all-gather.4
